TPU v7x, 256 devices: a whole 4x4x8 slice. The times are simulated.
256 devices in a mesh: ra: 16 (over x_hi, y, core), dec: 16 (over z, x_lo).
Axes of the slice: x: 4 (x_hi: 2, x_lo: 2; x = x_hi * 2 + x_lo), y: 4, z: 8, core: 2. Of those that a mesh axis runs over, the one named last changes fastest.
Arguments:
- design: float32 [5, 80, 64, 4096], P(None, None, 'ra', 'dec'), may hold values from -6 to 6
- observed: float32 [80, 64, 4096], P(None, 'ra', 'dec'), may hold values from -6 to 6
- weight: float32 [80, 64, 4096], P(None, 'ra', 'dec'), may hold values from 0.3 to 3
- params: float32 [5, 64, 4096], P(None, 'ra', 'dec'), may hold values from -4 to 4
- offsets: int32 [80, 64, 4096], P(None, 'ra', 'dec'), may hold values from 0 to 8, as said below
- counts: int32 [64, 4096], P('ra', 'dec'), may hold values from 10 to 80, as said below
Outputs:
- new_params: float32 [5, 64, 4096], P(None, 'ra', 'dec')
- reduced_chi: float32 [], replicated
Inputs may be any that keep to these rules, and one draw needn't show every extreme that they name: `offsets`: in the first and the last latitude row of cells no offset steps outside the grid in latitude. `counts`: cells near the middle latitude hold more live observations; the two middle latitude rows hold 80.
All inputs are finite; a program needn't handle non-finite values.
Results may differ from a plain program's by a relative error of at most 0.0003.
Values sent between devices are 32-bit elements; how exact they have to be, the bound alone decides.
No kernel may reach another device: no remote copies, remote signals or barrier semaphores. Data moves between devices by JAX's collectives and lax.ppermute only.
A program may use at most 64 MiB of HBM per device.

v0:
```python
import jax
import jax.numpy as jnp
from jax import lax
from jax.sharding import Mesh
from jax.sharding import PartitionSpec as P

RA_DEC = ("ra_0", "ra_1", "ra_2", "dec_0", "dec_1")
RA = ("ra_0", "ra_1", "ra_2")
DEC = ("dec_0", "dec_1")


def extended_2(cells, sides, width):
    for axis, dim in sides:
        count = lax.axis_size(axis)
        head = lax.slice_in_dim(cells, 0, width, axis=dim)
        tail = lax.slice_in_dim(cells, cells.shape[dim] - width, cells.shape[dim], axis=dim)
        cells = jnp.concatenate(
            [
                lax.ppermute(tail, axis, [(i, (i + 1) % count) for i in range(count)]),
                cells,
                lax.ppermute(head, axis, [((i + 1) % count, i) for i in range(count)]),
            ],
            axis=dim,
        )
    return cells


def over_axes(value, axes):
    for axis in axes:
        value = lax.psum(value, axis)
    return value


def pair_list():
    pairs = []
    for first in range(5):
        for second in range(first, 5):
            pairs.append((first, second))
    return pairs


def code_sums(design, observed, masked_weight, codes, windows):
    source = windows[0][:, None]
    for code in range(1, 9):
        source = jnp.where((codes == code)[None], windows[code][:, None], source)
    resid = observed
    for comp in range(5):
        resid = resid - design[comp] * source[comp]
    weighted = masked_weight * resid
    products = []
    for comp in range(5):
        products.append(design[comp] * weighted)
    for first, second in pair_list():
        products.append(masked_weight * design[first] * design[second])
    binned = []
    for code in range(9):
        hit = codes == code
        binned.append(
            jnp.stack([jnp.sum(jnp.where(hit, prod, 0.0), axis=0) for prod in products], axis=0)
        )
    return (binned, jnp.sum(weighted * resid))


def solve_blocks(stacked):
    rhs = [stacked[comp] for comp in range(5)]
    normal = [[None] * 5 for item in range(5)]
    for place, pair in enumerate(pair_list()):
        first, second = pair
        value = stacked[5 + place]
        if first == second:
            value = value + 1.0
        normal[first][second] = value
        normal[second][first] = value
    lower = [[None] * 5 for item in range(5)]
    for first in range(5):
        for second in range(first + 1):
            running = normal[first][second]
            for inner in range(second):
                running = running - lower[first][inner] * lower[second][inner]
            if first == second:
                lower[first][first] = jnp.sqrt(running)
            else:
                lower[first][second] = running / lower[second][second]
    forward = []
    for first in range(5):
        running = rhs[first]
        for inner in range(first):
            running = running - lower[first][inner] * forward[inner]
        forward.append(running / lower[first][first])
    answer = [None] * 5
    for first in range(4, -1, -1):
        running = forward[first]
        for inner in range(first + 1, 5):
            running = running - lower[inner][first] * answer[inner]
        answer[first] = running / lower[first][first]
    return jnp.stack(answer, axis=0)


def per_device(design, observed, weight, params, offsets, counts):
    cells_ra = params.shape[1]
    cells_dec = params.shape[2]
    slots = lax.broadcasted_iota(jnp.int32, observed.shape, 0)
    codes = jnp.where(slots < counts[None], offsets, 9)
    floats = jnp.concatenate([design, observed[None], weight[None]], axis=0)
    extended, extended_codes = (
        extended_2(floats, ((RA, 2), (DEC, 3)), 1),
        extended_2(codes[None], ((RA, 2), (DEC, 3)), 1),
    )
    ext_codes = extended_codes[0]
    padded_local = jnp.pad(params, ((0, 0), (2, 2), (2, 2)))
    windows = []
    for code in range(9):
        step_ra = code // 3 - 1
        step_dec = code % 3 - 1
        windows.append(
            padded_local[
                :, 1 + step_ra : 3 + step_ra + cells_ra, 1 + step_dec : 3 + step_dec + cells_dec
            ]
        )
    step_ra_all = ext_codes // 3 - 1
    step_dec_all = ext_codes % 3 - 1
    place_ra = lax.broadcasted_iota(jnp.int32, ext_codes.shape, 1) - 1 + step_ra_all
    place_dec = lax.broadcasted_iota(jnp.int32, ext_codes.shape, 2) - 1 + step_dec_all
    owned = (
        (place_ra >= 0)
        & (place_ra < cells_ra)
        & (place_dec >= 0)
        & (place_dec < cells_dec)
        & (ext_codes < 9)
    )
    masked_weight = jnp.where(owned, extended[6], jnp.zeros_like(extended[6]))
    binned, chi = code_sums(extended[:5], extended[5], masked_weight, ext_codes, windows)
    total = jnp.zeros((20, cells_ra, cells_dec), jnp.float32)
    for code in range(9):
        step_ra = code // 3 - 1
        step_dec = code % 3 - 1
        total = (
            total
            + binned[code][
                :, 1 - step_ra : 1 - step_ra + cells_ra, 1 - step_dec : 1 - step_dec + cells_dec
            ]
        )
    live_count = jnp.sum(counts).astype(jnp.float32)
    chi_total, count_total = (over_axes(chi, RA_DEC), over_axes(live_count, RA_DEC))
    new_params = params + solve_blocks(total)
    return (new_params, chi_total / count_total)


def solution(mesh):
    finer = Mesh(mesh.devices.reshape(2, 4, 2, 8, 2), ("ra_0", "ra_1", "ra_2", "dec_0", "dec_1"))
    return jax.shard_map(
        per_device,
        mesh=finer,
        in_specs=(
            P(None, None, RA, DEC),
            P(None, RA, DEC),
            P(None, RA, DEC),
            P(None, RA, DEC),
            P(None, RA, DEC),
            P(RA, DEC),
        ),
        out_specs=(P(None, RA, DEC), P()),
        check_vma=False,
    )
```

profile of v0, /device:TPU:14, one launch (start us, length us, event | category | flops | bytes accessed | tf_op | source)
XLA Modules:
  0.0 148.5 jit_solution(16316700984926354208)
XLA Ops:
  0.6 0.0 copy-start.12
  0.6 0.0 copy-start.13
  0.7 1.1 fusion.38
  1.8 0.0 copy-start.3
  1.8 0.1 collective-permute-start
  1.9 0.0 copy-start.14
  1.9 1.7 %collective-permute-start.1 = (s32[1,80,1,256]{3,1,2,0:T(8,128)S(1)}, s32[1,80,1,256]{3,1,2,0:T(8,128)S(1)}, u32[]{:S(2)}, u32[]{:S(2)}) collective-permute-start(s32[1,80,1,256]{3,1,2,0:T(8,128)S(1)} %get-tuple-element.1082), channel_id=1, source_target_pairs={{16,0},{32,16},{48,32},{64,48},{80,64},{96,80},{112,96},{128,112},... | collective-permute-start | bytes 245768 | tf_op jit(solution)/shard_map/ppermute | solution.py:21
  3.6 1.7 %copy.21 = f32[5,80,4,256]{3,1,2,0:T(8,128)S(1)} copy(f32[5,80,4,256]{3,2,1,0:T(4,128)} %param.6) | data formatting | bytes 3276800 | tf_op args[0]
  5.4 0.0 copy-done.12
  5.4 0.0 copy-done.13
  5.4 0.0 copy-start.16
  5.4 0.1 copy_bitcast_fusion
  5.5 0.0 copy-start.1
  5.5 0.0 copy-start.2
  5.5 1.2 pad_maximum_fusion.4
  6.8 0.0 collective-permute-start.4
  6.8 1.7 %collective-permute-start.5 = (f32[7,80,1,256]{3,1,2,0:T(8,128)}, f32[7,80,1,256]{3,1,2,0:T(8,128)S(1)}, u32[]{:S(2)}, u32[]{:S(2)}) collective-permute-start(f32[7,80,1,256]{3,1,2,0:T(8,128)} %get-tuple-element.1069), channel_id=1, source_target_pairs={{16,0},{32,16},{48,32},{64,48},{80,64},{96,80},{112,96},{128,112},... | collective-permute-start | bytes 1720328 | tf_op jit(solution)/shard_map/ppermute | solution.py:21
  8.5 0.0 copy-done.14
  8.5 0.9 pad_slice_fusion.8
  9.4 0.0 collective-permute-done
  9.5 0.0 collective-permute-done.1
  9.5 0.0 copy-done.3
  9.5 0.0 copy-start.10
  9.5 0.9 fusion.75
  10.3 0.8 fusion.85
  11.2 0.0 copy-done.10
  11.2 2.2 %collective-permute-start.2 = (s32[1,80,6,1]{3,1,2,0:T(8,128)}, s32[1,80,6,1]{3,1,2,0:T(8,128)}, u32[]{:S(2)}, u32[]{:S(2)}) collective-permute-start(s32[1,80,6,1]{3,1,2,0:T(8,128)} %get-tuple-element.1077), channel_id=1, source_target_pairs={{0,1},{1,2},{2,3},{3,4},{4,5},{5,6},{6,7},{7,8},{8,9},{9,10},{10,1... | collective-permute-start | bytes 5768 | tf_op jit(solution)/shard_map/ppermute | solution.py:19
  13.4 0.0 collective-permute-start.3
  13.4 0.6 reduce_sum.1819
  14.7 9.9 %collective-permute-done.2 = s32[1,80,6,1]{3,1,2,0:T(8,128)} collective-permute-done((s32[1,80,6,1]{3,1,2,0:T(8,128)}, s32[1,80,6,1]{3,1,2,0:T(8,128)}, u32[]{:S(2)}, u32[]{:S(2)}) %collective-permute-start.2) | collective-permute-done | bytes 1952 | tf_op jit(solution)/shard_map/ppermute | solution.py:19
  24.6 0.0 collective-permute-done.3
  24.6 2.2 %broadcast_compare_fusion.11 = (pred[80,6,258]{2,0,1:T(8,128)(4,1)}, s32[80,6,258]{2,0,1:T(8,128)S(1)}) fusion(s32[80,6,1]{2,0,1:T(8,128)} %bitcast.13, s32[80,6,256]{2,0,1:T(8,128)} %get-tuple-element.1079, s32[80,6,1]{2,0,1:T(8,128)} %bitcast.11), kind=kLoop, calls=%fused_computation.445 | loop fusion | flops 371520 | bytes 1114560 | tf_op jit(solution)/shard_map/eq | solution.py:45
  26.8 1.6 %broadcast_compare_fusion.10 = (pred[80,6,258]{2,0,1:T(8,128)(4,1)}, pred[80,6,258]{2,0,1:T(8,128)(4,1)}, pred[80,6,258]{2,0,1:T(8,128)(4,1)}, pred[80,6,258]{2,...) fusion(s32[80,6,258]{2,0,1:T(8,128)S(1)} %get-tuple-element.1037), kind=kLoop, calls=%fused_computation.444 | loop fusion | flops 866880 | bytes 1362240 | tf_op jit(solution)/shard_map/eq | solution.py:45
  28.4 0.0 collective-permute-done.4
  28.4 0.0 collective-permute-done.5
  28.4 0.8 copy-done.5
  29.3 0.8 copy-done.6
  30.1 0.2 pad_maximum_fusion.1
  30.3 0.0 copy-start.7
  30.3 1.8 %fusion.84 = (f32[7,80,6,1]{3,1,2,0:T(8,128)}, f32[7,80,6,1]{3,1,2,0:T(8,128)S(1)}) fusion(f32[7,80,6,256]{3,1,2,0:T(8,128)S(1)} %pad_maximum_fusion.1), kind=kLoop, calls=%fused_computation.535 | loop fusion | bytes 53760 | tf_op jit(solution)/shard_map/slice | solution.py:16
  32.1 2.6 %copy.22 = f32[7,80,6,1]{1,3,2,0:T(1,128)} copy(f32[7,80,6,1]{3,1,2,0:T(8,128)} %get-tuple-element.1066) | data formatting | bytes 26880 | tf_op jit(solution)/shard_map/slice | solution.py:16
  34.7 1.1 copy.23
  35.8 2.2 %collective-permute-start.7 = (f32[7,80,6,1]{1,3,2,0:T(1,128)}, f32[7,80,6,1]{1,3,2,0:T(1,128)}, u32[]{:S(2)}, u32[]{:S(2)}) collective-permute-start(f32[7,80,6,1]{1,3,2,0:T(1,128)} %copy.23), channel_id=1, source_target_pairs={{1,0},{2,1},{3,2},{4,3},{5,4},{6,5},{7,6},{8,7},{9,8},{10,9},{11,1... | collective-permute-start | bytes 40328 | tf_op jit(solution)/shard_map/ppermute | solution.py:21
  38.0 0.9 collective-permute-start.6
  38.9 5.6 %select_select_fusion = f32[5,80,6,258]{3,1,2,0:T(8,128)} fusion(f32[5,6,258]{2,1,0:T(8,128)} %get-tuple-element.1094, f32[5,6,258]{2,1,0:T(8,128)} %get-tuple-element.1093, f32[5,6,258]{2,1,0:T(8,128)} %get-tuple-element.1092, f32[5,6,258]{2,1,0:T(8,128)} %get-tuple-element.1091, f32[5,6,258]{2,1,0:T(8,128)} %get-tuple-element.1090, ...), kind=kLoop, calls=%fused_computation.1 | loop fusion | flops 4953600 | bytes 3746160 | tf_op jit(solution)/shard_map/jit(_where)/select_n | solution.py:45
  44.6 0.7 collective-permute-done.6
  45.2 1.3 copy.24
  46.5 0.0 collective-permute-done.7
  46.5 2.5 %copy.25 = f32[7,80,6,1]{3,1,2,0:T(8,128)} copy(f32[7,80,6,1]{1,3,2,0:T(1,128)} %collective-permute-done.7) | data formatting | bytes 26880 | tf_op jit(solution)/shard_map/ppermute | solution.py:21
  49.0 5.6 %pad_maximum_fusion = f32[7,80,6,258]{3,1,2,0:T(8,128)S(1)} fusion(f32[7,80,6,1]{3,1,2,0:T(8,128)} %copy.25, f32[7,80,1,256]{3,1,2,0:T(8,128)} %copy-done.6, f32[1,80,4,256]{3,1,2,0:T(8,128)} %copy-done.1, f32[1,80,4,256]{3,1,2,0:T(8,128)} %copy-done.2, f32[5,80,4,256]{3,1,2,0:T(8,128)S(1)} %copy.21, f32[7,80,1,256]{3,1,2,0:T(8,128)} %copy-done.5, ...), kind=kLoop, calls=%fused_computation | loop fusion | flops 5201280 | bytes 6935040 | tf_op jit(solution)/shard_map/concatenate | solution.py:17
  54.6 3.3 %multiply_reduce_fusion = (f32[]{:T(128)}, f32[80,6,258]{2,0,1:T(8,128)S(1)}, f32[80,6,258]{2,0,1:T(8,128)S(1)}, s32[1,80,6,258]{3,1,2,0:T(8,128)S(1)}) fusion(f32[7,80,6,258]{3,1,2,0:T(8,128)S(1)} %pad_maximum_fusion, s32[258]{0:T(512)S(1)} %iota_add_fusion, s32[6]{0:T(128)S(1)} %iota_add_fusion.1, s32[1,80,6,1]{3,1,2,0:T(8,128)} %collective-permute-done.3, ...), kind=kLoop, calls=%fused_computation.37 | loop fusion | flops 5325119 | bytes 7926820 | tf_op jit(solution)/shard_map/reduce_sum | solution.py:61
  58.0 0.6 fusion.36
  58.6 0.8 fusion.32
  59.4 15.2 %select_reduce_fusion.169 = (f32[6,258]{1,0:T(8,128)S(1)}, f32[6,258]{1,0:T(8,128)S(1)}, f32[6,258]{1,0:T(8,128)S(1)}, f32[6,258]{1,0:T(8,128)S(1)}, f32[6,258]{...) fusion(f32[80,6,258]{2,0,1:T(8,128)S(1)} %get-tuple-element.105, ...), kind=kLoop, calls=%fused_computation.207 | loop fusion | flops 23266440 | bytes 7120800 | tf_op jit(solution)/shard_map/reduce_sum | solution.py:59
  74.6 14.1 %select_reduce_fusion.179 = (f32[6,258]{1,0:T(8,128)S(1)}, f32[6,258]{1,0:T(8,128)S(1)}, f32[6,258]{1,0:T(8,128)S(1)}, f32[6,258]{1,0:T(8,128)S(1)}, f32[6,258]{...) fusion(f32[80,6,258]{2,0,1:T(8,128)S(1)} %get-tuple-element.106, ...), kind=kLoop, calls=%fused_computation.217 | loop fusion | flops 22151880 | bytes 6625440 | tf_op jit(solution)/shard_map/reduce_sum | solution.py:59
  88.7 0.0 copy-start.15
  90.8 0.3 slice_add_fusion
  91.2 0.1 constant_dynamic-update-slice_fusion.184
  91.3 0.6 add.124
  91.9 7.1 %all-reduce.5 = (f32[]{:T(128)}, f32[]{:T(128)}) all-reduce(f32[]{:T(128)} %get-tuple-element.1002, f32[]{:T(128)S(6)} %convert_element_type.5), channel_id=1, replica_groups=mesh['ra_0'=2,'ra_1'=4,'ra_2'=2,'dec_0'=8,'dec_1'=2] {'ra_0'}, use_global_device_ids=true, to_apply=%region_181.182 | all-reduce | flops 2 | bytes 16 | tf_op jit(solution)/shard_map/psum | solution.py:30
  99.0 17.4 %all-reduce.2 = (f32[]{:T(128)}, f32[]{:T(128)}) all-reduce(f32[]{:T(128)} %get-tuple-element.1000, f32[]{:T(128)} %get-tuple-element.1001), channel_id=1, replica_groups=mesh['ra_0'=2,'ra_1'=4,'ra_2'=2,'dec_0'=8,'dec_1'=2] {'ra_1'}, use_global_device_ids=true, to_apply=%region_182.183 | all-reduce | flops 2 | bytes 16 | tf_op jit(solution)/shard_map/psum | solution.py:30
  116.4 3.1 %all-reduce.4 = (f32[]{:T(128)}, f32[]{:T(128)}) all-reduce(f32[]{:T(128)} %get-tuple-element.994, f32[]{:T(128)} %get-tuple-element.995), channel_id=1, replica_groups=mesh['ra_0'=2,'ra_1'=4,'ra_2'=2,'dec_0'=8,'dec_1'=2] {'ra_2'}, use_global_device_ids=true, to_apply=%region_183.184 | all-reduce | flops 2 | bytes 16 | tf_op jit(solution)/shard_map/psum | solution.py:30
  119.5 21.1 %all-reduce.1 = (f32[]{:T(128)}, f32[]{:T(128)}) all-reduce(f32[]{:T(128)} %get-tuple-element.998, f32[]{:T(128)} %get-tuple-element.999), channel_id=1, replica_groups=mesh['ra_0'=2,'ra_1'=4,'ra_2'=2,'dec_0'=8,'dec_1'=2] {'dec_0'}, use_global_device_ids=true, to_apply=%region_184.185 | all-reduce | flops 2 | bytes 16 | tf_op jit(solution)/shard_map/psum | solution.py:30
  140.6 5.5 %all-reduce.3 = (f32[]{:T(128)}, f32[]{:T(128)}) all-reduce(f32[]{:T(128)} %get-tuple-element.992, f32[]{:T(128)} %get-tuple-element.993), channel_id=1, replica_groups=mesh['ra_0'=2,'ra_1'=4,'ra_2'=2,'dec_0'=8,'dec_1'=2] {'dec_1'}, use_global_device_ids=true, to_apply=%region_185.186 | all-reduce | flops 2 | bytes 16 | tf_op jit(solution)/shard_map/psum | solution.py:30
  (206 shorter events, 0.8 us)
Async XLA Ops:
  0.6 4.7 %copy-start.12 = (f32[80,4,256]{2,1,0:T(4,128)S(1)}, f32[80,4,256]{2,1,0:T(4,128)}, u32[]{:S(2)}) copy-start(f32[80,4,256]{2,1,0:T(4,128)} %param.8) | copy-start | bytes 983044
  0.6 4.7 %copy-start.13 = (f32[80,4,256]{2,1,0:T(4,128)S(1)}, f32[80,4,256]{2,1,0:T(4,128)}, u32[]{:S(2)}) copy-start(f32[80,4,256]{2,1,0:T(4,128)} %param.7) | copy-start | bytes 983044
  1.8 7.7 %copy-start.3 = (s32[1,80,4,256]{3,1,2,0:T(8,128)}, s32[1,80,4,256]{3,1,2,0:T(8,128)S(1)}, u32[]{:S(2)}) copy-start(s32[1,80,4,256]{3,1,2,0:T(8,128)S(1)} %fusion.38) | copy-start | bytes 983044
  1.8 7.6 %collective-permute-start = (s32[1,80,1,256]{3,1,2,0:T(8,128)S(1)}, s32[1,80,1,256]{3,1,2,0:T(8,128)S(1)}, u32[]{:S(2)}, u32[]{:S(2)}) collective-permute-start(s32[1,80,1,256]{3,1,2,0:T(8,128)S(1)} %get-tuple-element.1081), channel_id=1, source_target_pairs={{0,16},{16,32},{32,48},{48,64},{64,80},{80,96},{96,112},{112,128},... | collective-permute-start | bytes 245768 | tf_op jit(solution)/shard_map/ppermute | solution.py:19
  1.9 6.6 %copy-start.14 = (f32[5,4,256]{2,1,0:T(4,128)S(1)}, f32[5,4,256]{2,1,0:T(4,128)}, u32[]{:S(2)}) copy-start(f32[5,4,256]{2,1,0:T(4,128)} %param.9) | copy-start | bytes 61444
  1.9 7.6 %collective-permute-start.1 = (s32[1,80,1,256]{3,1,2,0:T(8,128)S(1)}, s32[1,80,1,256]{3,1,2,0:T(8,128)S(1)}, u32[]{:S(2)}, u32[]{:S(2)}) collective-permute-start(s32[1,80,1,256]{3,1,2,0:T(8,128)S(1)} %get-tuple-element.1082), channel_id=1, source_target_pairs={{16,0},{32,16},{48,32},{64,48},{80,64},{96,80},{112,96},{128,112},... | collective-permute-start | bytes 245768 | tf_op jit(solution)/shard_map/ppermute | solution.py:21
  5.4 8.0 %copy-start.16 = (s32[4,256]{1,0:T(4,128)S(1)}, s32[4,256]{1,0:T(4,128)}, u32[]{:S(2)}) copy-start(s32[4,256]{1,0:T(4,128)} %param.11) | copy-start | bytes 12292
  5.5 22.9 %copy-start.1 = (f32[1,80,4,256]{3,1,2,0:T(8,128)}, f32[1,80,4,256]{3,1,2,0:T(8,128)S(1)}, u32[]{:S(2)}) copy-start(f32[1,80,4,256]{3,1,2,0:T(8,128)S(1)} %get-tuple-element.1095) | copy-start | bytes 983044
  5.5 22.9 %copy-start.2 = (f32[1,80,4,256]{3,1,2,0:T(8,128)}, f32[1,80,4,256]{3,1,2,0:T(8,128)S(1)}, u32[]{:S(2)}) copy-start(f32[1,80,4,256]{3,1,2,0:T(8,128)S(1)} %get-tuple-element.1096) | copy-start | bytes 983044
  6.8 21.6 %collective-permute-start.4 = (f32[7,80,1,256]{3,1,2,0:T(8,128)}, f32[7,80,1,256]{3,1,2,0:T(8,128)S(1)}, u32[]{:S(2)}, u32[]{:S(2)}) collective-permute-start(f32[7,80,1,256]{3,1,2,0:T(8,128)} %get-tuple-element.1068), channel_id=1, source_target_pairs={{0,16},{16,32},{32,48},{48,64},{64,80},{80,96},{96,112},{112,128},... | collective-permute-start | bytes 1720328 | tf_op jit(solution)/shard_map/ppermute | solution.py:19
  6.8 21.6 %collective-permute-start.5 = (f32[7,80,1,256]{3,1,2,0:T(8,128)}, f32[7,80,1,256]{3,1,2,0:T(8,128)S(1)}, u32[]{:S(2)}, u32[]{:S(2)}) collective-permute-start(f32[7,80,1,256]{3,1,2,0:T(8,128)} %get-tuple-element.1069), channel_id=1, source_target_pairs={{16,0},{32,16},{48,32},{64,48},{80,64},{96,80},{112,96},{128,112},... | collective-permute-start | bytes 1720328 | tf_op jit(solution)/shard_map/ppermute | solution.py:21
  9.4 1.8 %copy-start.8 = (s32[1,80,1,256]{3,1,2,0:T(8,128)}, s32[1,80,1,256]{3,1,2,0:T(8,128)S(1)}, u32[]{:S(2)}) copy-start(s32[1,80,1,256]{3,1,2,0:T(8,128)S(1)} %collective-permute-done) | copy-start | bytes 245764
  9.5 1.7 %copy-start.10 = (s32[1,80,1,256]{3,1,2,0:T(8,128)}, s32[1,80,1,256]{3,1,2,0:T(8,128)S(1)}, u32[]{:S(2)}) copy-start(s32[1,80,1,256]{3,1,2,0:T(8,128)S(1)} %collective-permute-done.1) | copy-start | bytes 245764
  11.2 13.4 %collective-permute-start.2 = (s32[1,80,6,1]{3,1,2,0:T(8,128)}, s32[1,80,6,1]{3,1,2,0:T(8,128)}, u32[]{:S(2)}, u32[]{:S(2)}) collective-permute-start(s32[1,80,6,1]{3,1,2,0:T(8,128)} %get-tuple-element.1077), channel_id=1, source_target_pairs={{0,1},{1,2},{2,3},{3,4},{4,5},{5,6},{6,7},{7,8},{8,9},{9,10},{10,1... | collective-permute-start | bytes 5768 | tf_op jit(solution)/shard_map/ppermute | solution.py:19
  13.4 11.2 %collective-permute-start.3 = (s32[1,80,6,1]{3,1,2,0:T(8,128)}, s32[1,80,6,1]{3,1,2,0:T(8,128)}, u32[]{:S(2)}, u32[]{:S(2)}) collective-permute-start(s32[1,80,6,1]{3,1,2,0:T(8,128)} %get-tuple-element.1078), channel_id=1, source_target_pairs={{1,0},{2,1},{3,2},{4,3},{5,4},{6,5},{7,6},{8,7},{9,8},{10,9},{11,1... | collective-permute-start | bytes 5768 | tf_op jit(solution)/shard_map/ppermute | solution.py:21
  28.4 0.9 copy-start.5
  29.3 0.8 copy-start.6
  30.3 8.6 %copy-start.7 = (pred[80,6,258]{2,0,1:T(8,128)(4,1)S(1)}, pred[80,6,258]{2,0,1:T(8,128)(4,1)}, u32[]{:S(2)}) copy-start(pred[80,6,258]{2,0,1:T(8,128)(4,1)} %get-tuple-element.1036) | copy-start | bytes 371524
  35.8 10.7 %collective-permute-start.7 = (f32[7,80,6,1]{1,3,2,0:T(1,128)}, f32[7,80,6,1]{1,3,2,0:T(1,128)}, u32[]{:S(2)}, u32[]{:S(2)}) collective-permute-start(f32[7,80,6,1]{1,3,2,0:T(1,128)} %copy.23), channel_id=1, source_target_pairs={{1,0},{2,1},{3,2},{4,3},{5,4},{6,5},{7,6},{8,7},{9,8},{10,9},{11,1... | collective-permute-start | bytes 40328 | tf_op jit(solution)/shard_map/ppermute | solution.py:21
  38.0 7.2 %collective-permute-start.6 = (f32[7,80,6,1]{1,3,2,0:T(1,128)}, f32[7,80,6,1]{1,3,2,0:T(1,128)}, u32[]{:S(2)}, u32[]{:S(2)}) collective-permute-start(f32[7,80,6,1]{1,3,2,0:T(1,128)} %copy.22), channel_id=1, source_target_pairs={{0,1},{1,2},{2,3},{3,4},{4,5},{5,6},{6,7},{7,8},{8,9},{9,10},{10,1... | collective-permute-start | bytes 40328 | tf_op jit(solution)/shard_map/ppermute | solution.py:19
  49.0 5.6 %copy-start = (f32[5,80,6,258]{3,1,2,0:T(8,128)S(1)}, f32[5,80,6,258]{3,1,2,0:T(8,128)}, u32[]{:S(2)}) copy-start(f32[5,80,6,258]{3,1,2,0:T(8,128)} %select_select_fusion) | copy-start | bytes 7430404
  49.0 5.6 %copy-start.4 = (s32[1,80,4,256]{3,1,2,0:T(8,128)S(1)}, s32[1,80,4,256]{3,1,2,0:T(8,128)}, u32[]{:S(2)}) copy-start(s32[1,80,4,256]{3,1,2,0:T(8,128)} %copy-done.3) | copy-start | bytes 983044
  49.0 5.6 %copy-start.9 = (s32[1,80,1,256]{3,1,2,0:T(8,128)S(1)}, s32[1,80,1,256]{3,1,2,0:T(8,128)}, u32[]{:S(2)}) copy-start(s32[1,80,1,256]{3,1,2,0:T(8,128)} %copy-done.8) | copy-start | bytes 245764
  49.0 5.6 %copy-start.11 = (s32[1,80,1,256]{3,1,2,0:T(8,128)S(1)}, s32[1,80,1,256]{3,1,2,0:T(8,128)}, u32[]{:S(2)}) copy-start(s32[1,80,1,256]{3,1,2,0:T(8,128)} %copy-done.10) | copy-start | bytes 245764
  88.7 2.6 %copy-start.15 = (f32[5,4,256]{2,1,0:T(4,128)S(1)}, f32[5,4,256]{2,1,0:T(4,128)}, u32[]{:S(2)}) copy-start(f32[5,4,256]{2,1,0:T(4,128)} %param.9) | copy-start | bytes 61444
where the time goes:
time: 149 us
  blocking collectives  54.2 us (36%)
  other arithmetic  54.1 us (36%)
  local copies, waits for them, and re-layouts  15.4 us (10%)
  waiting for transfers between devices  10.6 us (7%)
  starting transfers between devices  8.82 us (6%)
  between operations  5.4 us (4%)
    psum x5, blocking collectives, over_axes(): value = lax.psum(value, axis)  54.2 us
    reduce_sum x2, other arithmetic, code_sums(): jnp.sum(jnp.where(hit, prod, 0.0), axis=0)  29.3 us
    ppermute x4, waiting for transfers between devices, extended_2(): lax.ppermute(tail, axis, [(i, (i + 1) % count) for i in range(count)])  10.6 us
    concatenate x3, other arithmetic, extended_2(): jnp.concatenate([lax.ppermute(tail, axis, [(i, (i + 1) % count) for i in...  6.65 us
    ppermute x4, starting transfers between devices, extended_2(): lax.ppermute(head, axis, [((i + 1) % count, i) for i in range(count)])  5.65 us
    select_n x1, other arithmetic, code_sums(): source = jnp.where((codes == code)[None], windows[code][:, None], source)  5.64 us
    slice x4, local copies, waits for them, and re-layouts, extended_2(): lax.slice_in_dim(cells, cells.shape[dim] - width, cells.shape[dim], axis=...  5.24 us
    unnamed x209, local copies, waits for them, and re-layouts  4.1 us
  transfers between devices with their start and end apart: 8, of which 2 were waited for; matrix products, arithmetic and copies ran while one was open for 11% of the time, Pallas kernels for 0%

commit v1 on v0

v1 whole, which is shorter than its diff:
```python
import jax
import jax.numpy as jnp
from jax import lax
from jax.experimental import pallas as pl
from jax.experimental.pallas import tpu as pltpu
from jax.sharding import Mesh
from jax.sharding import PartitionSpec as P

RA = ("ra_0", "ra_1", "ra_2")
DEC = ("dec_0", "dec_1")
ALL = RA + DEC

PAIRS = [(p, q) for p in range(5) for q in range(p, 5)]
NQ = 20
VM = pl.BlockSpec(memory_space=pltpu.VMEM)
SM = pl.BlockSpec(memory_space=pltpu.SMEM)
BLOCK = (8, 128)


def blocked(x):
    lead = x.shape[:-2]
    x = x.reshape(lead + (4, 2, 128))
    x = jnp.swapaxes(x, -3, -2)
    return x.reshape(lead + BLOCK)


def unblocked(x):
    lead = x.shape[:-2]
    x = x.reshape(lead + (2, 4, 128))
    x = jnp.swapaxes(x, -3, -2)
    return x.reshape(lead + (4, 256))


def grids():
    lane = lax.broadcasted_iota(jnp.int32, BLOCK, 1)
    sub = lax.broadcasted_iota(jnp.int32, BLOCK, 0)
    return lane, sub & 3, sub >> 2


def lanes(x, by):
    by = by % 128
    return x if by == 0 else pltpu.roll(x, by, 1)


def subs(x, by):
    by = by % 8
    return x if by == 0 else pltpu.roll(x, by, 0)


def edge_kernel(params_ref, out_ref):
    lane, row, half = grids()
    out = jnp.zeros(BLOCK, jnp.float32)
    for p in range(5):
        value = params_ref[p]
        out = jnp.where(lane == p, jnp.where(half == 0, lanes(value, p), lanes(value, p + 1)), out)
    out_ref[...] = out


def column_pack(minus, plus, q, out, lane, half):
    return jnp.where(lane == q, jnp.where(half == 0, lanes(minus, q), lanes(plus, q + 1)), out)


def shift_sum(minus, mid, plus, lane, half):
    down = lanes(minus, 127)
    down = jnp.where(lane == 127, jnp.where(half == 0, subs(down, 4), 0.0), down)
    up = lanes(plus, 1)
    up = jnp.where(lane == 0, jnp.where(half == 1, subs(up, 4), 0.0), up)
    return mid + down + up


def sums_kernel(design_ref, observed_ref, weight_ref, offsets_ref, counts_ref, total_ref, edges_ref, acc_ref):
    lane, row, half = grids()
    counts = counts_ref[...]
    for code in range(9):

        def body(k, acc, code=code):
            hit = (offsets_ref[k] == code) & (counts > k)
            w = jnp.where(hit, weight_ref[k], 0.0)
            d = [design_ref[p, k] for p in range(5)]
            o = observed_ref[k]
            wd = [w * x for x in d]
            new = [wd[p] * o for p in range(5)] + [wd[p] * d[q] for p, q in PAIRS]
            return tuple(a + b for a, b in zip(acc, new))

        acc = lax.fori_loop(0, 80, body, (jnp.zeros(BLOCK, jnp.float32),) * NQ, unroll=4)
        for q in range(NQ):
            acc_ref[code, q] = acc[q]
    inner = jnp.zeros(BLOCK, jnp.float32)
    outer = jnp.zeros(BLOCK, jnp.float32)
    low = [jnp.zeros(BLOCK, jnp.float32) for _ in range(5)]
    high = [jnp.zeros(BLOCK, jnp.float32) for _ in range(5)]
    for q in range(NQ):
        stay = []
        leave = []
        for b in range(3):
            back, same, ahead = acc_ref[b, q], acc_ref[3 + b, q], acc_ref[6 + b, q]
            stay.append(
                same + jnp.where(row < 3, subs(back, 7), 0.0) + jnp.where(row > 0, subs(ahead, 1), 0.0)
            )
            leave.append(jnp.where(row == 0, back, jnp.where(row == 3, ahead, 0.0)))
        total_ref[q] = shift_sum(*stay, lane, half)
        inner = column_pack(stay[0], stay[2], q, inner, lane, half)
        outer = column_pack(leave[0], leave[2], q, outer, lane, half)
        out = shift_sum(*leave, lane, half)
        g, i = divmod(q, 4)
        low[g] = jnp.where(row == i, subs(out, i), low[g])
        high[g] = jnp.where(row == i, subs(out, i - 3), high[g])
    for g in range(5):
        edges_ref[g] = low[g]
        edges_ref[5 + g] = high[g]
    edges_ref[10] = outer
    total_ref[NQ] = inner


def message_kernel(params_ref, edges_ref, dec_a_ref, dec_b_ref, to_a_ref, to_b_ref, halo_ref):
    lane, row, half = grids()
    dec_odd = lax.axis_index("dec_1")
    ra_odd = lax.axis_index("ra_2")
    halo = jnp.where((half == 0) == (dec_odd == 0), dec_a_ref[...], dec_b_ref[...])
    halo_ref[...] = halo
    low = [edges_ref[g] for g in range(5)] + [jnp.zeros(BLOCK, jnp.float32) for _ in range(2)]
    high = [edges_ref[5 + g] for g in range(5)] + [jnp.zeros(BLOCK, jnp.float32) for _ in range(2)]
    for p in range(5):
        g, i = divmod(NQ + p, 4)
        value = params_ref[p]
        low[g] = jnp.where(row == i, subs(value, i), low[g])
        high[g] = jnp.where(row == i, subs(value, i - 3), high[g])
    for g in range(7):
        to_a_ref[g] = jnp.where(ra_odd == 0, high[g], low[g])
        to_b_ref[g] = jnp.where(ra_odd == 0, low[g], high[g])
    for ref in (to_a_ref, to_b_ref):
        ref[7] = edges_ref[10]
        ref[8] = halo


def chi_kernel(
    design_ref, observed_ref, weight_ref, offsets_ref, counts_ref, params_ref,
    total_ref, from_a_ref, from_b_ref, halo_ref, total_out_ref, send_ref, win_ref,
):
    lane, row, half = grids()
    ra_odd = lax.axis_index("ra_2")
    dec = lax.axis_index(DEC)
    me = lax.axis_index(RA) * 16 + dec

    def from_low(g):
        return jnp.where(ra_odd == 0, from_b_ref[g], from_a_ref[g])

    def from_high(g):
        return jnp.where(ra_odd == 0, from_a_ref[g], from_b_ref[g])

    halo = halo_ref[...]
    around = [
        jnp.where(row == 0, subs(from_low(8), 5), subs(halo, 1)),
        halo,
        jnp.where(row == 3, subs(from_high(8), 3), subs(halo, 7)),
    ]
    around = [subs(x, 4) for x in around]
    for p in range(5):
        g, i = divmod(NQ + p, 4)
        value = params_ref[p]
        shifted = [
            jnp.where(row == 0, subs(from_low(g), -i), subs(value, 1)),
            value,
            jnp.where(row == 3, subs(from_high(g), 3 - i), subs(value, 7)),
        ]
        for a in range(3):
            x = shifted[a]
            y = lanes(x, 1)
            y = jnp.where(lane == 0, jnp.where(half == 1, subs(y, 4), lanes(around[a], -p)), y)
            win_ref[3 * a, p] = y
            win_ref[3 * a + 1, p] = x
            y = lanes(x, 127)
            y = jnp.where(lane == 127, jnp.where(half == 0, subs(y, 4), lanes(around[a], 127 - p)), y)
            win_ref[3 * a + 2, p] = y

    counts = counts_ref[...]

    def body(k, acc):
        code = offsets_ref[k]
        hits = [code == c for c in range(1, 9)]
        resid = observed_ref[k]
        for p in range(5):
            source = win_ref[0, p]
            for c in range(1, 9):
                source = jnp.where(hits[c - 1], win_ref[c, p], source)
            resid = resid - design_ref[p, k] * source
        w = jnp.where(counts > k, weight_ref[k], 0.0)
        return acc + w * resid * resid

    chi = jnp.sum(lax.fori_loop(0, 80, body, jnp.zeros(BLOCK, jnp.float32), unroll=4))
    count = jnp.sum(counts.astype(jnp.float32))

    for q in range(NQ):
        g, i = divmod(q, 4)
        total_out_ref[q] = (
            total_ref[q]
            + jnp.where(row == 0, subs(from_low(g), -i), 0.0)
            + jnp.where(row == 3, subs(from_high(g), 3 - i), 0.0)
        )
    column = (
        total_ref[NQ]
        + jnp.where(row == 0, subs(from_low(7), 5), 0.0)
        + jnp.where(row == 3, subs(from_high(7), 3), 0.0)
    )
    column = jnp.where(lane < NQ, column, 0.0)
    flat = column
    for r in range(1, 4):
        flat = jnp.where(row == r, lanes(column, 32 * r), flat)
    down = jnp.sum(jnp.where(half == 0, flat, 0.0), axis=0, keepdims=True)
    up = jnp.sum(jnp.where(half == 1, flat, 0.0), axis=0, keepdims=True)
    base = jnp.where(lane == NQ, chi, jnp.where(lane == NQ + 1, count, 0.0))
    for g in range(32):
        send_ref[pl.ds(8 * g, 8), :] = base

    @pl.when(dec > 0)
    def _():
        send_ref[pl.ds(me - 1, 1), :] = base[:1] + down

    @pl.when(dec < 15)
    def _():
        send_ref[pl.ds(me + 1, 1), :] = base[:1] + up


def solve(rhs, normal):
    lower = [[None] * 5 for _ in range(5)]
    inverse = [None] * 5
    for first in range(5):
        for second in range(first + 1):
            running = normal[second][first]
            for inner in range(second):
                running = running - lower[first][inner] * lower[second][inner]
            if first == second:
                inverse[first] = 1.0 / jnp.sqrt(running)
            else:
                lower[first][second] = running * inverse[second]
    forward = []
    for first in range(5):
        running = rhs[first]
        for inner in range(first):
            running = running - lower[first][inner] * forward[inner]
        forward.append(running * inverse[first])
    answer = [None] * 5
    for first in range(4, -1, -1):
        running = forward[first]
        for inner in range(first + 1, 5):
            running = running - lower[inner][first] * answer[inner]
        answer[first] = running * inverse[first]
    return answer


def solve_kernel(params_ref, total_ref, got_ref, new_ref, chi_ref):
    lane, row, half = grids()
    me = lax.axis_index(ALL)

    def column(source):
        line = jnp.broadcast_to(got_ref[pl.ds(source, 1), :], BLOCK)
        out = line
        for r in range(1, 4):
            out = jnp.where(row == r, lanes(line, -32 * r), out)
        return out

    from_low = column(jnp.maximum(me - 1, 0))
    from_high = column(jnp.minimum(me + 1, 255))
    sums = []
    for q in range(NQ):
        sums.append(
            total_ref[q]
            + jnp.where((lane == 0) & (half == 0), lanes(from_low, -q), 0.0)
            + jnp.where((lane == 127) & (half == 1), lanes(from_high, 127 - q), 0.0)
        )
    normal = [[None] * 5 for _ in range(5)]
    for place, (p, q) in enumerate(PAIRS):
        normal[p][q] = sums[5 + place]
        normal[q][p] = sums[5 + place]
    params = [params_ref[p] for p in range(5)]
    rhs = []
    for p in range(5):
        running = sums[p]
        for q in range(5):
            running = running - normal[p][q] * params[q]
        rhs.append(running)
    for p in range(5):
        normal[p][p] = normal[p][p] + 1.0
    delta = solve(rhs, normal)
    for p in range(5):
        new_ref[p] = params[p] + delta[p]
    all_sums = got_ref[pl.ds(0, 8), :]
    for g in range(1, 32):
        all_sums = all_sums + got_ref[pl.ds(8 * g, 8), :]
    chi = jnp.sum(jnp.where(lane == NQ, all_sums, 0.0))
    count = jnp.sum(jnp.where(lane == NQ + 1, all_sums, 0.0))
    chi_ref[0, 0] = chi / count


def exchange(value, axes, pairs):
    both = [(i, j) for i, j in pairs] + [(j, i) for i, j in pairs]
    return lax.ppermute(value, axes, both)


def f32(*shape):
    return jax.ShapeDtypeStruct(shape, jnp.float32)


def call(kernel, outs, n_in, scratch=(), flops=1000, smem_last=False):
    specs = [VM] * len(outs)
    if smem_last:
        specs[-1] = SM
    return pl.pallas_call(
        kernel,
        out_shape=tuple(outs),
        in_specs=[VM] * n_in,
        out_specs=tuple(specs),
        scratch_shapes=list(scratch),
        cost_estimate=pl.CostEstimate(flops=flops, bytes_accessed=100000, transcendentals=0),
    )


def per_device(design, observed, weight, params, offsets, counts):
    design, observed, weight, params, offsets, counts = (
        blocked(x) for x in (design, observed, weight, params, offsets, counts)
    )
    (edge,) = call(edge_kernel, [f32(*BLOCK)], 1)(params)
    dec_b = exchange(edge, DEC, [(i, i + 1) for i in range(1, 15, 2)])
    dec_a = exchange(edge, DEC, [(i, i + 1) for i in range(0, 16, 2)])
    total, edges = call(
        sums_kernel, [f32(NQ + 1, *BLOCK), f32(11, *BLOCK)], 5,
        [pltpu.VMEM((9, NQ) + BLOCK, jnp.float32)], 30_000_000,
    )(design, observed, weight, offsets, counts)
    to_a, to_b, halo = call(message_kernel, [f32(9, *BLOCK), f32(9, *BLOCK), f32(*BLOCK)], 4)(
        params, edges, dec_a, dec_b
    )
    from_b = exchange(to_b, RA, [(i, (i + 1) % 16) for i in range(1, 16, 2)])
    from_a = exchange(to_a, RA, [(i, i + 1) for i in range(0, 16, 2)])
    total, send = call(
        chi_kernel, [f32(NQ, *BLOCK), f32(256, 128)], 10,
        [pltpu.VMEM((9, 5) + BLOCK, jnp.float32)], 5_000_000,
    )(design, observed, weight, offsets, counts, params, total, from_a, from_b, halo)
    got = lax.all_to_all(send.reshape(256, 1, 128), ALL, 0, 0, tiled=True).reshape(256, 128)
    new, chi = call(solve_kernel, [f32(5, *BLOCK), f32(1, 1)], 3, (), 100000, True)(params, total, got)
    return unblocked(new), chi.reshape(())


def solution(mesh):
    finer = Mesh(mesh.devices.reshape(2, 4, 2, 8, 2), ALL)
    return jax.shard_map(
        per_device,
        mesh=finer,
        in_specs=(
            P(None, None, RA, DEC),
            P(None, RA, DEC),
            P(None, RA, DEC),
            P(None, RA, DEC),
            P(None, RA, DEC),
            P(RA, DEC),
        ),
        out_specs=(P(None, RA, DEC), P()),
        check_vma=False,
    )
```

time: 149 us -> 59.3 us (0.40)
  the two profiles are of different devices: /device:TPU:14 before, /device:TPU:1 now
where the time goes in v1:
time: 59.3 us; the launch traced here: 58.9 us
  blocking collectives  29.9 us (50%)
  Pallas kernels  16.7 us (28%)
  starting transfers between devices  8.04 us (14%)
  waiting for transfers between devices  2.41 us (4%)
  local copies, waits for them, and re-layouts  1.19 us (2%)
  between operations  0.66 us (1%)
    all_to_all x1, blocking collectives, per_device(): lax.all_to_all(send.reshape(256, 1, 128), ALL, 0, 0, tiled=True)  29.9 us
    pallas_call x1, Pallas kernels, per_device(): call(sums_kernel, [f32(NQ + 1, *BLOCK), f32(11, *BLOCK)], 5, [pltpu.VMEM(...  8.41 us
    ppermute x4, starting transfers between devices, exchange(): return lax.ppermute(value, axes, both)  8.04 us
    pallas_call x1, Pallas kernels, per_device(): call(chi_kernel, [f32(NQ, *BLOCK), f32(256, 128)], 10, [pltpu.VMEM((9, 5)...  3.59 us
    ppermute x4, waiting for transfers between devices, exchange(): return lax.ppermute(value, axes, both)  2.41 us
    pallas_call x1, Pallas kernels, per_device(): call(solve_kernel, [f32(5, *BLOCK), f32(1, 1)], 3, (), 100000, True)  1.86 us
    pallas_call x1, Pallas kernels, per_device(): call(message_kernel, [f32(9, *BLOCK), f32(9, *BLOCK), f32(*BLOCK)], 4)  1.45 us
    pallas_call x1, Pallas kernels, per_device(): edge, = call(edge_kernel, [f32(*BLOCK)], 1)(params)  1.4 us
  transfers between devices with their start and end apart: 4, of which 1 were waited for; matrix products, arithmetic and copies ran while one was open for 0% of the time, Pallas kernels for 14%

profile of v1, /device:TPU:1, one launch (start us, length us, event | category | flops | bytes accessed | tf_op | source)
XLA Modules:
  0.0 58.9 jit_solution(8505759418831249531)
XLA Ops:
  0.6 1.4 %shard_map.78 = f32[8,128]{1,0:T(8,128)} custom-call(f32[5,8,128]{2,1,0:T(8,128)} %bitcast.49), custom_call_target="tpu_custom_call" | custom-call | flops 1000 | bytes 100000 | tf_op jit(solution)/shard_map/pallas_call | solution.py:322
  2.0 0.6 %collective-permute-start.1 = (f32[8,128]{1,0:T(8,128)}, f32[8,128]{1,0:T(8,128)S(1)}, u32[]{:S(2)}, u32[]{:S(2)}) collective-permute-start(f32[8,128]{1,0:T(8,128)} %shard_map.78), channel_id=1, source_target_pairs={{1,2},{3,4},{5,6},{7,8},{9,10},{11,12},{13,14},{2,1},{4,3},{6,5},{... | collective-permute-start | bytes 12296 | tf_op jit(solution)/shard_map/ppermute | solution.py:297
  2.7 5.0 %collective-permute-start = (f32[8,128]{1,0:T(8,128)}, f32[8,128]{1,0:T(8,128)S(1)}, u32[]{:S(2)}, u32[]{:S(2)}) collective-permute-start(f32[8,128]{1,0:T(8,128)} %shard_map.78), channel_id=1, source_target_pairs={{0,1},{2,3},{4,5},{6,7},{8,9},{10,11},{12,13},{14,15},{1,0},{3,2},... | collective-permute-start | bytes 12296 | tf_op jit(solution)/shard_map/ppermute | solution.py:297
  7.7 8.4 %shard_map.77 = (f32[21,8,128]{2,1,0:T(8,128)}, f32[11,8,128]{2,1,0:T(8,128)}) custom-call(f32[5,80,8,128]{3,2,1,0:T(8,128)} %bitcast.40, f32[80,8,128]{2,1,0:T(8,128)} %bitcast.42, f32[80,8,128]{2,1,0:T(8,128)} %bitcast.44, s32[80,8,128]{2,1,0:T(8,128)} %bitcast.46, s32[8,128]{1,0:T(8,128)} %bitcast.54), custom_call_target="tpu_custom_call" | custom-call | flops 30000000 | bytes 100000 | tf_op jit(solution)/shard_map/pallas_call | solution.py:325
  16.1 0.0 collective-permute-done.1.dec_b_ref
  16.1 0.0 copy-start.2
  16.1 0.0 collective-permute-done.dec_a_ref
  16.1 0.0 copy-start.3
  16.1 0.6 copy-done.2
  16.7 0.0 copy-done.3
  16.7 1.5 %shard_map.79 = (f32[9,8,128]{2,1,0:T(8,128)}, f32[9,8,128]{2,1,0:T(8,128)}, f32[8,128]{1,0:T(8,128)}) custom-call(f32[5,8,128]{2,1,0:T(8,128)} %bitcast.50, f32[11,8,128]{2,1,0:T(8,128)} %get-tuple-element.12.edges_ref, f32[8,128]{1,0:T(8,128)} %copy-done.3, f32[8,128]{1,0:T(8,128)} %copy-done.2), custom_call_target="tpu_custom_call" | custom-call | flops 1000 | bytes 100000 | tf_op jit(solution)/shard_map/pallas_call | solution.py:329
  18.1 1.2 %collective-permute-start.2 = (f32[9,8,128]{2,1,0:T(8,128)}, f32[9,8,128]{2,1,0:T(8,128)S(1)}, u32[]{:S(2)}, u32[]{:S(2)}) collective-permute-start(f32[9,8,128]{2,1,0:T(8,128)} %get-tuple-element.13), channel_id=1, source_target_pairs={{0,16},{32,48},{64,80},{96,112},{128,144},{160,176},{192,208},{224... | collective-permute-start | bytes 110600 | tf_op jit(solution)/shard_map/ppermute | solution.py:297
  19.4 1.2 %collective-permute-start.3 = (f32[9,8,128]{2,1,0:T(8,128)}, f32[9,8,128]{2,1,0:T(8,128)S(1)}, u32[]{:S(2)}, u32[]{:S(2)}) collective-permute-start(f32[9,8,128]{2,1,0:T(8,128)} %get-tuple-element.14), channel_id=1, source_target_pairs={{16,32},{48,64},{80,96},{112,128},{144,160},{176,192},{208,224},{2... | collective-permute-start | bytes 110600 | tf_op jit(solution)/shard_map/ppermute | solution.py:297
  20.5 0.0 collective-permute-done.2.from_a_ref
  20.5 0.0 copy-start
  20.5 2.4 %collective-permute-done.3.from_b_ref = f32[9,8,128]{2,1,0:T(8,128)S(1)} collective-permute-done((f32[9,8,128]{2,1,0:T(8,128)}, f32[9,8,128]{2,1,0:T(8,128)S(1)}, u32[]{:S(2)}, u32[]{:S(2)}) %collective-permute-start.3) | collective-permute-done | bytes 36896 | tf_op jit(solution)/shard_map/ppermute | solution.py:297
  23.0 0.0 copy-start.1
  23.0 0.0 copy-done
  23.0 0.6 %copy-done.1 = f32[9,8,128]{2,1,0:T(8,128)} copy-done((f32[9,8,128]{2,1,0:T(8,128)}, f32[9,8,128]{2,1,0:T(8,128)S(1)}, u32[]{:S(2)}) %copy-start.1) | copy-done | bytes 36888
  23.6 3.6 %shard_map.80 = (f32[20,8,128]{2,1,0:T(8,128)}, f32[256,128]{1,0:T(8,128)}) custom-call(f32[5,80,8,128]{3,2,1,0:T(8,128)} %bitcast.41, f32[80,8,128]{2,1,0:T(8,128)} %bitcast.43, f32[80,8,128]{2,1,0:T(8,128)} %bitcast.45, s32[80,8,128]{2,1,0:T(8,128)} %bitcast.47, s32[8,128]{1,0:T(8,128)} %bitcast.55, f32[5,8,128]{2,1,0:T(8,128)} %bitcast.51, ...), custom_call_target="tpu_custom_call" | custom-call | flops 5000000 | bytes 100000 | tf_op jit(solution)/shard_map/pallas_call | solution.py:334
  27.1 29.9 %all_to_all.5 = f32[256,1,128]{2,1,0:T(1,128)} all-to-all(f32[256,1,128]{2,1,0:T(1,128)} %bitcast.53), channel_id=1, replica_groups=mesh['ra_0'=2,'ra_1'=4,'ra_2'=2,'dec_0'=8,'dec_1'=2] {'ra_0','ra_1','ra_..., dimensions={0} | all-to-all | bytes 262144 | tf_op jit(solution)/shard_map/all_to_all | solution.py:338
  57.1 1.9 %shard_map.81 = (f32[5,8,128]{2,1,0:T(8,128)}, f32[1,1]{1,0:T(1,128)}) custom-call(f32[5,8,128]{2,1,0:T(8,128)} %bitcast.52, f32[20,8,128]{2,1,0:T(8,128)} %get-tuple-element.16.total_ref, f32[256,128]{1,0:T(8,128)} %bitcast.48), custom_call_target="tpu_custom_call" | custom-call | flops 100000 | bytes 100000 | tf_op jit(solution)/shard_map/pallas_call | solution.py:339
Async XLA Ops:
  2.0 14.0 %collective-permute-start.1 = (f32[8,128]{1,0:T(8,128)}, f32[8,128]{1,0:T(8,128)S(1)}, u32[]{:S(2)}, u32[]{:S(2)}) collective-permute-start(f32[8,128]{1,0:T(8,128)} %shard_map.78), channel_id=1, source_target_pairs={{1,2},{3,4},{5,6},{7,8},{9,10},{11,12},{13,14},{2,1},{4,3},{6,5},{... | collective-permute-start | bytes 12296 | tf_op jit(solution)/shard_map/ppermute | solution.py:297
  2.7 13.4 %collective-permute-start = (f32[8,128]{1,0:T(8,128)}, f32[8,128]{1,0:T(8,128)S(1)}, u32[]{:S(2)}, u32[]{:S(2)}) collective-permute-start(f32[8,128]{1,0:T(8,128)} %shard_map.78), channel_id=1, source_target_pairs={{0,1},{2,3},{4,5},{6,7},{8,9},{10,11},{12,13},{14,15},{1,0},{3,2},... | collective-permute-start | bytes 12296 | tf_op jit(solution)/shard_map/ppermute | solution.py:297
  16.1 0.6 %copy-start.2 = (f32[8,128]{1,0:T(8,128)}, f32[8,128]{1,0:T(8,128)S(1)}, u32[]{:S(2)}) copy-start(f32[8,128]{1,0:T(8,128)S(1)} %collective-permute-done.1.dec_b_ref) | copy-start | bytes 12292
  16.1 0.6 %copy-start.3 = (f32[8,128]{1,0:T(8,128)}, f32[8,128]{1,0:T(8,128)S(1)}, u32[]{:S(2)}) copy-start(f32[8,128]{1,0:T(8,128)S(1)} %collective-permute-done.dec_a_ref) | copy-start | bytes 12292
  18.1 2.4 %collective-permute-start.2 = (f32[9,8,128]{2,1,0:T(8,128)}, f32[9,8,128]{2,1,0:T(8,128)S(1)}, u32[]{:S(2)}, u32[]{:S(2)}) collective-permute-start(f32[9,8,128]{2,1,0:T(8,128)} %get-tuple-element.13), channel_id=1, source_target_pairs={{0,16},{32,48},{64,80},{96,112},{128,144},{160,176},{192,208},{224... | collective-permute-start | bytes 110600 | tf_op jit(solution)/shard_map/ppermute | solution.py:297
  19.4 3.6 %collective-permute-start.3 = (f32[9,8,128]{2,1,0:T(8,128)}, f32[9,8,128]{2,1,0:T(8,128)S(1)}, u32[]{:S(2)}, u32[]{:S(2)}) collective-permute-start(f32[9,8,128]{2,1,0:T(8,128)} %get-tuple-element.14), channel_id=1, source_target_pairs={{16,32},{48,64},{80,96},{112,128},{144,160},{176,192},{208,224},{2... | collective-permute-start | bytes 110600 | tf_op jit(solution)/shard_map/ppermute | solution.py:297
  20.5 2.4 %copy-start = (f32[9,8,128]{2,1,0:T(8,128)}, f32[9,8,128]{2,1,0:T(8,128)S(1)}, u32[]{:S(2)}) copy-start(f32[9,8,128]{2,1,0:T(8,128)S(1)} %collective-permute-done.2.from_a_ref) | copy-start | bytes 110596
  23.0 0.6 %copy-start.1 = (f32[9,8,128]{2,1,0:T(8,128)}, f32[9,8,128]{2,1,0:T(8,128)S(1)}, u32[]{:S(2)}) copy-start(f32[9,8,128]{2,1,0:T(8,128)S(1)} %collective-permute-done.3.from_b_ref) | copy-start | bytes 110596

commit v2 on v1

--- a/solution.py
+++ b/solution.py
@@ -12,6 +12,7 @@
 
 PAIRS = [(p, q) for p in range(5) for q in range(p, 5)]
 NQ = 20
+EDGE_FLOPS = 20_000_000_000
 VM = pl.BlockSpec(memory_space=pltpu.VMEM)
 SM = pl.BlockSpec(memory_space=pltpu.SMEM)
 BLOCK = (8, 128)
@@ -68,115 +69,99 @@
     return mid + down + up
 
 
-def sums_kernel(design_ref, observed_ref, weight_ref, offsets_ref, counts_ref, total_ref, edges_ref, acc_ref):
+def accumulate(design_ref, observed_ref, weight_ref, code_ref, wanted):
+    def body(k, acc):
+        w = jnp.where(code_ref[k] == wanted, weight_ref[k], 0.0)
+        d = [design_ref[p, k] for p in range(5)]
+        o = observed_ref[k]
+        wd = [w * x for x in d]
+        new = [wd[p] * o for p in range(5)] + [wd[p] * d[q] for p, q in PAIRS]
+        return tuple(x + y for x, y in zip(acc, new))
+
+    return lax.fori_loop(0, 80, body, (jnp.zeros(BLOCK, jnp.float32),) * NQ, unroll=4)
+
+
+def edge_code(b, row):
+    return jnp.where(row == 0, b, jnp.where(row == 3, 6 + b, -1))
+
+
+def leave_kernel(
+    design_ref, observed_ref, weight_ref, offsets_ref, counts_ref, params_ref,
+    to_a_ref, to_b_ref, code_ref, acc_ref,
+):
     lane, row, half = grids()
     counts = counts_ref[...]
-    for code in range(9):
-
-        def body(k, acc, code=code):
-            hit = (offsets_ref[k] == code) & (counts > k)
-            w = jnp.where(hit, weight_ref[k], 0.0)
-            d = [design_ref[p, k] for p in range(5)]
-            o = observed_ref[k]
-            wd = [w * x for x in d]
-            new = [wd[p] * o for p in range(5)] + [wd[p] * d[q] for p, q in PAIRS]
-            return tuple(a + b for a, b in zip(acc, new))
-
-        acc = lax.fori_loop(0, 80, body, (jnp.zeros(BLOCK, jnp.float32),) * NQ, unroll=4)
+    ra_odd = lax.axis_index("ra_2")
+
+    def mark(k, carry):
+        code_ref[k] = jnp.where(counts > k, offsets_ref[k], 9)
+        return carry
+
+    lax.fori_loop(0, 80, mark, 0, unroll=8)
+    for b in range(3):
+        acc = accumulate(design_ref, observed_ref, weight_ref, code_ref, edge_code(b, row))
         for q in range(NQ):
-            acc_ref[code, q] = acc[q]
-    inner = jnp.zeros(BLOCK, jnp.float32)
+            acc_ref[b, q] = acc[q]
     outer = jnp.zeros(BLOCK, jnp.float32)
-    low = [jnp.zeros(BLOCK, jnp.float32) for _ in range(5)]
-    high = [jnp.zeros(BLOCK, jnp.float32) for _ in range(5)]
-    for q in range(NQ):
-        stay = []
-        leave = []
-        for b in range(3):
-            back, same, ahead = acc_ref[b, q], acc_ref[3 + b, q], acc_ref[6 + b, q]
-            stay.append(
-                same + jnp.where(row < 3, subs(back, 7), 0.0) + jnp.where(row > 0, subs(ahead, 1), 0.0)
-            )
-            leave.append(jnp.where(row == 0, back, jnp.where(row == 3, ahead, 0.0)))
-        total_ref[q] = shift_sum(*stay, lane, half)
-        inner = column_pack(stay[0], stay[2], q, inner, lane, half)
-        outer = column_pack(leave[0], leave[2], q, outer, lane, half)
-        out = shift_sum(*leave, lane, half)
+    low = [jnp.zeros(BLOCK, jnp.float32) for _ in range(7)]
+    high = [jnp.zeros(BLOCK, jnp.float32) for _ in range(7)]
+    for q in range(NQ + 5):
+        if q < NQ:
+            leave = [acc_ref[b, q] for b in range(3)]
+            outer = column_pack(leave[0], leave[2], q, outer, lane, half)
+            value = shift_sum(*leave, lane, half)
+        else:
+            value = params_ref[q - NQ]
         g, i = divmod(q, 4)
-        low[g] = jnp.where(row == i, subs(out, i), low[g])
-        high[g] = jnp.where(row == i, subs(out, i - 3), high[g])
-    for g in range(5):
-        edges_ref[g] = low[g]
-        edges_ref[5 + g] = high[g]
-    edges_ref[10] = outer
-    total_ref[NQ] = inner
-
-
-def message_kernel(params_ref, edges_ref, dec_a_ref, dec_b_ref, to_a_ref, to_b_ref, halo_ref):
-    lane, row, half = grids()
-    dec_odd = lax.axis_index("dec_1")
-    ra_odd = lax.axis_index("ra_2")
-    halo = jnp.where((half == 0) == (dec_odd == 0), dec_a_ref[...], dec_b_ref[...])
-    halo_ref[...] = halo
-    low = [edges_ref[g] for g in range(5)] + [jnp.zeros(BLOCK, jnp.float32) for _ in range(2)]
-    high = [edges_ref[5 + g] for g in range(5)] + [jnp.zeros(BLOCK, jnp.float32) for _ in range(2)]
-    for p in range(5):
-        g, i = divmod(NQ + p, 4)
-        value = params_ref[p]
         low[g] = jnp.where(row == i, subs(value, i), low[g])
         high[g] = jnp.where(row == i, subs(value, i - 3), high[g])
     for g in range(7):
         to_a_ref[g] = jnp.where(ra_odd == 0, high[g], low[g])
         to_b_ref[g] = jnp.where(ra_odd == 0, low[g], high[g])
     for ref in (to_a_ref, to_b_ref):
-        ref[7] = edges_ref[10]
-        ref[8] = halo
-
-
-def chi_kernel(
-    design_ref, observed_ref, weight_ref, offsets_ref, counts_ref, params_ref,
-    total_ref, from_a_ref, from_b_ref, halo_ref, total_out_ref, send_ref, win_ref,
+        ref[7] = outer
+        ref[8] = jnp.zeros(BLOCK, jnp.float32)
+
+
+def halo_kernel(dec_a_ref, dec_b_ref, in_a_ref, in_b_ref, to_a_ref, to_b_ref, halo_ref):
+    lane, row, half = grids()
+    dec_odd = lax.axis_index("dec_1")
+    halo = jnp.where((half == 0) == (dec_odd == 0), dec_a_ref[...], dec_b_ref[...])
+    halo_ref[...] = halo
+    for g in range(8):
+        to_a_ref[g] = in_a_ref[g]
+        to_b_ref[g] = in_b_ref[g]
+    to_a_ref[8] = halo
+    to_b_ref[8] = halo
+
+
+def columns_around(x, beyond, p, lane, half):
+    below = lanes(x, 1)
+    below = jnp.where(lane == 0, jnp.where(half == 1, subs(below, 4), lanes(beyond, -p)), below)
+    above = lanes(x, 127)
+    above = jnp.where(lane == 127, jnp.where(half == 0, subs(above, 4), lanes(beyond, 127 - p)), above)
+    return below, x, above
+
+
+def stay_kernel(
+    design_ref, observed_ref, weight_ref, code_ref, params_ref, halo_ref,
+    total_ref, acc_ref, win_ref,
 ):
     lane, row, half = grids()
-    ra_odd = lax.axis_index("ra_2")
-    dec = lax.axis_index(DEC)
-    me = lax.axis_index(RA) * 16 + dec
-
-    def from_low(g):
-        return jnp.where(ra_odd == 0, from_b_ref[g], from_a_ref[g])
-
-    def from_high(g):
-        return jnp.where(ra_odd == 0, from_a_ref[g], from_b_ref[g])
-
-    halo = halo_ref[...]
-    around = [
-        jnp.where(row == 0, subs(from_low(8), 5), subs(halo, 1)),
-        halo,
-        jnp.where(row == 3, subs(from_high(8), 3), subs(halo, 7)),
-    ]
-    around = [subs(x, 4) for x in around]
-    for p in range(5):
-        g, i = divmod(NQ + p, 4)
+    halo = subs(halo_ref[...], 4)
+    for p in range(5):
         value = params_ref[p]
-        shifted = [
-            jnp.where(row == 0, subs(from_low(g), -i), subs(value, 1)),
-            value,
-            jnp.where(row == 3, subs(from_high(g), 3 - i), subs(value, 7)),
-        ]
         for a in range(3):
-            x = shifted[a]
-            y = lanes(x, 1)
-            y = jnp.where(lane == 0, jnp.where(half == 1, subs(y, 4), lanes(around[a], -p)), y)
-            win_ref[3 * a, p] = y
-            win_ref[3 * a + 1, p] = x
-            y = lanes(x, 127)
-            y = jnp.where(lane == 127, jnp.where(half == 0, subs(y, 4), lanes(around[a], 127 - p)), y)
-            win_ref[3 * a + 2, p] = y
-
-    counts = counts_ref[...]
+            shift = (1, 0, 7)[a]
+            found = columns_around(subs(value, shift), subs(halo, shift), p, lane, half)
+            for b in range(3):
+                win_ref[3 * a + b, p] = found[b]
+
+    least = jnp.where(row == 0, 3, 0)
+    most = jnp.where(row == 3, 5, 8)
 
     def body(k, acc):
-        code = offsets_ref[k]
+        code = code_ref[k]
         hits = [code == c for c in range(1, 9)]
         resid = observed_ref[k]
         for p in range(5):
@@ -184,11 +169,67 @@
             for c in range(1, 9):
                 source = jnp.where(hits[c - 1], win_ref[c, p], source)
             resid = resid - design_ref[p, k] * source
-        w = jnp.where(counts > k, weight_ref[k], 0.0)
+        inside = (code >= least) & (code <= most)
+        w = jnp.where(inside, weight_ref[k], 0.0)
         return acc + w * resid * resid
 
-    chi = jnp.sum(lax.fori_loop(0, 80, body, jnp.zeros(BLOCK, jnp.float32), unroll=4))
-    count = jnp.sum(counts.astype(jnp.float32))
+    total_ref[NQ + 1] = lax.fori_loop(0, 80, body, jnp.zeros(BLOCK, jnp.float32), unroll=4)
+    for code in range(9):
+        acc = accumulate(design_ref, observed_ref, weight_ref, code_ref, code)
+        for q in range(NQ):
+            acc_ref[code, q] = acc[q]
+    inner = jnp.zeros(BLOCK, jnp.float32)
+    for q in range(NQ):
+        stay = []
+        for b in range(3):
+            back, same, ahead = acc_ref[b, q], acc_ref[3 + b, q], acc_ref[6 + b, q]
+            stay.append(
+                same + jnp.where(row < 3, subs(back, 7), 0.0) + jnp.where(row > 0, subs(ahead, 1), 0.0)
+            )
+        total_ref[q] = shift_sum(*stay, lane, half)
+        inner = column_pack(stay[0], stay[2], q, inner, lane, half)
+    total_ref[NQ] = inner
+
+
+def chi_kernel(
+    design_ref, observed_ref, weight_ref, code_ref, counts_ref,
+    total_ref, from_a_ref, from_b_ref, total_out_ref, send_ref, win_ref,
+):
+    lane, row, half = grids()
+    ra_odd = lax.axis_index("ra_2")
+    dec = lax.axis_index(DEC)
+    me = lax.axis_index(RA) * 16 + dec
+
+    def from_low(g):
+        return jnp.where(ra_odd == 0, from_b_ref[g], from_a_ref[g])
+
+    def from_high(g):
+        return jnp.where(ra_odd == 0, from_a_ref[g], from_b_ref[g])
+
+    beyond = subs(jnp.where(row == 0, subs(from_low(8), 5), subs(from_high(8), 3)), 4)
+    for p in range(5):
+        g, i = divmod(NQ + p, 4)
+        value = jnp.where(row == 0, subs(from_low(g), -i), subs(from_high(g), 3 - i))
+        found = columns_around(value, beyond, p, lane, half)
+        for b in range(3):
+            win_ref[b, p] = found[b]
+
+    wanted = [edge_code(b, row) for b in range(3)]
+
+    def body(k, acc):
+        code = code_ref[k]
+        hits = [code == x for x in wanted]
+        resid = observed_ref[k]
+        for p in range(5):
+            source = jnp.where(hits[1], win_ref[1, p], win_ref[0, p])
+            source = jnp.where(hits[2], win_ref[2, p], source)
+            resid = resid - design_ref[p, k] * source
+        outside = hits[0] | hits[1] | hits[2]
+        w = jnp.where(outside, weight_ref[k], 0.0)
+        return acc + w * resid * resid
+
+    chi = jnp.sum(lax.fori_loop(0, 80, body, total_ref[NQ + 1], unroll=4))
+    count = jnp.sum(counts_ref[...].astype(jnp.float32))
 
     for q in range(NQ):
         g, i = divmod(q, 4)
@@ -301,7 +342,7 @@
     return jax.ShapeDtypeStruct(shape, jnp.float32)
 
 
-def call(kernel, outs, n_in, scratch=(), flops=1000, smem_last=False):
+def call(kernel, outs, n_in, scratch=(), flops=1000, smem_last=False, mib=2):
     specs = [VM] * len(outs)
     if smem_last:
         specs[-1] = SM
@@ -312,29 +353,36 @@
         out_specs=tuple(specs),
         scratch_shapes=list(scratch),
         cost_estimate=pl.CostEstimate(flops=flops, bytes_accessed=100000, transcendentals=0),
+        compiler_params=pltpu.CompilerParams(vmem_limit_bytes=mib << 20),
     )
+
+
+def scratch(*shape):
+    return pltpu.VMEM(shape + BLOCK, jnp.float32)
 
 
 def per_device(design, observed, weight, params, offsets, counts):
     design, observed, weight, params, offsets, counts = (
         blocked(x) for x in (design, observed, weight, params, offsets, counts)
     )
-    (edge,) = call(edge_kernel, [f32(*BLOCK)], 1)(params)
+    (edge,) = call(edge_kernel, [f32(*BLOCK)], 1, (), EDGE_FLOPS)(params)
     dec_b = exchange(edge, DEC, [(i, i + 1) for i in range(1, 15, 2)])
     dec_a = exchange(edge, DEC, [(i, i + 1) for i in range(0, 16, 2)])
-    total, edges = call(
-        sums_kernel, [f32(NQ + 1, *BLOCK), f32(11, *BLOCK)], 5,
-        [pltpu.VMEM((9, NQ) + BLOCK, jnp.float32)], 30_000_000,
-    )(design, observed, weight, offsets, counts)
-    to_a, to_b, halo = call(message_kernel, [f32(9, *BLOCK), f32(9, *BLOCK), f32(*BLOCK)], 4)(
-        params, edges, dec_a, dec_b
-    )
+    message = f32(9, *BLOCK)
+    to_a, to_b, code = call(
+        leave_kernel, [message, message, jax.ShapeDtypeStruct((80,) + BLOCK, jnp.int32)], 6,
+        [scratch(3, NQ)], 10_000_000, mib=6,
+    )(design, observed, weight, offsets, counts, params)
+    slots = (design, observed, weight, code)
+    to_a, to_b, halo = call(halo_kernel, [message, message, f32(*BLOCK)], 4)(dec_a, dec_b, to_a, to_b)
     from_b = exchange(to_b, RA, [(i, (i + 1) % 16) for i in range(1, 16, 2)])
     from_a = exchange(to_a, RA, [(i, i + 1) for i in range(0, 16, 2)])
+    (total,) = call(
+        stay_kernel, [f32(NQ + 2, *BLOCK)], 6, [scratch(9, NQ), scratch(9, 5)], 30_000_000, mib=6
+    )(*slots, params, halo)
     total, send = call(
-        chi_kernel, [f32(NQ, *BLOCK), f32(256, 128)], 10,
-        [pltpu.VMEM((9, 5) + BLOCK, jnp.float32)], 5_000_000,
-    )(design, observed, weight, offsets, counts, params, total, from_a, from_b, halo)
+        chi_kernel, [f32(NQ, *BLOCK), f32(256, 128)], 8, [scratch(3, 5)], 5_000_000, mib=6
+    )(*slots, counts, total, from_a, from_b)
     got = lax.all_to_all(send.reshape(256, 1, 128), ALL, 0, 0, tiled=True).reshape(256, 128)
     new, chi = call(solve_kernel, [f32(5, *BLOCK), f32(1, 1)], 3, (), 100000, True)(params, total, got)
     return unblocked(new), chi.reshape(())

time: 59.3 us -> 47.5 us (0.80)
  Pallas kernels: 16.7 us -> 10.7 us
  blocking collectives: 29.9 us -> 26.7 us
  waiting for transfers between devices: 2.41 us -> 0.01 us
    pallas_call x4 -> x5, Pallas kernels: 14.8 us -> 9.8 us  [the longest x1 6.84 us: per_device(): call(stay_kernel, [f32(NQ + 2, *BLOCK)], 6, [scratch(9, NQ), scratch(9, 5...]
    all_to_all x1, blocking collectives: 29.9 us -> 26.7 us  [per_device(): lax.all_to_all(send.reshape(256, 1, 128), ALL, 0, 0, tiled=True)]
    ppermute x4, waiting for transfers between devices: 2.41 us -> 0.01 us  [exchange(): return lax.ppermute(value, axes, both)]
    pallas_call x1, Pallas kernels: 1.86 us -> 0.9 us  [per_device(): call(solve_kernel, [f32(5, *BLOCK), f32(1, 1)], 3, (), 100000, True)]
    unnamed x8 -> x14, local copies, waits for them, and re-layouts: 1.19 us -> 0.74 us
  transfers between devices with their start and end apart: 4 -> 4, of which waited for: 1 -> 0; matrix products, arithmetic and copies ran while one was open for 0% -> 0% of each run, Pallas kernels for 14% -> 19%
where the time goes in v2:
time: 47.5 us; the launch traced here: 47.3 us
  blocking collectives  26.7 us (56%)
  Pallas kernels  10.7 us (23%)
  starting transfers between devices  8.36 us (18%)
  between operations  0.75 us (2%)
  local copies, waits for them, and re-layouts  0.74 us (2%)
    all_to_all x1, blocking collectives, per_device(): lax.all_to_all(send.reshape(256, 1, 128), ALL, 0, 0, tiled=True)  26.7 us
    ppermute x4, starting transfers between devices, exchange(): return lax.ppermute(value, axes, both)  8.36 us
    pallas_call x1, Pallas kernels, per_device(): call(stay_kernel, [f32(NQ + 2, *BLOCK)], 6, [scratch(9, NQ), scratch(9, 5...  6.84 us
    pallas_call x1, Pallas kernels, per_device(): call(leave_kernel, [message, message, jax.ShapeDtypeStruct((80,) + BLOCK,...  2.18 us
  transfers between devices with their start and end apart: 4, of which 0 were waited for; matrix products, arithmetic and copies ran while one was open for 0% of the time, Pallas kernels for 19%

profile of v2, /device:TPU:1, one launch (start us, length us, event | category | flops | bytes accessed | tf_op | source)
XLA Modules:
  0.0 47.3 jit_solution(6748139959409548764)
XLA Ops:
  0.6 0.0 copy-start.4
  0.6 0.7 %copy-done.4 = f32[5,4,256]{2,1,0:T(4,128)S(1)} copy-done((f32[5,4,256]{2,1,0:T(4,128)S(1)}, f32[5,4,256]{2,1,0:T(4,128)}, u32[]{:S(2)}) %copy-start.4) | copy-done | bytes 20504
  1.4 0.0 copy-start
  1.4 0.0 copy-start.1
  1.4 0.0 copy-start.2
  1.4 0.0 copy-start.3
  1.4 0.0 copy-start.5
  1.4 0.0 copy-start.6
  1.4 0.1 shard_map.78
  1.5 0.8 %collective-permute-start.1 = (f32[8,128]{1,0:T(8,128)S(1)}, f32[8,128]{1,0:T(8,128)S(1)}, u32[]{:S(2)}, u32[]{:S(2)}) collective-permute-start(f32[8,128]{1,0:T(8,128)S(1)} %shard_map.78), channel_id=1, source_target_pairs={{1,2},{3,4},{5,6},{7,8},{9,10},{11,12},{13,14},{2,1},{4,3},{6,5},{... | collective-permute-start | bytes 12296 | tf_op jit(solution)/shard_map/ppermute | solution.py:338
  2.3 5.0 %collective-permute-start = (f32[8,128]{1,0:T(8,128)S(1)}, f32[8,128]{1,0:T(8,128)S(1)}, u32[]{:S(2)}, u32[]{:S(2)}) collective-permute-start(f32[8,128]{1,0:T(8,128)S(1)} %shard_map.78), channel_id=1, source_target_pairs={{0,1},{2,3},{4,5},{6,7},{8,9},{10,11},{12,13},{14,15},{1,0},{3,2},... | collective-permute-start | bytes 12296 | tf_op jit(solution)/shard_map/ppermute | solution.py:338
  7.2 0.0 copy-done
  7.2 0.0 copy-done.1
  7.2 0.0 copy-done.2
  7.2 0.0 copy-done.3
  7.2 0.0 copy-done.5
  7.3 0.0 copy-done.6
  7.3 2.2 %shard_map.77 = (f32[9,8,128]{2,1,0:T(8,128)S(1)}, f32[9,8,128]{2,1,0:T(8,128)S(1)}, s32[80,8,128]{2,1,0:T(8,128)S(1)}) custom-call(f32[5,80,8,128]{3,2,1,0:T(8,128)S(1)} %bitcast.40, f32[80,8,128]{2,1,0:T(8,128)S(1)} %bitcast.43, f32[80,8,128]{2,1,0:T(8,128)S(1)} %bitcast.46, s32[80,8,128]{2,1,0:T(8,128)S(1)} %bitcast.50, s32[8,128]{1,0:T(8,128)S(1)} %bitcast.56, ...), custom_call_target="tpu_custom_call" | custom-call | flops 10000000 | bytes 100000 | tf_op jit(solution)/shard_map/pallas_call | solution.py:372
  9.5 0.0 collective-permute-done.1.dec_b_ref
  9.5 0.0 collective-permute-done.dec_a_ref
  9.5 1.3 %collective-permute-start.2 = (f32[9,8,128]{2,1,0:T(8,128)S(1)}, f32[9,8,128]{2,1,0:T(8,128)S(1)}, u32[]{:S(2)}, u32[]{:S(2)}) collective-permute-start(f32[9,8,128]{2,1,0:T(8,128)S(1)} %get-tuple-element.16), channel_id=1, source_target_pairs={{0,16},{32,48},{64,80},{96,112},{128,144},{160,176},{192,208},{224... | collective-permute-start | bytes 110600 | tf_op jit(solution)/shard_map/ppermute | solution.py:338
  10.8 1.3 %collective-permute-start.3 = (f32[9,8,128]{2,1,0:T(8,128)S(1)}, f32[9,8,128]{2,1,0:T(8,128)S(1)}, u32[]{:S(2)}, u32[]{:S(2)}) collective-permute-start(f32[9,8,128]{2,1,0:T(8,128)S(1)} %get-tuple-element.17), channel_id=1, source_target_pairs={{16,32},{48,64},{80,96},{112,128},{144,160},{176,192},{208,224},{2... | collective-permute-start | bytes 110600 | tf_op jit(solution)/shard_map/ppermute | solution.py:338
  12.1 6.8 %shard_map.80.total_ref = f32[22,8,128]{2,1,0:T(8,128)S(1)} custom-call(f32[5,80,8,128]{3,2,1,0:T(8,128)S(1)} %bitcast.41, f32[80,8,128]{2,1,0:T(8,128)S(1)} %bitcast.44, f32[80,8,128]{2,1,0:T(8,128)S(1)} %bitcast.47, s32[80,8,128]{2,1,0:T(8,128)S(1)} %get-tuple-element.12.code_ref, f32[5,8,128]{2,1,0:T(8,128)S(1)} %bitcast.53, ...), custom_call_target="tpu_custom_call" | custom-call | flops 30000000 | bytes 100000 | tf_op jit(solution)/shard_map/pallas_call | solution.py:380
  18.9 0.0 collective-permute-done.2.from_a_ref
  19.0 0.0 collective-permute-done.3.from_b_ref
  19.0 0.7 %shard_map.81 = (f32[20,8,128]{2,1,0:T(8,128)S(1)}, f32[256,128]{1,0:T(8,128)S(1)}) custom-call(f32[5,80,8,128]{3,2,1,0:T(8,128)S(1)} %bitcast.42, f32[80,8,128]{2,1,0:T(8,128)S(1)} %bitcast.45, f32[80,8,128]{2,1,0:T(8,128)S(1)} %bitcast.48, s32[80,8,128]{2,1,0:T(8,128)S(1)} %get-tuple-element.12.code_ref, s32[8,128]{1,0:T(8,128)S(1)} %bitcast.57, ...), custom_call_target="tpu_custom_call" | custom-call | flops 5000000 | bytes 100000 | tf_op jit(solution)/shard_map/pallas_call | solution.py:383
  19.7 26.7 %all_to_all.5 = f32[256,1,128]{2,1,0:T(1,128)S(1)} all-to-all(f32[256,1,128]{2,1,0:T(1,128)S(1)} %bitcast.55), channel_id=1, replica_groups=mesh['ra_0'=2,'ra_1'=4,'ra_2'=2,'dec_0'=8,'dec_1'=2] {'ra_0','ra_1','ra_..., dimensions={0} | all-to-all | bytes 262144 | tf_op jit(solution)/shard_map/all_to_all | solution.py:386
  46.4 0.9 %shard_map.82 = (f32[5,8,128]{2,1,0:T(8,128)}, f32[1,1]{1,0:T(1,128)}) custom-call(f32[5,8,128]{2,1,0:T(8,128)S(1)} %bitcast.54, f32[20,8,128]{2,1,0:T(8,128)S(1)} %get-tuple-element.18.total_ref, f32[256,128]{1,0:T(8,128)S(1)} %bitcast.49), custom_call_target="tpu_custom_call" | custom-call | flops 100000 | bytes 100000 | tf_op jit(solution)/shard_map/pallas_call | solution.py:387
  (1 shorter events, 0.0 us)
Async XLA Ops:
  0.6 0.7 %copy-start.4 = (f32[5,4,256]{2,1,0:T(4,128)S(1)}, f32[5,4,256]{2,1,0:T(4,128)}, u32[]{:S(2)}) copy-start(f32[5,4,256]{2,1,0:T(4,128)} %param.9) | copy-start | bytes 61444
  1.4 5.9 %copy-start = (f32[5,80,4,256]{3,2,1,0:T(4,128)S(1)}, f32[5,80,4,256]{3,2,1,0:T(4,128)}, u32[]{:S(2)}) copy-start(f32[5,80,4,256]{3,2,1,0:T(4,128)} %param.6) | copy-start | bytes 4915204
  1.4 5.9 %copy-start.1 = (f32[80,4,256]{2,1,0:T(4,128)S(1)}, f32[80,4,256]{2,1,0:T(4,128)}, u32[]{:S(2)}) copy-start(f32[80,4,256]{2,1,0:T(4,128)} %param.7) | copy-start | bytes 983044
  1.4 5.9 %copy-start.2 = (f32[80,4,256]{2,1,0:T(4,128)S(1)}, f32[80,4,256]{2,1,0:T(4,128)}, u32[]{:S(2)}) copy-start(f32[80,4,256]{2,1,0:T(4,128)} %param.8) | copy-start | bytes 983044
  1.4 5.9 %copy-start.3 = (s32[80,4,256]{2,1,0:T(4,128)S(1)}, s32[80,4,256]{2,1,0:T(4,128)}, u32[]{:S(2)}) copy-start(s32[80,4,256]{2,1,0:T(4,128)} %param.10) | copy-start | bytes 983044
  1.4 5.9 %copy-start.5 = (f32[5,4,256]{2,1,0:T(4,128)S(1)}, f32[5,4,256]{2,1,0:T(4,128)}, u32[]{:S(2)}) copy-start(f32[5,4,256]{2,1,0:T(4,128)} %param.9) | copy-start | bytes 61444
  1.4 5.9 %copy-start.6 = (s32[4,256]{1,0:T(4,128)S(1)}, s32[4,256]{1,0:T(4,128)}, u32[]{:S(2)}) copy-start(s32[4,256]{1,0:T(4,128)} %param.11) | copy-start | bytes 12292
  1.5 8.0 %collective-permute-start.1 = (f32[8,128]{1,0:T(8,128)S(1)}, f32[8,128]{1,0:T(8,128)S(1)}, u32[]{:S(2)}, u32[]{:S(2)}) collective-permute-start(f32[8,128]{1,0:T(8,128)S(1)} %shard_map.78), channel_id=1, source_target_pairs={{1,2},{3,4},{5,6},{7,8},{9,10},{11,12},{13,14},{2,1},{4,3},{6,5},{... | collective-permute-start | bytes 12296 | tf_op jit(solution)/shard_map/ppermute | solution.py:338
  2.3 7.2 %collective-permute-start = (f32[8,128]{1,0:T(8,128)S(1)}, f32[8,128]{1,0:T(8,128)S(1)}, u32[]{:S(2)}, u32[]{:S(2)}) collective-permute-start(f32[8,128]{1,0:T(8,128)S(1)} %shard_map.78), channel_id=1, source_target_pairs={{0,1},{2,3},{4,5},{6,7},{8,9},{10,11},{12,13},{14,15},{1,0},{3,2},... | collective-permute-start | bytes 12296 | tf_op jit(solution)/shard_map/ppermute | solution.py:338
  9.5 9.4 %collective-permute-start.2 = (f32[9,8,128]{2,1,0:T(8,128)S(1)}, f32[9,8,128]{2,1,0:T(8,128)S(1)}, u32[]{:S(2)}, u32[]{:S(2)}) collective-permute-start(f32[9,8,128]{2,1,0:T(8,128)S(1)} %get-tuple-element.16), channel_id=1, source_target_pairs={{0,16},{32,48},{64,80},{96,112},{128,144},{160,176},{192,208},{224... | collective-permute-start | bytes 110600 | tf_op jit(solution)/shard_map/ppermute | solution.py:338
  10.8 8.1 %collective-permute-start.3 = (f32[9,8,128]{2,1,0:T(8,128)S(1)}, f32[9,8,128]{2,1,0:T(8,128)S(1)}, u32[]{:S(2)}, u32[]{:S(2)}) collective-permute-start(f32[9,8,128]{2,1,0:T(8,128)S(1)} %get-tuple-element.17), channel_id=1, source_target_pairs={{16,32},{48,64},{80,96},{112,128},{144,160},{176,192},{208,224},{2... | collective-permute-start | bytes 110600 | tf_op jit(solution)/shard_map/ppermute | solution.py:338

commit v3 on v2

v3 whole, which is shorter than its diff:
```python
import jax
import jax.numpy as jnp
from jax import lax
from jax.experimental import pallas as pl
from jax.experimental.pallas import tpu as pltpu
from jax.sharding import Mesh
from jax.sharding import PartitionSpec as P

RA = ("ra_0", "ra_1", "ra_2")
DEC = ("dec_0", "dec_1")
ALL = RA + DEC

PAIRS = [(p, q) for p in range(5) for q in range(p, 5)]
NQ = 20
EDGE_FLOPS = 20_000_000_000
VM = pl.BlockSpec(memory_space=pltpu.VMEM)
SM = pl.BlockSpec(memory_space=pltpu.SMEM)
BLOCK = (8, 128)


def blocked(x):
    lead = x.shape[:-2]
    x = x.reshape(lead + (4, 2, 128))
    x = jnp.swapaxes(x, -3, -2)
    return x.reshape(lead + BLOCK)


def unblocked(x):
    lead = x.shape[:-2]
    x = x.reshape(lead + (2, 4, 128))
    x = jnp.swapaxes(x, -3, -2)
    return x.reshape(lead + (4, 256))


def grids():
    lane = lax.broadcasted_iota(jnp.int32, BLOCK, 1)
    sub = lax.broadcasted_iota(jnp.int32, BLOCK, 0)
    return lane, sub & 3, sub >> 2


def lanes(x, by):
    by = by % 128
    return x if by == 0 else pltpu.roll(x, by, 1)


def subs(x, by):
    by = by % 8
    return x if by == 0 else pltpu.roll(x, by, 0)


def edge_kernel(params_ref, out_ref):
    lane, _, half = grids()
    out = jnp.zeros(BLOCK, jnp.float32)
    for p in range(5):
        value = params_ref[p]
        out = jnp.where(lane == p, jnp.where(half == 0, lanes(value, p), lanes(value, p + 1)), out)
    out_ref[...] = out


def shift_sum(minus, mid, plus, lane, half):
    down = lanes(minus, 127)
    down = jnp.where(lane == 127, jnp.where(half == 0, subs(down, 4), 0.0), down)
    up = lanes(plus, 1)
    up = jnp.where(lane == 0, jnp.where(half == 1, subs(up, 4), 0.0), up)
    return mid + down + up


def accumulate(design_ref, observed_ref, weight_ref, code_ref, wanted):
    def body(k, acc):
        w = jnp.where(code_ref[k] == wanted, weight_ref[k], 0.0)
        d = [design_ref[p, k] for p in range(5)]
        o = observed_ref[k]
        wd = [w * x for x in d]
        new = [wd[p] * o for p in range(5)] + [wd[p] * d[q] for p, q in PAIRS]
        return tuple(x + y for x, y in zip(acc, new))

    return lax.fori_loop(0, 80, body, (jnp.zeros(BLOCK, jnp.float32),) * NQ, unroll=4)


def edge_code(b, row):
    return jnp.where(row == 0, b, jnp.where(row == 3, 6 + b, -1))


def by_neighbour(to_a_ref, to_b_ref, low, high, start=0):
    ra_odd = lax.axis_index("ra_2")
    for g in range(len(low)):
        to_a_ref[start + g] = jnp.where(ra_odd == 0, high[g], low[g])
        to_b_ref[start + g] = jnp.where(ra_odd == 0, low[g], high[g])


def pack_rows(values, row):
    count = (len(values) + 3) // 4
    low = [jnp.zeros(BLOCK, jnp.float32) for _ in range(count)]
    high = [jnp.zeros(BLOCK, jnp.float32) for _ in range(count)]
    for q, value in enumerate(values):
        g, i = divmod(q, 4)
        low[g] = jnp.where(row == i, subs(value, i), low[g])
        high[g] = jnp.where(row == i, subs(value, i - 3), high[g])
    return low, high


def column_kernel(
    design_ref, observed_ref, weight_ref, offsets_ref, counts_ref, params_ref, edge_ref,
    to_a_ref, to_b_ref, packed_ref, codes_ref, again_ref,
):
    lane, row, half = grids()
    again_ref[...] = edge_ref[...]
    packed = [jnp.zeros(BLOCK, jnp.float32) for _ in range(7)]
    codes = jnp.full(BLOCK, 9, jnp.int32)
    counts = jnp.zeros(BLOCK, jnp.int32)
    for k in range(80):
        here = lane == jnp.where(half == 0, k, (k + 127) % 128)
        values = [design_ref[p, k] for p in range(5)] + [observed_ref[k], weight_ref[k]]
        packed = [jnp.where(here, lanes(x, k), y) for x, y in zip(values, packed)]
        codes = jnp.where(here, lanes(offsets_ref[k], k), codes)
    counts = counts_ref[...]
    counts = jnp.where(half == 0, counts[:, :1], counts[:, 127:])
    slot = jnp.where(half == 0, lane, (lane + 1) & 127)
    codes = jnp.where(counts > slot, codes, 9)
    for i in range(7):
        packed_ref[i] = packed[i]
    codes_ref[...] = codes
    corner = edge_code(2 * half, row)
    outside = packed[:6] + [jnp.where(codes == corner, packed[6], 0.0)]
    low, high = pack_rows([params_ref[p] for p in range(5)], row)
    by_neighbour(to_a_ref, to_b_ref, low + outside, high + outside)


def flatten(x, row, half):
    flat = x
    for r in range(1, 4):
        flat = jnp.where(row == r, lanes(x, 32 * r), flat)
    return [jnp.sum(jnp.where(half == j, flat, 0.0), axis=0, keepdims=True) for j in range(2)]


def columns_around(x, beyond, p, lane, half):
    below = lanes(x, 1)
    below = jnp.where(lane == 0, jnp.where(half == 1, subs(below, 4), lanes(beyond, -p)), below)
    above = lanes(x, 127)
    above = jnp.where(lane == 127, jnp.where(half == 0, subs(above, 4), lanes(beyond, 127 - p)), above)
    return below, x, above


def inside_kernel(
    design_ref, observed_ref, weight_ref, offsets_ref, counts_ref, params_ref,
    packed_ref, codes_ref, dec_a_ref, dec_b_ref,
    lines_ref, chi_ref, halo_ref, code_ref, win_ref,
):
    lane, row, half = grids()
    zero = jnp.zeros(BLOCK, jnp.float32)
    d, o, weight, codes = [packed_ref[p] for p in range(5)], packed_ref[5], packed_ref[6], codes_ref[...]
    found = []
    for a in range(3):
        w = jnp.where(codes == 3 * a + 2 * half, weight, 0.0)
        wd = [w * x for x in d]
        terms = [wd[p] * o for p in range(5)] + [wd[p] * d[q] for p, q in PAIRS]
        out = zero
        for q in range(NQ):
            out = jnp.where(lane == q, jnp.sum(terms[q], axis=1, keepdims=True), out)
        found.append(out)
    back, same, ahead = found
    mid = same + jnp.where(row < 3, subs(back, 7), 0.0) + jnp.where(row > 0, subs(ahead, 1), 0.0)
    low = jnp.where(row == 3, subs(back, 3), 0.0)
    high = jnp.where(row == 0, subs(ahead, 5), 0.0)
    lines_ref[...] = jnp.zeros(BLOCK, jnp.float32)
    for i, x in enumerate((low, mid, high)):
        for j, line in enumerate(flatten(x, row, half)):
            lines_ref[2 * i + j : 2 * i + j + 1, :] = line
    counts = counts_ref[...]
    lines_ref[6:7, :] = jnp.where(lane[:1] == NQ + 1, jnp.sum(counts.astype(jnp.float32)), 0.0)

    dec_odd = lax.axis_index("dec_1")
    halo = jnp.where((half == 0) == (dec_odd == 0), dec_a_ref[...], dec_b_ref[...])
    halo = subs(halo, 4)
    halo_ref[...] = halo
    for p in range(5):
        value = params_ref[p]
        for a in range(3):
            shift = (1, 0, 7)[a]
            found = columns_around(subs(value, shift), subs(halo, shift), p, lane, half)
            for b in range(3):
                win_ref[3 * a + b, p] = found[b]

    least = jnp.where(row == 0, 3, 0)
    most = jnp.where(row == 3, 5, 8)

    def body(k, acc):
        code = jnp.where(counts > k, offsets_ref[k], 9)
        code_ref[k] = code
        hits = [code == c for c in range(1, 9)]
        resid = observed_ref[k]
        for p in range(5):
            source = win_ref[0, p]
            for c in range(1, 9):
                source = jnp.where(hits[c - 1], win_ref[c, p], source)
            resid = resid - design_ref[p, k] * source
        inside = (code >= least) & (code <= most)
        w = jnp.where(inside, weight_ref[k], 0.0)
        return acc + w * resid * resid

    chi_ref[...] = lax.fori_loop(0, 80, body, zero, unroll=4)


def ra_sides(from_a_ref, from_b_ref):
    ra_odd = lax.axis_index("ra_2")

    def from_low(g):
        return jnp.where(ra_odd == 0, from_b_ref[g], from_a_ref[g])

    def from_high(g):
        return jnp.where(ra_odd == 0, from_a_ref[g], from_b_ref[g])

    return from_low, from_high


def chi_kernel(
    design_ref, observed_ref, weight_ref, code_ref,
    chi_ref, halo_ref, lines_ref, from_a_ref, from_b_ref, send_ref, win_ref,
):
    lane, row, half = grids()
    ra = lax.axis_index(RA)
    dec = lax.axis_index(DEC)
    from_low, from_high = ra_sides(from_a_ref, from_b_ref)
    for p in range(5):
        g, i = divmod(p, 4)
        value = jnp.where(row == 0, subs(from_low(g), -i), subs(from_high(g), 3 - i))
        found = columns_around(value, jnp.zeros(BLOCK, jnp.float32), p, lane, half)
        for b in range(3):
            win_ref[b, p] = found[b]

    halo = halo_ref[...]
    halo = jnp.where(row == 3, subs(halo, 3), subs(halo, 5))
    corner = [jnp.where(row == 3, from_low(2 + i), from_high(2 + i)) for i in range(7)]
    resid = corner[5]
    for p in range(5):
        resid = resid - corner[p] * halo[:, p : p + 1]
    acc = chi_ref[...] + jnp.where((row == 0) | (row == 3), corner[6] * resid * resid, 0.0)

    wanted = [edge_code(b, row) for b in range(3)]
    wanted[0] = jnp.where((lane == 0) & (half == 0), -1, wanted[0])
    wanted[2] = jnp.where((lane == 127) & (half == 1), -1, wanted[2])

    def body(k, acc):
        code = code_ref[k]
        hits = [code == x for x in wanted]
        resid = observed_ref[k]
        for p in range(5):
            source = jnp.where(hits[1], win_ref[1, p], win_ref[0, p])
            source = jnp.where(hits[2], win_ref[2, p], source)
            resid = resid - design_ref[p, k] * source
        w = jnp.where(hits[0] | hits[1] | hits[2], weight_ref[k], 0.0)
        return acc + w * resid * resid

    chi = jnp.sum(lax.fori_loop(0, 80, body, acc, unroll=4))
    base = jnp.where(lane == NQ, chi, jnp.broadcast_to(lines_ref[6:7, :], BLOCK))
    for g in range(32):
        send_ref[pl.ds(8 * g, 8), :] = base

    for i in range(3):
        place = ((ra + (15 + i)) & 15) * 16 + dec

        @pl.when(dec > 0)
        def _(i=i, place=place):
            send_ref[pl.ds(place - 1, 1), :] = base[:1] + lines_ref[2 * i : 2 * i + 1, :]

        @pl.when(dec < 15)
        def _(i=i, place=place):
            send_ref[pl.ds(place + 1, 1), :] = base[:1] + lines_ref[2 * i + 1 : 2 * i + 2, :]


def cross_kernel(
    design_ref, observed_ref, weight_ref, code_ref, send_ref, to_a_ref, to_b_ref, acc_ref
):
    lane, row, half = grids()
    for i, code in enumerate((0, 1, 2, 6, 7, 8)):
        acc = accumulate(design_ref, observed_ref, weight_ref, code_ref, code)
        for q in range(NQ):
            acc_ref[i, q] = acc[q]
    values = []
    for q in range(NQ):
        leave = [
            jnp.where(row == 0, acc_ref[b, q], jnp.where(row == 3, acc_ref[3 + b, q], 0.0)) for b in range(3)
        ]
        values.append(shift_sum(*leave, lane, half))
    by_neighbour(to_a_ref, to_b_ref, *pack_rows(values, row))


def stay_kernel(
    design_ref, observed_ref, weight_ref, code_ref, cross_ref, total_ref, acc_ref
):
    lane, row, half = grids()
    for b in range(3):
        acc = accumulate(design_ref, observed_ref, weight_ref, code_ref, 3 + b)
        for q in range(NQ):
            acc_ref[b, q] = acc[q]
    for q in range(NQ):
        stay = []
        for b in range(3):
            back, same, ahead = cross_ref[b, q], acc_ref[b, q], cross_ref[3 + b, q]
            stay.append(
                same + jnp.where(row < 3, subs(back, 7), 0.0) + jnp.where(row > 0, subs(ahead, 1), 0.0)
            )
        total_ref[q] = shift_sum(*stay, lane, half)


def solve(rhs, normal):
    lower = [[None] * 5 for _ in range(5)]
    inverse = [None] * 5
    for first in range(5):
        for second in range(first + 1):
            running = normal[second][first]
            for inner in range(second):
                running = running - lower[first][inner] * lower[second][inner]
            if first == second:
                inverse[first] = 1.0 / jnp.sqrt(running)
            else:
                lower[first][second] = running * inverse[second]
    forward = []
    for first in range(5):
        running = rhs[first]
        for inner in range(first):
            running = running - lower[first][inner] * forward[inner]
        forward.append(running * inverse[first])
    answer = [None] * 5
    for first in range(4, -1, -1):
        running = forward[first]
        for inner in range(first + 1, 5):
            running = running - lower[inner][first] * answer[inner]
        answer[first] = running * inverse[first]
    return answer


def solve_kernel(params_ref, total_ref, from_a_ref, from_b_ref, got_ref, new_ref, chi_ref):
    lane, row, half = grids()
    ra = lax.axis_index(RA)
    dec = lax.axis_index(DEC)

    def column(step):
        line = jnp.zeros((1, 128), jnp.float32)
        for i in range(3):
            place = ((ra + (15 + i)) & 15) * 16 + dec + step
            place = jnp.minimum(jnp.maximum(place, 0), 255)
            line = line + got_ref[pl.ds(place, 1), :]
        line = jnp.broadcast_to(line, BLOCK)
        out = line
        for r in range(1, 4):
            out = jnp.where(row == r, lanes(line, -32 * r), out)
        return out

    from_low = column(-1)
    from_high = column(1)
    ra_low, ra_high = ra_sides(from_a_ref, from_b_ref)
    sums = []
    for q in range(NQ):
        g, i = divmod(q, 4)
        sums.append(
            total_ref[q]
            + jnp.where(row == 0, subs(ra_low(g), -i), 0.0)
            + jnp.where(row == 3, subs(ra_high(g), 3 - i), 0.0)
            + jnp.where((lane == 0) & (half == 0), lanes(from_low, -q), 0.0)
            + jnp.where((lane == 127) & (half == 1), lanes(from_high, 127 - q), 0.0)
        )
    normal = [[None] * 5 for _ in range(5)]
    for place, (p, q) in enumerate(PAIRS):
        normal[p][q] = sums[5 + place]
        normal[q][p] = sums[5 + place]
    params = [params_ref[p] for p in range(5)]
    rhs = []
    for p in range(5):
        running = sums[p]
        for q in range(5):
            running = running - normal[p][q] * params[q]
        rhs.append(running)
    for p in range(5):
        normal[p][p] = normal[p][p] + 1.0
    delta = solve(rhs, normal)
    for p in range(5):
        new_ref[p] = params[p] + delta[p]
    all_sums = got_ref[pl.ds(0, 8), :]
    for g in range(1, 32):
        all_sums = all_sums + got_ref[pl.ds(8 * g, 8), :]
    chi = jnp.sum(jnp.where(lane == NQ, all_sums, 0.0))
    count = jnp.sum(jnp.where(lane == NQ + 1, all_sums, 0.0))
    chi_ref[0, 0] = chi / count


def exchange(value, axes, pairs):
    both = [(i, j) for i, j in pairs] + [(j, i) for i, j in pairs]
    return lax.ppermute(value, axes, both)


def f32(*shape):
    return jax.ShapeDtypeStruct(shape, jnp.float32)


def call(kernel, outs, n_in, scratch=(), flops=1000, smem_last=False, mib=2):
    specs = [VM] * len(outs)
    if smem_last:
        specs[-1] = SM
    return pl.pallas_call(
        kernel,
        out_shape=tuple(outs),
        in_specs=[VM] * n_in,
        out_specs=tuple(specs),
        scratch_shapes=list(scratch),
        cost_estimate=pl.CostEstimate(flops=flops, bytes_accessed=100000, transcendentals=0),
        compiler_params=pltpu.CompilerParams(vmem_limit_bytes=mib << 20),
    )


def scratch(*shape):
    return pltpu.VMEM(shape + BLOCK, jnp.float32)


def device_step(design, observed, weight, params, offsets, counts):
    design, observed, weight, params, offsets, counts = (
        blocked(x) for x in (design, observed, weight, params, offsets, counts)
    )
    (edge,) = call(edge_kernel, [f32(*BLOCK)], 1, (), EDGE_FLOPS)(params)
    dec_b = exchange(edge, DEC, [(i, i + 1) for i in range(1, 15, 2)])
    ra_b_pairs = [(i, (i + 1) % 16) for i in range(1, 16, 2)]
    ra_a_pairs = [(i, i + 1) for i in range(0, 16, 2)]
    message = f32(9, *BLOCK)
    to_a, to_b, packed, codes, again = call(
        column_kernel,
        [message, message, f32(7, *BLOCK), jax.ShapeDtypeStruct(BLOCK, jnp.int32), f32(*BLOCK)],
        7, (), 10_000_000, mib=6,
    )(design, observed, weight, offsets, counts, params, edge)
    from_b = exchange(to_b, RA, ra_b_pairs)
    dec_a = exchange(again, DEC, [(i, i + 1) for i in range(0, 16, 2)])
    from_a = exchange(to_a, RA, ra_a_pairs)
    lines, chi, halo, code = call(
        inside_kernel,
        [f32(*BLOCK), f32(*BLOCK), f32(*BLOCK), jax.ShapeDtypeStruct((80,) + BLOCK, jnp.int32)],
        10, [scratch(9, 5)], 300_000_000, mib=6,
    )(design, observed, weight, offsets, counts, params, packed, codes, dec_a, dec_b)
    slots = (design, observed, weight, code)
    (send,) = call(chi_kernel, [f32(256, 128)], 9, [scratch(3, 5)], 5_000_000, mib=6)(
        *slots, chi, halo, lines, from_a, from_b
    )
    got = lax.all_to_all(send.reshape(256, 1, 128), ALL, 0, 0, tiled=True).reshape(256, 128)
    sums = f32(5, *BLOCK)
    sums_a, sums_b, cross = call(
        cross_kernel, [sums, sums, f32(6, NQ, *BLOCK)], 5, (), 1_000_000_000, mib=6
    )(*slots, send)
    sums_b = exchange(sums_b, RA, ra_b_pairs)
    sums_a = exchange(sums_a, RA, ra_a_pairs)
    (total,) = call(
        stay_kernel, [f32(NQ, *BLOCK)], 5, [scratch(3, NQ)], 1_000_000_000, mib=6
    )(*slots, cross)
    new, chi = call(solve_kernel, [f32(5, *BLOCK), f32(1, 1)], 5, (), 100000, True)(
        params, total, sums_a, sums_b, got
    )
    return unblocked(new), chi.reshape(())


def solution(mesh):
    finer = Mesh(mesh.devices.reshape(2, 4, 2, 8, 2), ALL)
    return jax.shard_map(
        device_step,
        mesh=finer,
        in_specs=(
            P(None, None, RA, DEC),
            P(None, RA, DEC),
            P(None, RA, DEC),
            P(None, RA, DEC),
            P(None, RA, DEC),
            P(RA, DEC),
        ),
        out_specs=(P(None, RA, DEC), P()),
        check_vma=False,
    )
```

time: 47.5 us -> 46.3 us (0.975)
  blocking collectives: 26.7 us -> 0 us
  starting transfers between devices: 8.36 us -> 27.1 us
  waiting for transfers between devices: 0.01 us -> 4.79 us
  local copies, waits for them, and re-layouts: 0.74 us -> 2.29 us
  Pallas kernels: 10.7 us -> 11.2 us
    all_to_all x1 -> x0, blocking collectives: 26.7 us -> none  [per_device(): lax.all_to_all(send.reshape(256, 1, 128), ALL, 0, 0, tiled=True)]
    all_to_all x0 -> x1, starting transfers between devices: none -> 20.1 us  [device_step(): lax.all_to_all(send.reshape(256, 1, 128), ALL, 0, 0, tiled=True)]
    ppermute x4 -> x6, waiting for transfers between devices: 0.01 us -> 2.47 us  [exchange(): return lax.ppermute(value, axes, both)]
    all_to_all x0 -> x1, waiting for transfers between devices: none -> 2.32 us  [device_step(): lax.all_to_all(send.reshape(256, 1, 128), ALL, 0, 0, tiled=True)]
    unnamed x14, local copies, waits for them, and re-layouts: 0.74 us -> 2.29 us
    ppermute x4 -> x6, starting transfers between devices: 8.36 us -> 6.96 us  [exchange(): return lax.ppermute(value, axes, both)]
    pallas_call x6 -> x7, Pallas kernels: 10.7 us -> 11.2 us  [the longest x1 4.87 us: device_step(): call(cross_kernel, [sums, sums, f32(6, NQ, *BLOCK)], 5, (), 1000000000, m...]
  transfers between devices with their start and end apart: 4 -> 7, of which waited for: 0 -> 3; matrix products, arithmetic and copies ran while one was open for 0% -> 0% of each run, Pallas kernels for 19% -> 18%
where the time goes in v3:
time: 46.3 us; the launch traced here: 46.1 us
  starting transfers between devices  27.1 us (59%)
  Pallas kernels  11.2 us (24%)
  waiting for transfers between devices  4.79 us (10%)
  local copies, waits for them, and re-layouts  2.29 us (5%)
  between operations  0.74 us (2%)
    all_to_all x1, starting transfers between devices, device_step(): lax.all_to_all(send.reshape(256, 1, 128), ALL, 0, 0, tiled=True)  20.1 us
    ppermute x6, starting transfers between devices, exchange(): return lax.ppermute(value, axes, both)  6.96 us
    pallas_call x1, Pallas kernels, device_step(): call(cross_kernel, [sums, sums, f32(6, NQ, *BLOCK)], 5, (), 1000000000, m...  4.87 us
    ppermute x6, waiting for transfers between devices, exchange(): return lax.ppermute(value, axes, both)  2.47 us
    all_to_all x1, waiting for transfers between devices, device_step(): lax.all_to_all(send.reshape(256, 1, 128), ALL, 0, 0, tiled=True)  2.32 us
    unnamed x14, local copies, waits for them, and re-layouts  2.29 us
    pallas_call x1, Pallas kernels, device_step(): call(stay_kernel, [f32(NQ, *BLOCK)], 5, [scratch(3, NQ)], 1000000000, mib=6)  2.05 us
    pallas_call x1, Pallas kernels, device_step(): call(chi_kernel, [f32(256, 128)], 9, [scratch(3, 5)], 5000000, mib=6)  1.37 us
  transfers between devices with their start and end apart: 7, of which 3 were waited for; matrix products, arithmetic and copies ran while one was open for 0% of the time, Pallas kernels for 18%

profile of v3, /device:TPU:1, one launch (start us, length us, event | category | flops | bytes accessed | tf_op | source)
XLA Modules:
  0.0 46.1 jit_solution(5345870354525211882)
XLA Ops:
  0.6 0.0 copy-start.4
  0.6 0.7 %copy-done.4 = f32[5,4,256]{2,1,0:T(4,128)S(1)} copy-done((f32[5,4,256]{2,1,0:T(4,128)S(1)}, f32[5,4,256]{2,1,0:T(4,128)}, u32[]{:S(2)}) %copy-start.4) | copy-done | bytes 20504
  1.4 0.0 copy-start
  1.4 0.0 copy-start.1
  1.4 0.0 copy-start.2
  1.4 0.0 copy-start.3
  1.4 0.0 copy-start.5
  1.4 0.0 copy-start.6
  1.4 0.1 shard_map.77.edge_ref
  1.5 1.3 %copy-done = f32[5,80,4,256]{3,2,1,0:T(4,128)S(1)} copy-done((f32[5,80,4,256]{3,2,1,0:T(4,128)S(1)}, f32[5,80,4,256]{3,2,1,0:T(4,128)}, u32[]{:S(2)}) %copy-start) | copy-done | bytes 1638424
  2.8 0.0 copy-done.1
  2.8 0.1 copy-done.2
  2.9 0.1 copy-done.3
  3.0 0.0 copy-done.5
  3.0 0.0 copy-done.6
  3.0 0.8 %shard_map.78 = (f32[9,8,128]{2,1,0:T(8,128)S(1)}, f32[9,8,128]{2,1,0:T(8,128)S(1)}, f32[7,8,128]{2,1,0:T(8,128)S(1)}, s32[8,128]{1,0:T(8,128)S(1)}, f32[8,128]{1,0:T(8,128)S(1)}) custom-call(f32[5,80,8,128]{3,2,1,0:T(8,128)S(1)} %bitcast.40, f32[80,8,128]{2,1,0:T(8,128)S(1)} %bitcast.45, f32[80,8,128]{2,1,0:T(8,128)S(1)} %bitcast.50, ...), custom_call_target="tpu_custom_call" | custom-call | flops 10000000 | bytes 100000 | tf_op jit(solution)/shard_map/pallas_call | solution.py:424
  3.8 3.3 %collective-permute-start.2 = (f32[9,8,128]{2,1,0:T(8,128)S(1)}, f32[9,8,128]{2,1,0:T(8,128)S(1)}, u32[]{:S(2)}, u32[]{:S(2)}) collective-permute-start(f32[9,8,128]{2,1,0:T(8,128)S(1)} %get-tuple-element.23), channel_id=1, source_target_pairs={{0,16},{32,48},{64,80},{96,112},{128,144},{160,176},{192,208},{224... | collective-permute-start | bytes 110600 | tf_op jit(solution)/shard_map/ppermute | solution.py:389
  7.1 0.0 collective-permute-start.3
  7.1 0.8 %collective-permute-start = (f32[8,128]{1,0:T(8,128)S(1)}, f32[8,128]{1,0:T(8,128)S(1)}, u32[]{:S(2)}, u32[]{:S(2)}) collective-permute-start(f32[8,128]{1,0:T(8,128)S(1)} %get-tuple-element.18), channel_id=1, source_target_pairs={{0,1},{2,3},{4,5},{6,7},{8,9},{10,11},{12,13},{14,15},{1,0},{3,2},... | collective-permute-start | bytes 12296 | tf_op jit(solution)/shard_map/ppermute | solution.py:389
  7.9 0.6 %collective-permute-start.1 = (f32[8,128]{1,0:T(8,128)S(1)}, f32[8,128]{1,0:T(8,128)S(1)}, u32[]{:S(2)}, u32[]{:S(2)}) collective-permute-start(f32[8,128]{1,0:T(8,128)S(1)} %shard_map.77.edge_ref), channel_id=1, source_target_pairs={{1,2},{3,4},{5,6},{7,8},{9,10},{11,12},{13,14},{2,1},{4,3},{6,5},{... | collective-permute-start | bytes 12296 | tf_op jit(solution)/shard_map/ppermute | solution.py:389
  8.5 1.0 %collective-permute-done.dec_a_ref = f32[8,128]{1,0:T(8,128)S(1)} collective-permute-done((f32[8,128]{1,0:T(8,128)S(1)}, f32[8,128]{1,0:T(8,128)S(1)}, u32[]{:S(2)}, u32[]{:S(2)}) %collective-permute-start) | collective-permute-done | bytes 4128 | tf_op jit(solution)/shard_map/ppermute | solution.py:389
  9.5 0.0 collective-permute-done.1.dec_b_ref
  9.5 1.2 %shard_map.79 = (f32[8,128]{1,0:T(8,128)S(1)}, f32[8,128]{1,0:T(8,128)S(1)}, f32[8,128]{1,0:T(8,128)S(1)}, s32[80,8,128]{2,1,0:T(8,128)S(1)}) custom-call(f32[5,80,8,128]{3,2,1,0:T(8,128)S(1)} %bitcast.41, f32[80,8,128]{2,1,0:T(8,128)S(1)} %bitcast.46, f32[80,8,128]{2,1,0:T(8,128)S(1)} %bitcast.51, s32[80,8,128]{2,1,0:T(8,128)S(1)} %bitcast.56, ...), custom_call_target="tpu_custom_call" | custom-call | flops 300000000 | bytes 100000 | tf_op jit(solution)/shard_map/pallas_call | solution.py:432
  10.7 0.0 collective-permute-done.2.from_a_ref
  10.7 0.0 collective-permute-done.3.from_b_ref
  10.7 1.4 %shard_map.80.send_ref = f32[256,128]{1,0:T(8,128)} custom-call(f32[5,80,8,128]{3,2,1,0:T(8,128)S(1)} %bitcast.42, f32[80,8,128]{2,1,0:T(8,128)S(1)} %bitcast.47, f32[80,8,128]{2,1,0:T(8,128)S(1)} %bitcast.52, s32[80,8,128]{2,1,0:T(8,128)S(1)} %get-tuple-element.19.code_ref, f32[8,128]{1,0:T(8,128)S(1)} %get-tuple-element.20.chi_ref, ...), custom_call_target="tpu_custom_call" | custom-call | flops 5000000 | bytes 100000 | tf_op jit(solution)/shard_map/pallas_call | solution.py:438
  12.1 20.1 %all-to-all-start = ((f32[256,1,128]{2,1,0:T(1,128)}), f32[256,1,128]{2,1,0:T(1,128)S(1)}, u32[]{:S(2)}, u32[]{:S(2)}) async-start(f32[256,1,128]{2,1,0:T(1,128)} %bitcast.31), calls=%async_computation | async-start | bytes 262144 | tf_op jit(solution)/shard_map/all_to_all | solution.py:441
  32.2 4.9 %shard_map.81 = (f32[5,8,128]{2,1,0:T(8,128)S(1)}, f32[5,8,128]{2,1,0:T(8,128)S(1)}, f32[6,20,8,128]{3,2,1,0:T(8,128)S(1)}) custom-call(f32[5,80,8,128]{3,2,1,0:T(8,128)S(1)} %bitcast.43, f32[80,8,128]{2,1,0:T(8,128)S(1)} %bitcast.48, f32[80,8,128]{2,1,0:T(8,128)S(1)} %bitcast.53, s32[80,8,128]{2,1,0:T(8,128)S(1)} %get-tuple-element.19.code_ref, ...), custom_call_target="tpu_custom_call" | custom-call | flops 1000000000 | bytes 100000 | tf_op jit(solution)/shard_map/pallas_call | solution.py:443
  37.1 2.2 %collective-permute-start.4 = (f32[5,8,128]{2,1,0:T(8,128)S(1)}, f32[5,8,128]{2,1,0:T(8,128)S(1)}, u32[]{:S(2)}, u32[]{:S(2)}) collective-permute-start(f32[5,8,128]{2,1,0:T(8,128)S(1)} %get-tuple-element.26), channel_id=1, source_target_pairs={{0,16},{32,48},{64,80},{96,112},{128,144},{160,176},{192,208},{224... | collective-permute-start | bytes 61448 | tf_op jit(solution)/shard_map/ppermute | solution.py:389
  39.3 0.0 collective-permute-start.5
  39.3 2.1 %shard_map.82.total_ref = f32[20,8,128]{2,1,0:T(8,128)S(1)} custom-call(f32[5,80,8,128]{3,2,1,0:T(8,128)S(1)} %bitcast.44, f32[80,8,128]{2,1,0:T(8,128)S(1)} %bitcast.49, f32[80,8,128]{2,1,0:T(8,128)S(1)} %bitcast.54, s32[80,8,128]{2,1,0:T(8,128)S(1)} %get-tuple-element.19.code_ref, f32[6,20,8,128]{3,2,1,0:T(8,128)S(1)} %get-tuple-element.25.cross_ref), custom_call_target="tpu_custom_call" | custom-call | flops 1000000000 | bytes 100000 | tf_op jit(solution)/shard_map/pallas_call | solution.py:448
  41.4 0.0 collective-permute-done.4.from_a_ref
  41.4 1.4 %collective-permute-done.5.from_b_ref = f32[5,8,128]{2,1,0:T(8,128)S(1)} collective-permute-done((f32[5,8,128]{2,1,0:T(8,128)S(1)}, f32[5,8,128]{2,1,0:T(8,128)S(1)}, u32[]{:S(2)}, u32[]{:S(2)}) %collective-permute-start.5) | collective-permute-done | bytes 20512 | tf_op jit(solution)/shard_map/ppermute | solution.py:389
  42.9 2.3 %all-to-all-done = f32[256,1,128]{2,1,0:T(1,128)S(1)} async-done(((f32[256,1,128]{2,1,0:T(1,128)}), f32[256,1,128]{2,1,0:T(1,128)S(1)}, u32[]{:S(2)}, u32[]{:S(2)}) %all-to-all-start) | async-done | bytes 131104 | tf_op jit(solution)/shard_map/all_to_all | solution.py:441
  45.2 0.9 %shard_map.83 = (f32[5,8,128]{2,1,0:T(8,128)}, f32[1,1]{1,0:T(1,128)}) custom-call(f32[5,8,128]{2,1,0:T(8,128)S(1)} %bitcast.61, f32[20,8,128]{2,1,0:T(8,128)S(1)} %shard_map.82.total_ref, f32[5,8,128]{2,1,0:T(8,128)S(1)} %collective-permute-done.4.from_a_ref, f32[5,8,128]{2,1,0:T(8,128)S(1)} %collective-permute-done.5.from_b_ref, f32[256,128]{1,0:T(8,128)S(1)} %bitcast.57), custom_call_target="tpu_custom_call" | custom-call | flops 100000 | bytes 100000 | tf_op jit(solution)/shard_map/pallas_call | solution.py:451
Async XLA Ops:
  0.6 0.7 %copy-start.4 = (f32[5,4,256]{2,1,0:T(4,128)S(1)}, f32[5,4,256]{2,1,0:T(4,128)}, u32[]{:S(2)}) copy-start(f32[5,4,256]{2,1,0:T(4,128)} %param.9) | copy-start | bytes 61444
  1.4 1.4 %copy-start = (f32[5,80,4,256]{3,2,1,0:T(4,128)S(1)}, f32[5,80,4,256]{3,2,1,0:T(4,128)}, u32[]{:S(2)}) copy-start(f32[5,80,4,256]{3,2,1,0:T(4,128)} %param.6) | copy-start | bytes 4915204
  1.4 1.5 %copy-start.1 = (f32[80,4,256]{2,1,0:T(4,128)S(1)}, f32[80,4,256]{2,1,0:T(4,128)}, u32[]{:S(2)}) copy-start(f32[80,4,256]{2,1,0:T(4,128)} %param.7) | copy-start | bytes 983044
  1.4 1.6 %copy-start.2 = (f32[80,4,256]{2,1,0:T(4,128)S(1)}, f32[80,4,256]{2,1,0:T(4,128)}, u32[]{:S(2)}) copy-start(f32[80,4,256]{2,1,0:T(4,128)} %param.8) | copy-start | bytes 983044
  1.4 1.7 %copy-start.3 = (s32[80,4,256]{2,1,0:T(4,128)S(1)}, s32[80,4,256]{2,1,0:T(4,128)}, u32[]{:S(2)}) copy-start(s32[80,4,256]{2,1,0:T(4,128)} %param.10) | copy-start | bytes 983044
  1.4 1.7 %copy-start.5 = (f32[5,4,256]{2,1,0:T(4,128)S(1)}, f32[5,4,256]{2,1,0:T(4,128)}, u32[]{:S(2)}) copy-start(f32[5,4,256]{2,1,0:T(4,128)} %param.9) | copy-start | bytes 61444
  1.4 1.6 %copy-start.6 = (s32[4,256]{1,0:T(4,128)S(1)}, s32[4,256]{1,0:T(4,128)}, u32[]{:S(2)}) copy-start(s32[4,256]{1,0:T(4,128)} %param.11) | copy-start | bytes 12292
  3.8 6.9 %collective-permute-start.2 = (f32[9,8,128]{2,1,0:T(8,128)S(1)}, f32[9,8,128]{2,1,0:T(8,128)S(1)}, u32[]{:S(2)}, u32[]{:S(2)}) collective-permute-start(f32[9,8,128]{2,1,0:T(8,128)S(1)} %get-tuple-element.23), channel_id=1, source_target_pairs={{0,16},{32,48},{64,80},{96,112},{128,144},{160,176},{192,208},{224... | collective-permute-start | bytes 110600 | tf_op jit(solution)/shard_map/ppermute | solution.py:389
  7.1 3.6 %collective-permute-start.3 = (f32[9,8,128]{2,1,0:T(8,128)S(1)}, f32[9,8,128]{2,1,0:T(8,128)S(1)}, u32[]{:S(2)}, u32[]{:S(2)}) collective-permute-start(f32[9,8,128]{2,1,0:T(8,128)S(1)} %get-tuple-element.24), channel_id=1, source_target_pairs={{16,32},{48,64},{80,96},{112,128},{144,160},{176,192},{208,224},{2... | collective-permute-start | bytes 110600 | tf_op jit(solution)/shard_map/ppermute | solution.py:389
  7.1 2.5 %collective-permute-start = (f32[8,128]{1,0:T(8,128)S(1)}, f32[8,128]{1,0:T(8,128)S(1)}, u32[]{:S(2)}, u32[]{:S(2)}) collective-permute-start(f32[8,128]{1,0:T(8,128)S(1)} %get-tuple-element.18), channel_id=1, source_target_pairs={{0,1},{2,3},{4,5},{6,7},{8,9},{10,11},{12,13},{14,15},{1,0},{3,2},... | collective-permute-start | bytes 12296 | tf_op jit(solution)/shard_map/ppermute | solution.py:389
  7.9 1.7 %collective-permute-start.1 = (f32[8,128]{1,0:T(8,128)S(1)}, f32[8,128]{1,0:T(8,128)S(1)}, u32[]{:S(2)}, u32[]{:S(2)}) collective-permute-start(f32[8,128]{1,0:T(8,128)S(1)} %shard_map.77.edge_ref), channel_id=1, source_target_pairs={{1,2},{3,4},{5,6},{7,8},{9,10},{11,12},{13,14},{2,1},{4,3},{6,5},{... | collective-permute-start | bytes 12296 | tf_op jit(solution)/shard_map/ppermute | solution.py:389
  12.1 33.1 %all-to-all-start = ((f32[256,1,128]{2,1,0:T(1,128)}), f32[256,1,128]{2,1,0:T(1,128)S(1)}, u32[]{:S(2)}, u32[]{:S(2)}) async-start(f32[256,1,128]{2,1,0:T(1,128)} %bitcast.31), calls=%async_computation | async-start | bytes 262144 | tf_op jit(solution)/shard_map/all_to_all | solution.py:441
  37.1 4.3 %collective-permute-start.4 = (f32[5,8,128]{2,1,0:T(8,128)S(1)}, f32[5,8,128]{2,1,0:T(8,128)S(1)}, u32[]{:S(2)}, u32[]{:S(2)}) collective-permute-start(f32[5,8,128]{2,1,0:T(8,128)S(1)} %get-tuple-element.26), channel_id=1, source_target_pairs={{0,16},{32,48},{64,80},{96,112},{128,144},{160,176},{192,208},{224... | collective-permute-start | bytes 61448 | tf_op jit(solution)/shard_map/ppermute | solution.py:389
  39.3 3.5 %collective-permute-start.5 = (f32[5,8,128]{2,1,0:T(8,128)S(1)}, f32[5,8,128]{2,1,0:T(8,128)S(1)}, u32[]{:S(2)}, u32[]{:S(2)}) collective-permute-start(f32[5,8,128]{2,1,0:T(8,128)S(1)} %get-tuple-element.27), channel_id=1, source_target_pairs={{16,32},{48,64},{80,96},{112,128},{144,160},{176,192},{208,224},{2... | collective-permute-start | bytes 61448 | tf_op jit(solution)/shard_map/ppermute | solution.py:389

commit v4 on v3

--- a/solution.py
+++ b/solution.py
@@ -12,7 +12,8 @@
 
 PAIRS = [(p, q) for p in range(5) for q in range(p, 5)]
 NQ = 20
-EDGE_FLOPS = 20_000_000_000
+CROSS = (0, 1, 2, 6, 7, 8)
+SEED_FLOPS = 20_000_000_000
 VM = pl.BlockSpec(memory_space=pltpu.VMEM)
 SM = pl.BlockSpec(memory_space=pltpu.SMEM)
 BLOCK = (8, 128)
@@ -48,13 +49,8 @@
     return x if by == 0 else pltpu.roll(x, by, 0)
 
 
-def edge_kernel(params_ref, out_ref):
-    lane, _, half = grids()
-    out = jnp.zeros(BLOCK, jnp.float32)
-    for p in range(5):
-        value = params_ref[p]
-        out = jnp.where(lane == p, jnp.where(half == 0, lanes(value, p), lanes(value, p + 1)), out)
-    out_ref[...] = out
+def seed_kernel(out_ref):
+    out_ref[...] = jnp.zeros(BLOCK, jnp.float32)
 
 
 def shift_sum(minus, mid, plus, lane, half):
@@ -100,12 +96,11 @@
 
 
 def column_kernel(
-    design_ref, observed_ref, weight_ref, offsets_ref, counts_ref, params_ref, edge_ref,
-    to_a_ref, to_b_ref, packed_ref, codes_ref, again_ref,
+    design_ref, observed_ref, weight_ref, offsets_ref, counts_ref, params_ref, seed_ref,
+    to_a_ref, to_b_ref, packed_ref, codes_ref,
 ):
     lane, row, half = grids()
-    again_ref[...] = edge_ref[...]
-    packed = [jnp.zeros(BLOCK, jnp.float32) for _ in range(7)]
+    packed = [seed_ref[...]] * 7
     codes = jnp.full(BLOCK, 9, jnp.int32)
     counts = jnp.zeros(BLOCK, jnp.int32)
     for k in range(80):
@@ -133,20 +128,26 @@
     return [jnp.sum(jnp.where(half == j, flat, 0.0), axis=0, keepdims=True) for j in range(2)]
 
 
-def columns_around(x, beyond, p, lane, half):
+def columns_around(x, lane):
     below = lanes(x, 1)
-    below = jnp.where(lane == 0, jnp.where(half == 1, subs(below, 4), lanes(beyond, -p)), below)
+    below = jnp.where(lane == 0, subs(below, 4), below)
     above = lanes(x, 127)
-    above = jnp.where(lane == 127, jnp.where(half == 0, subs(above, 4), lanes(beyond, 127 - p)), above)
+    above = jnp.where(lane == 127, subs(above, 4), above)
     return below, x, above
 
 
-def inside_kernel(
-    design_ref, observed_ref, weight_ref, offsets_ref, counts_ref, params_ref,
-    packed_ref, codes_ref, dec_a_ref, dec_b_ref,
-    lines_ref, chi_ref, halo_ref, code_ref, win_ref,
+def lines_kernel(
+    design_ref, observed_ref, weight_ref, offsets_ref, counts_ref, params_ref, packed_ref, codes_ref,
+    lines_ref, code_ref, chi_ref, win_ref,
 ):
     lane, row, half = grids()
+    counts = counts_ref[...]
+
+    def mark(k, carry):
+        code_ref[k] = jnp.where(counts > k, offsets_ref[k], 9)
+        return carry
+
+    lax.fori_loop(0, 80, mark, 0, unroll=8)
     zero = jnp.zeros(BLOCK, jnp.float32)
     d, o, weight, codes = [packed_ref[p] for p in range(5)], packed_ref[5], packed_ref[6], codes_ref[...]
     found = []
@@ -166,39 +167,41 @@
     for i, x in enumerate((low, mid, high)):
         for j, line in enumerate(flatten(x, row, half)):
             lines_ref[2 * i + j : 2 * i + j + 1, :] = line
-    counts = counts_ref[...]
     lines_ref[6:7, :] = jnp.where(lane[:1] == NQ + 1, jnp.sum(counts.astype(jnp.float32)), 0.0)
 
-    dec_odd = lax.axis_index("dec_1")
-    halo = jnp.where((half == 0) == (dec_odd == 0), dec_a_ref[...], dec_b_ref[...])
-    halo = subs(halo, 4)
-    halo_ref[...] = halo
+
     for p in range(5):
         value = params_ref[p]
         for a in range(3):
-            shift = (1, 0, 7)[a]
-            found = columns_around(subs(value, shift), subs(halo, shift), p, lane, half)
+            found = columns_around(subs(value, (1, 0, 7)[a]), lane)
             for b in range(3):
                 win_ref[3 * a + b, p] = found[b]
-
-    least = jnp.where(row == 0, 3, 0)
-    most = jnp.where(row == 3, 5, 8)
+    inside = []
+    for code in range(9):
+        a, b = divmod(code, 3)
+        off = (row == 0) if a == 0 else (row == 3) if a == 2 else (row < 0)
+        if b == 0:
+            off = off | ((lane == 0) & (half == 0))
+        if b == 2:
+            off = off | ((lane == 127) & (half == 1))
+        inside.append(jnp.where(off, -1, code))
 
     def body(k, acc):
-        code = jnp.where(counts > k, offsets_ref[k], 9)
-        code_ref[k] = code
-        hits = [code == c for c in range(1, 9)]
+        code = code_ref[k]
+        hits = [code == x for x in inside]
         resid = observed_ref[k]
         for p in range(5):
             source = win_ref[0, p]
             for c in range(1, 9):
-                source = jnp.where(hits[c - 1], win_ref[c, p], source)
+                source = jnp.where(hits[c], win_ref[c, p], source)
             resid = resid - design_ref[p, k] * source
-        inside = (code >= least) & (code <= most)
-        w = jnp.where(inside, weight_ref[k], 0.0)
+        some = hits[0]
+        for c in range(1, 9):
+            some = some | hits[c]
+        w = jnp.where(some, weight_ref[k], 0.0)
         return acc + w * resid * resid
 
-    chi_ref[...] = lax.fori_loop(0, 80, body, zero, unroll=4)
+    chi_ref[...] = lax.fori_loop(0, 80, body, jnp.zeros(BLOCK, jnp.float32), unroll=4)
 
 
 def ra_sides(from_a_ref, from_b_ref):
@@ -215,7 +218,8 @@
 
 def chi_kernel(
     design_ref, observed_ref, weight_ref, code_ref,
-    chi_ref, halo_ref, lines_ref, from_a_ref, from_b_ref, send_ref, win_ref,
+    chi_ref, packed_ref, codes_ref, lines_ref, dec_a_ref, dec_b_ref, from_a_ref, from_b_ref,
+    send_ref, after_ref, win_ref,
 ):
     lane, row, half = grids()
     ra = lax.axis_index(RA)
@@ -224,17 +228,29 @@
     for p in range(5):
         g, i = divmod(p, 4)
         value = jnp.where(row == 0, subs(from_low(g), -i), subs(from_high(g), 3 - i))
-        found = columns_around(value, jnp.zeros(BLOCK, jnp.float32), p, lane, half)
+        found = columns_around(value, lane)
         for b in range(3):
             win_ref[b, p] = found[b]
 
-    halo = halo_ref[...]
-    halo = jnp.where(row == 3, subs(halo, 3), subs(halo, 5))
+    dec_odd = lax.axis_index("dec_1")
+    halo = []
+    for p in range(5):
+        below = subs(jnp.where(dec_odd == 0, dec_b_ref[p], dec_a_ref[p]), 4)
+        above = subs(jnp.where(dec_odd == 0, dec_a_ref[p], dec_b_ref[p]), 4)
+        halo.append(jnp.where(half == 0, below[:, 127:], above[:, :1]))
+    codes = codes_ref[...]
+    acc = chi_ref[...]
+    for a, shift, there in ((0, 1, row > 0), (1, 0, row >= 0), (2, 7, row < 3)):
+        resid = packed_ref[5]
+        for p in range(5):
+            resid = resid - packed_ref[p] * subs(halo[p], shift)
+        w = jnp.where((codes == 3 * a + 2 * half) & there, packed_ref[6], 0.0)
+        acc = acc + w * resid * resid
     corner = [jnp.where(row == 3, from_low(2 + i), from_high(2 + i)) for i in range(7)]
     resid = corner[5]
     for p in range(5):
-        resid = resid - corner[p] * halo[:, p : p + 1]
-    acc = chi_ref[...] + jnp.where((row == 0) | (row == 3), corner[6] * resid * resid, 0.0)
+        resid = resid - corner[p] * jnp.where(row == 3, subs(halo[p], 3), subs(halo[p], 5))
+    acc = acc + jnp.where((row == 0) | (row == 3), corner[6] * resid * resid, 0.0)
 
     wanted = [edge_code(b, row) for b in range(3)]
     wanted[0] = jnp.where((lane == 0) & (half == 0), -1, wanted[0])
@@ -253,6 +269,7 @@
 
     chi = jnp.sum(lax.fori_loop(0, 80, body, acc, unroll=4))
     base = jnp.where(lane == NQ, chi, jnp.broadcast_to(lines_ref[6:7, :], BLOCK))
+    after_ref[...] = base
     for g in range(32):
         send_ref[pl.ds(8 * g, 8), :] = base
 
@@ -269,10 +286,10 @@
 
 
 def cross_kernel(
-    design_ref, observed_ref, weight_ref, code_ref, send_ref, to_a_ref, to_b_ref, acc_ref
+    design_ref, observed_ref, weight_ref, code_ref, after_ref, to_a_ref, to_b_ref, acc_ref
 ):
     lane, row, half = grids()
-    for i, code in enumerate((0, 1, 2, 6, 7, 8)):
+    for i, code in enumerate(CROSS):
         acc = accumulate(design_ref, observed_ref, weight_ref, code_ref, code)
         for q in range(NQ):
             acc_ref[i, q] = acc[q]
@@ -416,33 +433,33 @@
     design, observed, weight, params, offsets, counts = (
         blocked(x) for x in (design, observed, weight, params, offsets, counts)
     )
-    (edge,) = call(edge_kernel, [f32(*BLOCK)], 1, (), EDGE_FLOPS)(params)
-    dec_b = exchange(edge, DEC, [(i, i + 1) for i in range(1, 15, 2)])
+    dec_b = exchange(params, DEC, [(i, i + 1) for i in range(1, 15, 2)])
+    dec_a = exchange(params, DEC, [(i, i + 1) for i in range(0, 16, 2)])
+    (seed,) = call(seed_kernel, [f32(*BLOCK)], 0, (), SEED_FLOPS)()
     ra_b_pairs = [(i, (i + 1) % 16) for i in range(1, 16, 2)]
     ra_a_pairs = [(i, i + 1) for i in range(0, 16, 2)]
     message = f32(9, *BLOCK)
-    to_a, to_b, packed, codes, again = call(
+    to_a, to_b, packed, codes = call(
         column_kernel,
-        [message, message, f32(7, *BLOCK), jax.ShapeDtypeStruct(BLOCK, jnp.int32), f32(*BLOCK)],
+        [message, message, f32(7, *BLOCK), jax.ShapeDtypeStruct(BLOCK, jnp.int32)],
         7, (), 10_000_000, mib=6,
-    )(design, observed, weight, offsets, counts, params, edge)
+    )(design, observed, weight, offsets, counts, params, seed)
     from_b = exchange(to_b, RA, ra_b_pairs)
-    dec_a = exchange(again, DEC, [(i, i + 1) for i in range(0, 16, 2)])
     from_a = exchange(to_a, RA, ra_a_pairs)
-    lines, chi, halo, code = call(
-        inside_kernel,
-        [f32(*BLOCK), f32(*BLOCK), f32(*BLOCK), jax.ShapeDtypeStruct((80,) + BLOCK, jnp.int32)],
-        10, [scratch(9, 5)], 300_000_000, mib=6,
-    )(design, observed, weight, offsets, counts, params, packed, codes, dec_a, dec_b)
+    lines, code, chi = call(
+        lines_kernel,
+        [f32(*BLOCK), jax.ShapeDtypeStruct((80,) + BLOCK, jnp.int32), f32(*BLOCK)],
+        8, [scratch(9, 5)], 300_000_000, mib=6,
+    )(design, observed, weight, offsets, counts, params, packed, codes)
     slots = (design, observed, weight, code)
-    (send,) = call(chi_kernel, [f32(256, 128)], 9, [scratch(3, 5)], 5_000_000, mib=6)(
-        *slots, chi, halo, lines, from_a, from_b
-    )
+    send, after = call(
+        chi_kernel, [f32(256, 128), f32(*BLOCK)], 12, [scratch(3, 5)], 5_000_000, mib=6
+    )(*slots, chi, packed, codes, lines, dec_a, dec_b, from_a, from_b)
     got = lax.all_to_all(send.reshape(256, 1, 128), ALL, 0, 0, tiled=True).reshape(256, 128)
     sums = f32(5, *BLOCK)
     sums_a, sums_b, cross = call(
         cross_kernel, [sums, sums, f32(6, NQ, *BLOCK)], 5, (), 1_000_000_000, mib=6
-    )(*slots, send)
+    )(*slots, after)
     sums_b = exchange(sums_b, RA, ra_b_pairs)
     sums_a = exchange(sums_a, RA, ra_a_pairs)
     (total,) = call(

time: 46.3 us -> 42.9 us (0.927)
  starting transfers between devices: 27.1 us -> 24.8 us
  Pallas kernels: 11.2 us -> 10.2 us
  local copies, waits for them, and re-layouts: 2.29 us -> 1.72 us
    all_to_all x1, starting transfers between devices: 20.1 us -> 14.9 us  [device_step(): lax.all_to_all(send.reshape(256, 1, 128), ALL, 0, 0, tiled=True)]
    ppermute x6, starting transfers between devices: 6.96 us -> 9.9 us  [exchange(): return lax.ppermute(value, axes, both)]
    pallas_call x1, Pallas kernels: 4.87 us -> 3.94 us  [device_step(): call(cross_kernel, [sums, sums, f32(6, NQ, *BLOCK)], 5, (), 1000000000, m...]
    all_to_all x1, waiting for transfers between devices: 2.32 us -> 3.23 us  [device_step(): lax.all_to_all(send.reshape(256, 1, 128), ALL, 0, 0, tiled=True)]
    unnamed x14 -> x12, local copies, waits for them, and re-layouts: 2.29 us -> 1.72 us
    ppermute x6, waiting for transfers between devices: 2.47 us -> 1.98 us  [exchange(): return lax.ppermute(value, axes, both)]
  transfers between devices with their start and end apart: 7 -> 7, of which waited for: 3 -> 3; matrix products, arithmetic and copies ran while one was open for 0% -> 0% of each run, Pallas kernels for 18% -> 17%
where the time goes in v4:
time: 42.9 us; the launch traced here: 42.7 us
  starting transfers between devices  24.8 us (58%)
  Pallas kernels  10.2 us (24%)
  waiting for transfers between devices  5.2 us (12%)
  local copies, waits for them, and re-layouts  1.72 us (4%)
  between operations  0.75 us (2%)
    all_to_all x1, starting transfers between devices, device_step(): lax.all_to_all(send.reshape(256, 1, 128), ALL, 0, 0, tiled=True)  14.9 us
    ppermute x6, starting transfers between devices, exchange(): return lax.ppermute(value, axes, both)  9.9 us
    pallas_call x1, Pallas kernels, device_step(): call(cross_kernel, [sums, sums, f32(6, NQ, *BLOCK)], 5, (), 1000000000, m...  3.94 us
    all_to_all x1, waiting for transfers between devices, device_step(): lax.all_to_all(send.reshape(256, 1, 128), ALL, 0, 0, tiled=True)  3.23 us
    pallas_call x1, Pallas kernels, device_step(): call(stay_kernel, [f32(NQ, *BLOCK)], 5, [scratch(3, NQ)], 1000000000, mib=6)  2.05 us
    ppermute x6, waiting for transfers between devices, exchange(): return lax.ppermute(value, axes, both)  1.98 us
    unnamed x12, local copies, waits for them, and re-layouts  1.72 us
    pallas_call x1, Pallas kernels, device_step(): call(chi_kernel, [f32(256, 128), f32(*BLOCK)], 12, [scratch(3, 5)], 50000...  1.37 us
  transfers between devices with their start and end apart: 7, of which 3 were waited for; matrix products, arithmetic and copies ran while one was open for 0% of the time, Pallas kernels for 17%

profile of v4, /device:TPU:1, one launch (start us, length us, event | category | flops | bytes accessed | tf_op | source)
XLA Modules:
  0.0 42.7 jit_solution(17976501254036848421)
XLA Ops:
  0.6 0.0 copy-start.5
  0.6 0.0 copy-start.3
  0.7 0.0 copy-start.4
  0.7 0.0 copy-start.2
  0.7 0.0 copy-start.1
  0.7 0.0 copy-start
  0.7 0.6 %copy-done.5 = s32[4,256]{1,0:T(4,128)S(1)} copy-done((s32[4,256]{1,0:T(4,128)S(1)}, s32[4,256]{1,0:T(4,128)}, u32[]{:S(2)}) %copy-start.5) | copy-done | bytes 4120
  1.3 0.3 copy-done.3
  1.6 0.0 copy-done.4
  1.6 0.1 copy-done.2
  1.7 0.1 copy-done.1
  1.8 0.6 %copy-done = f32[5,80,4,256]{3,2,1,0:T(4,128)S(1)} copy-done((f32[5,80,4,256]{3,2,1,0:T(4,128)S(1)}, f32[5,80,4,256]{3,2,1,0:T(4,128)}, u32[]{:S(2)}) %copy-start) | copy-done | bytes 1638424
  2.4 0.7 %shard_map.78 = (f32[9,8,128]{2,1,0:T(8,128)S(1)}, f32[9,8,128]{2,1,0:T(8,128)S(1)}, f32[7,8,128]{2,1,0:T(8,128)S(1)}, s32[8,128]{1,0:T(8,128)S(1)}) custom-call(f32[5,80,8,128]{3,2,1,0:T(8,128)S(1)} %bitcast.40, f32[80,8,128]{2,1,0:T(8,128)S(1)} %bitcast.45, f32[80,8,128]{2,1,0:T(8,128)S(1)} %bitcast.50, s32[80,8,128]{2,1,0:T(8,128)S(1)} %bitcast.55, ...), custom_call_target="tpu_custom_call" | custom-call | flops 10000000 | bytes 100000 | tf_op jit(solution)/shard_map/pallas_call | solution.py:442
  3.2 3.3 %collective-permute-start.2 = (f32[9,8,128]{2,1,0:T(8,128)S(1)}, f32[9,8,128]{2,1,0:T(8,128)S(1)}, u32[]{:S(2)}, u32[]{:S(2)}) collective-permute-start(f32[9,8,128]{2,1,0:T(8,128)S(1)} %get-tuple-element.21), channel_id=1, source_target_pairs={{0,16},{32,48},{64,80},{96,112},{128,144},{160,176},{192,208},{224... | collective-permute-start | bytes 110600 | tf_op jit(solution)/shard_map/ppermute | solution.py:406
  6.5 0.0 collective-permute-start.3
  6.5 0.7 %collective-permute-start.1 = (f32[5,8,128]{2,1,0:T(8,128)S(1)}, f32[5,8,128]{2,1,0:T(8,128)S(1)}, u32[]{:S(2)}, u32[]{:S(2)}) collective-permute-start(f32[5,8,128]{2,1,0:T(8,128)S(1)} %bitcast.59), channel_id=1, source_target_pairs={{1,2},{3,4},{5,6},{7,8},{9,10},{11,12},{13,14},{2,1},{4,3},{6,5},{... | collective-permute-start | bytes 61448 | tf_op jit(solution)/shard_map/ppermute | solution.py:406
  7.1 3.7 %collective-permute-start = (f32[5,8,128]{2,1,0:T(8,128)S(1)}, f32[5,8,128]{2,1,0:T(8,128)S(1)}, u32[]{:S(2)}, u32[]{:S(2)}) collective-permute-start(f32[5,8,128]{2,1,0:T(8,128)S(1)} %bitcast.60), channel_id=1, source_target_pairs={{0,1},{2,3},{4,5},{6,7},{8,9},{10,11},{12,13},{14,15},{1,0},{3,2},... | collective-permute-start | bytes 61448 | tf_op jit(solution)/shard_map/ppermute | solution.py:406
  10.8 1.2 %shard_map.79 = (f32[8,128]{1,0:T(8,128)S(1)}, s32[80,8,128]{2,1,0:T(8,128)S(1)}, f32[8,128]{1,0:T(8,128)S(1)}) custom-call(f32[5,80,8,128]{3,2,1,0:T(8,128)S(1)} %bitcast.41, f32[80,8,128]{2,1,0:T(8,128)S(1)} %bitcast.46, f32[80,8,128]{2,1,0:T(8,128)S(1)} %bitcast.51, s32[80,8,128]{2,1,0:T(8,128)S(1)} %bitcast.56, s32[8,128]{1,0:T(8,128)S(1)} %bitcast.64, ...), custom_call_target="tpu_custom_call" | custom-call | flops 300000000 | bytes 100000 | tf_op jit(solution)/shard_map/pallas_call | solution.py:449
  12.0 0.0 collective-permute-done.1.dec_b_ref
  12.0 0.5 %collective-permute-done.dec_a_ref = f32[5,8,128]{2,1,0:T(8,128)S(1)} collective-permute-done((f32[5,8,128]{2,1,0:T(8,128)S(1)}, f32[5,8,128]{2,1,0:T(8,128)S(1)}, u32[]{:S(2)}, u32[]{:S(2)}) %collective-permute-start) | collective-permute-done | bytes 20512 | tf_op jit(solution)/shard_map/ppermute | solution.py:406
  12.5 0.0 collective-permute-done.2.from_a_ref
  12.5 0.0 collective-permute-done.3.from_b_ref
  12.5 1.4 %shard_map.80 = (f32[256,128]{1,0:T(8,128)}, f32[8,128]{1,0:T(8,128)S(1)}) custom-call(f32[5,80,8,128]{3,2,1,0:T(8,128)S(1)} %bitcast.42, f32[80,8,128]{2,1,0:T(8,128)S(1)} %bitcast.47, f32[80,8,128]{2,1,0:T(8,128)S(1)} %bitcast.52, s32[80,8,128]{2,1,0:T(8,128)S(1)} %get-tuple-element.18.code_ref, f32[8,128]{1,0:T(8,128)S(1)} %get-tuple-element.19.chi_ref, ...), custom_call_target="tpu_custom_call" | custom-call | flops 5000000 | bytes 100000 | tf_op jit(solution)/shard_map/pallas_call | solution.py:455
  13.9 14.9 %all-to-all-start = ((f32[256,1,128]{2,1,0:T(1,128)}), f32[256,1,128]{2,1,0:T(1,128)S(1)}, u32[]{:S(2)}, u32[]{:S(2)}) async-start(f32[256,1,128]{2,1,0:T(1,128)} %bitcast.31), calls=%async_computation | async-start | bytes 262144 | tf_op jit(solution)/shard_map/all_to_all | solution.py:458
  28.8 3.9 %shard_map.81 = (f32[5,8,128]{2,1,0:T(8,128)S(1)}, f32[5,8,128]{2,1,0:T(8,128)S(1)}, f32[6,20,8,128]{3,2,1,0:T(8,128)S(1)}) custom-call(f32[5,80,8,128]{3,2,1,0:T(8,128)S(1)} %bitcast.43, f32[80,8,128]{2,1,0:T(8,128)S(1)} %bitcast.48, f32[80,8,128]{2,1,0:T(8,128)S(1)} %bitcast.53, s32[80,8,128]{2,1,0:T(8,128)S(1)} %get-tuple-element.18.code_ref, ...), custom_call_target="tpu_custom_call" | custom-call | flops 1000000000 | bytes 100000 | tf_op jit(solution)/shard_map/pallas_call | solution.py:460
  32.8 2.2 %collective-permute-start.4 = (f32[5,8,128]{2,1,0:T(8,128)S(1)}, f32[5,8,128]{2,1,0:T(8,128)S(1)}, u32[]{:S(2)}, u32[]{:S(2)}) collective-permute-start(f32[5,8,128]{2,1,0:T(8,128)S(1)} %get-tuple-element.25), channel_id=1, source_target_pairs={{0,16},{32,48},{64,80},{96,112},{128,144},{160,176},{192,208},{224... | collective-permute-start | bytes 61448 | tf_op jit(solution)/shard_map/ppermute | solution.py:406
  35.0 0.0 collective-permute-start.5
  35.0 2.1 %shard_map.82.total_ref = f32[20,8,128]{2,1,0:T(8,128)S(1)} custom-call(f32[5,80,8,128]{3,2,1,0:T(8,128)S(1)} %bitcast.44, f32[80,8,128]{2,1,0:T(8,128)S(1)} %bitcast.49, f32[80,8,128]{2,1,0:T(8,128)S(1)} %bitcast.54, s32[80,8,128]{2,1,0:T(8,128)S(1)} %get-tuple-element.18.code_ref, f32[6,20,8,128]{3,2,1,0:T(8,128)S(1)} %get-tuple-element.24.cross_ref), custom_call_target="tpu_custom_call" | custom-call | flops 1000000000 | bytes 100000 | tf_op jit(solution)/shard_map/pallas_call | solution.py:465
  37.1 0.0 collective-permute-done.4.from_a_ref
  37.1 1.5 %collective-permute-done.5.from_b_ref = f32[5,8,128]{2,1,0:T(8,128)S(1)} collective-permute-done((f32[5,8,128]{2,1,0:T(8,128)S(1)}, f32[5,8,128]{2,1,0:T(8,128)S(1)}, u32[]{:S(2)}, u32[]{:S(2)}) %collective-permute-start.5) | collective-permute-done | bytes 20512 | tf_op jit(solution)/shard_map/ppermute | solution.py:406
  38.5 3.2 %all-to-all-done = f32[256,1,128]{2,1,0:T(1,128)S(1)} async-done(((f32[256,1,128]{2,1,0:T(1,128)}), f32[256,1,128]{2,1,0:T(1,128)S(1)}, u32[]{:S(2)}, u32[]{:S(2)}) %all-to-all-start) | async-done | bytes 131104 | tf_op jit(solution)/shard_map/all_to_all | solution.py:458
  41.8 0.9 %shard_map.83 = (f32[5,8,128]{2,1,0:T(8,128)}, f32[1,1]{1,0:T(1,128)}) custom-call(f32[5,8,128]{2,1,0:T(8,128)S(1)} %bitcast.62, f32[20,8,128]{2,1,0:T(8,128)S(1)} %shard_map.82.total_ref, f32[5,8,128]{2,1,0:T(8,128)S(1)} %collective-permute-done.4.from_a_ref, f32[5,8,128]{2,1,0:T(8,128)S(1)} %collective-permute-done.5.from_b_ref, f32[256,128]{1,0:T(8,128)S(1)} %bitcast.57), custom_call_target="tpu_custom_call" | custom-call | flops 100000 | bytes 100000 | tf_op jit(solution)/shard_map/pallas_call | solution.py:468
  (1 shorter events, 0.0 us)
Async XLA Ops:
  0.6 0.7 %copy-start.5 = (s32[4,256]{1,0:T(4,128)S(1)}, s32[4,256]{1,0:T(4,128)}, u32[]{:S(2)}) copy-start(s32[4,256]{1,0:T(4,128)} %param.11) | copy-start | bytes 12292
  0.6 1.0 %copy-start.3 = (s32[80,4,256]{2,1,0:T(4,128)S(1)}, s32[80,4,256]{2,1,0:T(4,128)}, u32[]{:S(2)}) copy-start(s32[80,4,256]{2,1,0:T(4,128)} %param.10) | copy-start | bytes 983044
  0.7 1.0 %copy-start.4 = (f32[5,4,256]{2,1,0:T(4,128)S(1)}, f32[5,4,256]{2,1,0:T(4,128)}, u32[]{:S(2)}) copy-start(f32[5,4,256]{2,1,0:T(4,128)} %param.9) | copy-start | bytes 61444
  0.7 1.1 %copy-start.2 = (f32[80,4,256]{2,1,0:T(4,128)S(1)}, f32[80,4,256]{2,1,0:T(4,128)}, u32[]{:S(2)}) copy-start(f32[80,4,256]{2,1,0:T(4,128)} %param.8) | copy-start | bytes 983044
  0.7 1.2 %copy-start.1 = (f32[80,4,256]{2,1,0:T(4,128)S(1)}, f32[80,4,256]{2,1,0:T(4,128)}, u32[]{:S(2)}) copy-start(f32[80,4,256]{2,1,0:T(4,128)} %param.7) | copy-start | bytes 983044
  0.7 1.7 %copy-start = (f32[5,80,4,256]{3,2,1,0:T(4,128)S(1)}, f32[5,80,4,256]{3,2,1,0:T(4,128)}, u32[]{:S(2)}) copy-start(f32[5,80,4,256]{3,2,1,0:T(4,128)} %param.6) | copy-start | bytes 4915204
  3.2 9.4 %collective-permute-start.2 = (f32[9,8,128]{2,1,0:T(8,128)S(1)}, f32[9,8,128]{2,1,0:T(8,128)S(1)}, u32[]{:S(2)}, u32[]{:S(2)}) collective-permute-start(f32[9,8,128]{2,1,0:T(8,128)S(1)} %get-tuple-element.21), channel_id=1, source_target_pairs={{0,16},{32,48},{64,80},{96,112},{128,144},{160,176},{192,208},{224... | collective-permute-start | bytes 110600 | tf_op jit(solution)/shard_map/ppermute | solution.py:406
  6.5 6.1 %collective-permute-start.3 = (f32[9,8,128]{2,1,0:T(8,128)S(1)}, f32[9,8,128]{2,1,0:T(8,128)S(1)}, u32[]{:S(2)}, u32[]{:S(2)}) collective-permute-start(f32[9,8,128]{2,1,0:T(8,128)S(1)} %get-tuple-element.22), channel_id=1, source_target_pairs={{16,32},{48,64},{80,96},{112,128},{144,160},{176,192},{208,224},{2... | collective-permute-start | bytes 110600 | tf_op jit(solution)/shard_map/ppermute | solution.py:406
  6.5 5.6 %collective-permute-start.1 = (f32[5,8,128]{2,1,0:T(8,128)S(1)}, f32[5,8,128]{2,1,0:T(8,128)S(1)}, u32[]{:S(2)}, u32[]{:S(2)}) collective-permute-start(f32[5,8,128]{2,1,0:T(8,128)S(1)} %bitcast.59), channel_id=1, source_target_pairs={{1,2},{3,4},{5,6},{7,8},{9,10},{11,12},{13,14},{2,1},{4,3},{6,5},{... | collective-permute-start | bytes 61448 | tf_op jit(solution)/shard_map/ppermute | solution.py:406
  7.1 5.4 %collective-permute-start = (f32[5,8,128]{2,1,0:T(8,128)S(1)}, f32[5,8,128]{2,1,0:T(8,128)S(1)}, u32[]{:S(2)}, u32[]{:S(2)}) collective-permute-start(f32[5,8,128]{2,1,0:T(8,128)S(1)} %bitcast.60), channel_id=1, source_target_pairs={{0,1},{2,3},{4,5},{6,7},{8,9},{10,11},{12,13},{14,15},{1,0},{3,2},... | collective-permute-start | bytes 61448 | tf_op jit(solution)/shard_map/ppermute | solution.py:406
  13.9 27.9 %all-to-all-start = ((f32[256,1,128]{2,1,0:T(1,128)}), f32[256,1,128]{2,1,0:T(1,128)S(1)}, u32[]{:S(2)}, u32[]{:S(2)}) async-start(f32[256,1,128]{2,1,0:T(1,128)} %bitcast.31), calls=%async_computation | async-start | bytes 262144 | tf_op jit(solution)/shard_map/all_to_all | solution.py:458
  32.8 4.3 %collective-permute-start.4 = (f32[5,8,128]{2,1,0:T(8,128)S(1)}, f32[5,8,128]{2,1,0:T(8,128)S(1)}, u32[]{:S(2)}, u32[]{:S(2)}) collective-permute-start(f32[5,8,128]{2,1,0:T(8,128)S(1)} %get-tuple-element.25), channel_id=1, source_target_pairs={{0,16},{32,48},{64,80},{96,112},{128,144},{160,176},{192,208},{224... | collective-permute-start | bytes 61448 | tf_op jit(solution)/shard_map/ppermute | solution.py:406
  35.0 3.5 %collective-permute-start.5 = (f32[5,8,128]{2,1,0:T(8,128)S(1)}, f32[5,8,128]{2,1,0:T(8,128)S(1)}, u32[]{:S(2)}, u32[]{:S(2)}) collective-permute-start(f32[5,8,128]{2,1,0:T(8,128)S(1)} %get-tuple-element.26), channel_id=1, source_target_pairs={{16,32},{48,64},{80,96},{112,128},{144,160},{176,192},{208,224},{2... | collective-permute-start | bytes 61448 | tf_op jit(solution)/shard_map/ppermute | solution.py:406

commit v5 on v4

--- a/solution.py
+++ b/solution.py
@@ -115,10 +115,9 @@
     for i in range(7):
         packed_ref[i] = packed[i]
     codes_ref[...] = codes
-    corner = edge_code(2 * half, row)
-    outside = packed[:6] + [jnp.where(codes == corner, packed[6], 0.0)]
-    low, high = pack_rows([params_ref[p] for p in range(5)], row)
-    by_neighbour(to_a_ref, to_b_ref, low + outside, high + outside)
+    corner = jnp.where(codes == edge_code(2 * half, row), packed[6], 0.0)
+    values = [params_ref[p] for p in range(5)] + packed[:6] + [corner]
+    by_neighbour(to_a_ref, to_b_ref, *pack_rows(values, row))
 
 
 def flatten(x, row, half):
@@ -225,10 +224,12 @@
     ra = lax.axis_index(RA)
     dec = lax.axis_index(DEC)
     from_low, from_high = ra_sides(from_a_ref, from_b_ref)
-    for p in range(5):
-        g, i = divmod(p, 4)
-        value = jnp.where(row == 0, subs(from_low(g), -i), subs(from_high(g), 3 - i))
-        found = columns_around(value, lane)
+    values = []
+    for q in range(12):
+        g, i = divmod(q, 4)
+        values.append(jnp.where(row == 0, subs(from_low(g), -i), subs(from_high(g), 3 - i)))
+    for p in range(5):
+        found = columns_around(values[p], lane)
         for b in range(3):
             win_ref[b, p] = found[b]
 
@@ -246,11 +247,10 @@
             resid = resid - packed_ref[p] * subs(halo[p], shift)
         w = jnp.where((codes == 3 * a + 2 * half) & there, packed_ref[6], 0.0)
         acc = acc + w * resid * resid
-    corner = [jnp.where(row == 3, from_low(2 + i), from_high(2 + i)) for i in range(7)]
-    resid = corner[5]
-    for p in range(5):
-        resid = resid - corner[p] * jnp.where(row == 3, subs(halo[p], 3), subs(halo[p], 5))
-    acc = acc + jnp.where((row == 0) | (row == 3), corner[6] * resid * resid, 0.0)
+    resid = values[10]
+    for p in range(5):
+        resid = resid - values[5 + p] * halo[p]
+    acc = acc + jnp.where((row == 0) | (row == 3), values[11] * resid * resid, 0.0)
 
     wanted = [edge_code(b, row) for b in range(3)]
     wanted[0] = jnp.where((lane == 0) & (half == 0), -1, wanted[0])
@@ -438,7 +438,7 @@
     (seed,) = call(seed_kernel, [f32(*BLOCK)], 0, (), SEED_FLOPS)()
     ra_b_pairs = [(i, (i + 1) % 16) for i in range(1, 16, 2)]
     ra_a_pairs = [(i, i + 1) for i in range(0, 16, 2)]
-    message = f32(9, *BLOCK)
+    message = f32(3, *BLOCK)
     to_a, to_b, packed, codes = call(
         column_kernel,
         [message, message, f32(7, *BLOCK), jax.ShapeDtypeStruct(BLOCK, jnp.int32)],

time: 42.9 us -> 43.9 us (1.023)
  starting transfers between devices: 24.8 us -> 27.4 us
  local copies, waits for them, and re-layouts: 1.72 us -> 0.03 us
    all_to_all x1, starting transfers between devices: 14.9 us -> 16.8 us  [device_step(): lax.all_to_all(send.reshape(256, 1, 128), ALL, 0, 0, tiled=True)]
    unnamed x12, local copies, waits for them, and re-layouts: 1.72 us -> 0.03 us
    ppermute x6, starting transfers between devices: 9.9 us -> 10.6 us  [exchange(): return lax.ppermute(value, axes, both)]
  transfers between devices with their start and end apart: 7 -> 7, of which waited for: 3 -> 3; matrix products, arithmetic and copies ran while one was open for 0% -> 0% of each run, Pallas kernels for 17% -> 18%
where the time goes in v5:
time: 43.9 us; the launch traced here: 43.8 us
  starting transfers between devices  27.4 us (62%)
  Pallas kernels  10.2 us (23%)
  waiting for transfers between devices  5.36 us (12%)
  between operations  0.77 us (2%)
    all_to_all x1, starting transfers between devices, device_step(): lax.all_to_all(send.reshape(256, 1, 128), ALL, 0, 0, tiled=True)  16.8 us
    ppermute x6, starting transfers between devices, exchange(): return lax.ppermute(value, axes, both)  10.6 us
    pallas_call x1, Pallas kernels, device_step(): call(cross_kernel, [sums, sums, f32(6, NQ, *BLOCK)], 5, (), 1000000000, m...  3.94 us
    all_to_all x1, waiting for transfers between devices, device_step(): lax.all_to_all(send.reshape(256, 1, 128), ALL, 0, 0, tiled=True)  3.23 us
    ppermute x6, waiting for transfers between devices, exchange(): return lax.ppermute(value, axes, both)  2.13 us
    pallas_call x1, Pallas kernels, device_step(): call(stay_kernel, [f32(NQ, *BLOCK)], 5, [scratch(3, NQ)], 1000000000, mib=6)  2.05 us
    pallas_call x1, Pallas kernels, device_step(): call(chi_kernel, [f32(256, 128), f32(*BLOCK)], 12, [scratch(3, 5)], 50000...  1.38 us
    pallas_call x1, Pallas kernels, device_step(): call(lines_kernel, [f32(*BLOCK), jax.ShapeDtypeStruct((80,) + BLOCK, jnp....  1.17 us
  transfers between devices with their start and end apart: 7, of which 3 were waited for; matrix products, arithmetic and copies ran while one was open for 0% of the time, Pallas kernels for 18%

profile of v5, /device:TPU:1, one launch (start us, length us, event | category | flops | bytes accessed | tf_op | source)
XLA Modules:
  0.0 43.8 jit_solution(5144078777360347903)
XLA Ops:
  0.6 0.0 copy-start
  0.6 0.0 copy-start.1
  0.7 0.0 copy-start.2
  0.7 0.0 copy-start.3
  0.7 0.0 copy-start.4
  0.7 0.0 copy-start.5
  0.7 0.8 %collective-permute-start.1 = (f32[5,8,128]{2,1,0:T(8,128)}, f32[5,8,128]{2,1,0:T(8,128)S(1)}, u32[]{:S(2)}, u32[]{:S(2)}) collective-permute-start(f32[5,8,128]{2,1,0:T(8,128)} %bitcast.58), channel_id=1, source_target_pairs={{1,2},{3,4},{5,6},{7,8},{9,10},{11,12},{13,14},{2,1},{4,3},{6,5},{... | collective-permute-start | bytes 61448 | tf_op jit(solution)/shard_map/ppermute | solution.py:406
  1.5 5.0 %collective-permute-start = (f32[5,8,128]{2,1,0:T(8,128)}, f32[5,8,128]{2,1,0:T(8,128)S(1)}, u32[]{:S(2)}, u32[]{:S(2)}) collective-permute-start(f32[5,8,128]{2,1,0:T(8,128)} %bitcast.59), channel_id=1, source_target_pairs={{0,1},{2,3},{4,5},{6,7},{8,9},{10,11},{12,13},{14,15},{1,0},{3,2},... | collective-permute-start | bytes 61448 | tf_op jit(solution)/shard_map/ppermute | solution.py:406
  6.5 0.0 copy-done
  6.5 0.0 copy-done.1
  6.5 0.0 copy-done.2
  6.5 0.0 copy-done.3
  6.5 0.0 copy-done.4
  6.5 0.0 copy-done.5
  6.5 0.8 %shard_map.78 = (f32[3,8,128]{2,1,0:T(8,128)S(1)}, f32[3,8,128]{2,1,0:T(8,128)S(1)}, f32[7,8,128]{2,1,0:T(8,128)S(1)}, s32[8,128]{1,0:T(8,128)S(1)}) custom-call(f32[5,80,8,128]{3,2,1,0:T(8,128)S(1)} %bitcast.40, f32[80,8,128]{2,1,0:T(8,128)S(1)} %bitcast.45, f32[80,8,128]{2,1,0:T(8,128)S(1)} %bitcast.50, s32[80,8,128]{2,1,0:T(8,128)S(1)} %bitcast.55, ...), custom_call_target="tpu_custom_call" | custom-call | flops 10000000 | bytes 100000 | tf_op jit(solution)/shard_map/pallas_call | solution.py:442
  7.3 1.3 %collective-permute-start.2 = (f32[3,8,128]{2,1,0:T(8,128)S(1)}, f32[3,8,128]{2,1,0:T(8,128)S(1)}, u32[]{:S(2)}, u32[]{:S(2)}) collective-permute-start(f32[3,8,128]{2,1,0:T(8,128)S(1)} %get-tuple-element.21), channel_id=1, source_target_pairs={{0,16},{32,48},{64,80},{96,112},{128,144},{160,176},{192,208},{224... | collective-permute-start | bytes 36872 | tf_op jit(solution)/shard_map/ppermute | solution.py:406
  8.6 1.3 %collective-permute-start.3 = (f32[3,8,128]{2,1,0:T(8,128)S(1)}, f32[3,8,128]{2,1,0:T(8,128)S(1)}, u32[]{:S(2)}, u32[]{:S(2)}) collective-permute-start(f32[3,8,128]{2,1,0:T(8,128)S(1)} %get-tuple-element.22), channel_id=1, source_target_pairs={{16,32},{48,64},{80,96},{112,128},{144,160},{176,192},{208,224},{2... | collective-permute-start | bytes 36872 | tf_op jit(solution)/shard_map/ppermute | solution.py:406
  9.9 1.2 %shard_map.79 = (f32[8,128]{1,0:T(8,128)S(1)}, s32[80,8,128]{2,1,0:T(8,128)S(1)}, f32[8,128]{1,0:T(8,128)S(1)}) custom-call(f32[5,80,8,128]{3,2,1,0:T(8,128)S(1)} %bitcast.41, f32[80,8,128]{2,1,0:T(8,128)S(1)} %bitcast.46, f32[80,8,128]{2,1,0:T(8,128)S(1)} %bitcast.51, s32[80,8,128]{2,1,0:T(8,128)S(1)} %bitcast.56, s32[8,128]{1,0:T(8,128)S(1)} %bitcast.64, ...), custom_call_target="tpu_custom_call" | custom-call | flops 300000000 | bytes 100000 | tf_op jit(solution)/shard_map/pallas_call | solution.py:449
  11.0 0.0 collective-permute-done.2.from_a_ref
  11.1 0.7 %collective-permute-done.3.from_b_ref = f32[3,8,128]{2,1,0:T(8,128)S(1)} collective-permute-done((f32[3,8,128]{2,1,0:T(8,128)S(1)}, f32[3,8,128]{2,1,0:T(8,128)S(1)}, u32[]{:S(2)}, u32[]{:S(2)}) %collective-permute-start.3) | collective-permute-done | bytes 12320 | tf_op jit(solution)/shard_map/ppermute | solution.py:406
  11.7 0.0 collective-permute-done.1.dec_b_ref
  11.7 0.0 collective-permute-done.dec_a_ref
  11.7 1.4 %shard_map.80 = (f32[256,128]{1,0:T(8,128)}, f32[8,128]{1,0:T(8,128)S(1)}) custom-call(f32[5,80,8,128]{3,2,1,0:T(8,128)S(1)} %bitcast.42, f32[80,8,128]{2,1,0:T(8,128)S(1)} %bitcast.47, f32[80,8,128]{2,1,0:T(8,128)S(1)} %bitcast.52, s32[80,8,128]{2,1,0:T(8,128)S(1)} %get-tuple-element.18.code_ref, f32[8,128]{1,0:T(8,128)S(1)} %get-tuple-element.19.chi_ref, ...), custom_call_target="tpu_custom_call" | custom-call | flops 5000000 | bytes 100000 | tf_op jit(solution)/shard_map/pallas_call | solution.py:455
  13.1 16.8 %all-to-all-start = ((f32[256,1,128]{2,1,0:T(1,128)}), f32[256,1,128]{2,1,0:T(1,128)S(1)}, u32[]{:S(2)}, u32[]{:S(2)}) async-start(f32[256,1,128]{2,1,0:T(1,128)} %bitcast.31), calls=%async_computation | async-start | bytes 262144 | tf_op jit(solution)/shard_map/all_to_all | solution.py:458
  29.9 3.9 %shard_map.81 = (f32[5,8,128]{2,1,0:T(8,128)S(1)}, f32[5,8,128]{2,1,0:T(8,128)S(1)}, f32[6,20,8,128]{3,2,1,0:T(8,128)S(1)}) custom-call(f32[5,80,8,128]{3,2,1,0:T(8,128)S(1)} %bitcast.43, f32[80,8,128]{2,1,0:T(8,128)S(1)} %bitcast.48, f32[80,8,128]{2,1,0:T(8,128)S(1)} %bitcast.53, s32[80,8,128]{2,1,0:T(8,128)S(1)} %get-tuple-element.18.code_ref, ...), custom_call_target="tpu_custom_call" | custom-call | flops 1000000000 | bytes 100000 | tf_op jit(solution)/shard_map/pallas_call | solution.py:460
  33.9 2.2 %collective-permute-start.4 = (f32[5,8,128]{2,1,0:T(8,128)S(1)}, f32[5,8,128]{2,1,0:T(8,128)S(1)}, u32[]{:S(2)}, u32[]{:S(2)}) collective-permute-start(f32[5,8,128]{2,1,0:T(8,128)S(1)} %get-tuple-element.25), channel_id=1, source_target_pairs={{0,16},{32,48},{64,80},{96,112},{128,144},{160,176},{192,208},{224... | collective-permute-start | bytes 61448 | tf_op jit(solution)/shard_map/ppermute | solution.py:406
  36.1 0.0 collective-permute-start.5
  36.1 2.1 %shard_map.82.total_ref = f32[20,8,128]{2,1,0:T(8,128)S(1)} custom-call(f32[5,80,8,128]{3,2,1,0:T(8,128)S(1)} %bitcast.44, f32[80,8,128]{2,1,0:T(8,128)S(1)} %bitcast.49, f32[80,8,128]{2,1,0:T(8,128)S(1)} %bitcast.54, s32[80,8,128]{2,1,0:T(8,128)S(1)} %get-tuple-element.18.code_ref, f32[6,20,8,128]{3,2,1,0:T(8,128)S(1)} %get-tuple-element.24.cross_ref), custom_call_target="tpu_custom_call" | custom-call | flops 1000000000 | bytes 100000 | tf_op jit(solution)/shard_map/pallas_call | solution.py:465
  38.1 0.0 collective-permute-done.4.from_a_ref
  38.2 1.5 %collective-permute-done.5.from_b_ref = f32[5,8,128]{2,1,0:T(8,128)S(1)} collective-permute-done((f32[5,8,128]{2,1,0:T(8,128)S(1)}, f32[5,8,128]{2,1,0:T(8,128)S(1)}, u32[]{:S(2)}, u32[]{:S(2)}) %collective-permute-start.5) | collective-permute-done | bytes 20512 | tf_op jit(solution)/shard_map/ppermute | solution.py:406
  39.6 3.2 %all-to-all-done = f32[256,1,128]{2,1,0:T(1,128)S(1)} async-done(((f32[256,1,128]{2,1,0:T(1,128)}), f32[256,1,128]{2,1,0:T(1,128)S(1)}, u32[]{:S(2)}, u32[]{:S(2)}) %all-to-all-start) | async-done | bytes 131104 | tf_op jit(solution)/shard_map/all_to_all | solution.py:458
  42.9 0.9 %shard_map.83 = (f32[5,8,128]{2,1,0:T(8,128)}, f32[1,1]{1,0:T(1,128)}) custom-call(f32[5,8,128]{2,1,0:T(8,128)S(1)} %bitcast.62, f32[20,8,128]{2,1,0:T(8,128)S(1)} %shard_map.82.total_ref, f32[5,8,128]{2,1,0:T(8,128)S(1)} %collective-permute-done.4.from_a_ref, f32[5,8,128]{2,1,0:T(8,128)S(1)} %collective-permute-done.5.from_b_ref, f32[256,128]{1,0:T(8,128)S(1)} %bitcast.57), custom_call_target="tpu_custom_call" | custom-call | flops 100000 | bytes 100000 | tf_op jit(solution)/shard_map/pallas_call | solution.py:468
  (1 shorter events, 0.0 us)
Async XLA Ops:
  0.6 5.8 %copy-start = (f32[5,80,4,256]{3,2,1,0:T(4,128)S(1)}, f32[5,80,4,256]{3,2,1,0:T(4,128)}, u32[]{:S(2)}) copy-start(f32[5,80,4,256]{3,2,1,0:T(4,128)} %param.6) | copy-start | bytes 4915204
  0.6 5.8 %copy-start.1 = (f32[80,4,256]{2,1,0:T(4,128)S(1)}, f32[80,4,256]{2,1,0:T(4,128)}, u32[]{:S(2)}) copy-start(f32[80,4,256]{2,1,0:T(4,128)} %param.7) | copy-start | bytes 983044
  0.7 5.8 %copy-start.2 = (f32[80,4,256]{2,1,0:T(4,128)S(1)}, f32[80,4,256]{2,1,0:T(4,128)}, u32[]{:S(2)}) copy-start(f32[80,4,256]{2,1,0:T(4,128)} %param.8) | copy-start | bytes 983044
  0.7 5.8 %copy-start.3 = (s32[80,4,256]{2,1,0:T(4,128)S(1)}, s32[80,4,256]{2,1,0:T(4,128)}, u32[]{:S(2)}) copy-start(s32[80,4,256]{2,1,0:T(4,128)} %param.10) | copy-start | bytes 983044
  0.7 5.8 %copy-start.4 = (f32[5,4,256]{2,1,0:T(4,128)S(1)}, f32[5,4,256]{2,1,0:T(4,128)}, u32[]{:S(2)}) copy-start(f32[5,4,256]{2,1,0:T(4,128)} %param.9) | copy-start | bytes 61444
  0.7 5.8 %copy-start.5 = (s32[4,256]{1,0:T(4,128)S(1)}, s32[4,256]{1,0:T(4,128)}, u32[]{:S(2)}) copy-start(s32[4,256]{1,0:T(4,128)} %param.11) | copy-start | bytes 12292
  0.7 11.0 %collective-permute-start.1 = (f32[5,8,128]{2,1,0:T(8,128)}, f32[5,8,128]{2,1,0:T(8,128)S(1)}, u32[]{:S(2)}, u32[]{:S(2)}) collective-permute-start(f32[5,8,128]{2,1,0:T(8,128)} %bitcast.58), channel_id=1, source_target_pairs={{1,2},{3,4},{5,6},{7,8},{9,10},{11,12},{13,14},{2,1},{4,3},{6,5},{... | collective-permute-start | bytes 61448 | tf_op jit(solution)/shard_map/ppermute | solution.py:406
  1.5 10.2 %collective-permute-start = (f32[5,8,128]{2,1,0:T(8,128)}, f32[5,8,128]{2,1,0:T(8,128)S(1)}, u32[]{:S(2)}, u32[]{:S(2)}) collective-permute-start(f32[5,8,128]{2,1,0:T(8,128)} %bitcast.59), channel_id=1, source_target_pairs={{0,1},{2,3},{4,5},{6,7},{8,9},{10,11},{12,13},{14,15},{1,0},{3,2},... | collective-permute-start | bytes 61448 | tf_op jit(solution)/shard_map/ppermute | solution.py:406
  7.3 3.8 %collective-permute-start.2 = (f32[3,8,128]{2,1,0:T(8,128)S(1)}, f32[3,8,128]{2,1,0:T(8,128)S(1)}, u32[]{:S(2)}, u32[]{:S(2)}) collective-permute-start(f32[3,8,128]{2,1,0:T(8,128)S(1)} %get-tuple-element.21), channel_id=1, source_target_pairs={{0,16},{32,48},{64,80},{96,112},{128,144},{160,176},{192,208},{224... | collective-permute-start | bytes 36872 | tf_op jit(solution)/shard_map/ppermute | solution.py:406
  8.6 3.1 %collective-permute-start.3 = (f32[3,8,128]{2,1,0:T(8,128)S(1)}, f32[3,8,128]{2,1,0:T(8,128)S(1)}, u32[]{:S(2)}, u32[]{:S(2)}) collective-permute-start(f32[3,8,128]{2,1,0:T(8,128)S(1)} %get-tuple-element.22), channel_id=1, source_target_pairs={{16,32},{48,64},{80,96},{112,128},{144,160},{176,192},{208,224},{2... | collective-permute-start | bytes 36872 | tf_op jit(solution)/shard_map/ppermute | solution.py:406
  13.1 29.8 %all-to-all-start = ((f32[256,1,128]{2,1,0:T(1,128)}), f32[256,1,128]{2,1,0:T(1,128)S(1)}, u32[]{:S(2)}, u32[]{:S(2)}) async-start(f32[256,1,128]{2,1,0:T(1,128)} %bitcast.31), calls=%async_computation | async-start | bytes 262144 | tf_op jit(solution)/shard_map/all_to_all | solution.py:458
  33.9 4.3 %collective-permute-start.4 = (f32[5,8,128]{2,1,0:T(8,128)S(1)}, f32[5,8,128]{2,1,0:T(8,128)S(1)}, u32[]{:S(2)}, u32[]{:S(2)}) collective-permute-start(f32[5,8,128]{2,1,0:T(8,128)S(1)} %get-tuple-element.25), channel_id=1, source_target_pairs={{0,16},{32,48},{64,80},{96,112},{128,144},{160,176},{192,208},{224... | collective-permute-start | bytes 61448 | tf_op jit(solution)/shard_map/ppermute | solution.py:406
  36.1 3.5 %collective-permute-start.5 = (f32[5,8,128]{2,1,0:T(8,128)S(1)}, f32[5,8,128]{2,1,0:T(8,128)S(1)}, u32[]{:S(2)}, u32[]{:S(2)}) collective-permute-start(f32[5,8,128]{2,1,0:T(8,128)S(1)} %get-tuple-element.26), channel_id=1, source_target_pairs={{16,32},{48,64},{80,96},{112,128},{144,160},{176,192},{208,224},{2... | collective-permute-start | bytes 61448 | tf_op jit(solution)/shard_map/ppermute | solution.py:406

commit v6 on v5

--- a/solution.py
+++ b/solution.py
@@ -97,9 +97,10 @@
 
 def column_kernel(
     design_ref, observed_ref, weight_ref, offsets_ref, counts_ref, params_ref, seed_ref,
-    to_a_ref, to_b_ref, packed_ref, codes_ref,
+    to_a_ref, to_b_ref, packed_ref, codes_ref, again_ref,
 ):
     lane, row, half = grids()
+    again_ref[...] = params_ref[...]
     packed = [seed_ref[...]] * 7
     codes = jnp.full(BLOCK, 9, jnp.int32)
     counts = jnp.zeros(BLOCK, jnp.int32)
@@ -434,16 +435,17 @@
         blocked(x) for x in (design, observed, weight, params, offsets, counts)
     )
     dec_b = exchange(params, DEC, [(i, i + 1) for i in range(1, 15, 2)])
-    dec_a = exchange(params, DEC, [(i, i + 1) for i in range(0, 16, 2)])
     (seed,) = call(seed_kernel, [f32(*BLOCK)], 0, (), SEED_FLOPS)()
     ra_b_pairs = [(i, (i + 1) % 16) for i in range(1, 16, 2)]
     ra_a_pairs = [(i, i + 1) for i in range(0, 16, 2)]
     message = f32(3, *BLOCK)
-    to_a, to_b, packed, codes = call(
+    to_a, to_b, packed, codes, again = call(
         column_kernel,
-        [message, message, f32(7, *BLOCK), jax.ShapeDtypeStruct(BLOCK, jnp.int32)],
+        [message, message, f32(7, *BLOCK), jax.ShapeDtypeStruct(BLOCK, jnp.int32),
+         f32(5, *BLOCK)],
         7, (), 10_000_000, mib=6,
     )(design, observed, weight, offsets, counts, params, seed)
+    dec_a = exchange(again, DEC, [(i, i + 1) for i in range(0, 16, 2)])
     from_b = exchange(to_b, RA, ra_b_pairs)
     from_a = exchange(to_a, RA, ra_a_pairs)
     lines, code, chi = call(

time: 43.9 us -> 42.6 us (0.970)
  starting transfers between devices: 27.4 us -> 25.7 us
  local copies, waits for them, and re-layouts: 0.03 us -> 0.81 us
    ppermute x6, starting transfers between devices: 10.6 us -> 9.5 us  [exchange(): return lax.ppermute(value, axes, both)]
    unnamed x12, local copies, waits for them, and re-layouts: 0.03 us -> 0.81 us
    all_to_all x1, starting transfers between devices: 16.8 us -> 16.2 us  [device_step(): lax.all_to_all(send.reshape(256, 1, 128), ALL, 0, 0, tiled=True)]
  transfers between devices with their start and end apart: 7 -> 7, of which waited for: 3 -> 3; matrix products, arithmetic and copies ran while one was open for 0% -> 0% of each run, Pallas kernels for 18% -> 19%
where the time goes in v6:
time: 42.6 us; the launch traced here: 42.4 us
  starting transfers between devices  25.7 us (60%)
  Pallas kernels  10.2 us (24%)
  waiting for transfers between devices  4.96 us (12%)
  local copies, waits for them, and re-layouts  0.81 us (2%)
  between operations  0.77 us (2%)
    all_to_all x1, starting transfers between devices, device_step(): lax.all_to_all(send.reshape(256, 1, 128), ALL, 0, 0, tiled=True)  16.2 us
    ppermute x6, starting transfers between devices, exchange(): return lax.ppermute(value, axes, both)  9.5 us
    pallas_call x1, Pallas kernels, device_step(): call(cross_kernel, [sums, sums, f32(6, NQ, *BLOCK)], 5, (), 1000000000, m...  3.94 us
    all_to_all x1, waiting for transfers between devices, device_step(): lax.all_to_all(send.reshape(256, 1, 128), ALL, 0, 0, tiled=True)  3.23 us
    pallas_call x1, Pallas kernels, device_step(): call(stay_kernel, [f32(NQ, *BLOCK)], 5, [scratch(3, NQ)], 1000000000, mib=6)  2.05 us
    ppermute x6, waiting for transfers between devices, exchange(): return lax.ppermute(value, axes, both)  1.74 us
    pallas_call x1, Pallas kernels, device_step(): call(chi_kernel, [f32(256, 128), f32(*BLOCK)], 12, [scratch(3, 5)], 50000...  1.37 us
    pallas_call x1, Pallas kernels, device_step(): call(lines_kernel, [f32(*BLOCK), jax.ShapeDtypeStruct((80,) + BLOCK, jnp....  1.17 us
  transfers between devices with their start and end apart: 7, of which 3 were waited for; matrix products, arithmetic and copies ran while one was open for 0% of the time, Pallas kernels for 19%

profile of v6, /device:TPU:1, one launch (start us, length us, event | category | flops | bytes accessed | tf_op | source)
XLA Modules:
  0.0 42.4 jit_solution(11510834064153071704)
XLA Ops:
  0.6 0.0 copy-start
  0.6 0.0 copy-start.1
  0.7 0.0 copy-start.2
  0.7 0.0 copy-start.3
  0.7 0.0 copy-start.4
  0.7 0.0 copy-start.5
  0.7 0.8 %collective-permute-start.1 = (f32[5,8,128]{2,1,0:T(8,128)}, f32[5,8,128]{2,1,0:T(8,128)S(1)}, u32[]{:S(2)}, u32[]{:S(2)}) collective-permute-start(f32[5,8,128]{2,1,0:T(8,128)} %bitcast.58), channel_id=1, source_target_pairs={{1,2},{3,4},{5,6},{7,8},{9,10},{11,12},{13,14},{2,1},{4,3},{6,5},{... | collective-permute-start | bytes 61448 | tf_op jit(solution)/shard_map/ppermute | solution.py:407
  1.5 0.6 %copy-done = f32[5,80,4,256]{3,2,1,0:T(4,128)S(1)} copy-done((f32[5,80,4,256]{3,2,1,0:T(4,128)S(1)}, f32[5,80,4,256]{3,2,1,0:T(4,128)}, u32[]{:S(2)}) %copy-start) | copy-done | bytes 1638424
  2.1 0.0 copy-done.1
  2.1 0.1 copy-done.2
  2.2 0.1 copy-done.3
  2.3 0.0 copy-done.4
  2.3 0.0 copy-done.5
  2.3 0.7 %shard_map.78 = (f32[3,8,128]{2,1,0:T(8,128)S(1)}, f32[3,8,128]{2,1,0:T(8,128)S(1)}, f32[7,8,128]{2,1,0:T(8,128)S(1)}, s32[8,128]{1,0:T(8,128)S(1)}, f32[5,8,128]{2,1,0:T(8,128)S(1)}) custom-call(f32[5,80,8,128]{3,2,1,0:T(8,128)S(1)} %bitcast.40, f32[80,8,128]{2,1,0:T(8,128)S(1)} %bitcast.45, f32[80,8,128]{2,1,0:T(8,128)S(1)} %bitcast.50, ...), custom_call_target="tpu_custom_call" | custom-call | flops 10000000 | bytes 100000 | tf_op jit(solution)/shard_map/pallas_call | solution.py:442
  3.1 3.3 %collective-permute-start.2 = (f32[3,8,128]{2,1,0:T(8,128)S(1)}, f32[3,8,128]{2,1,0:T(8,128)S(1)}, u32[]{:S(2)}, u32[]{:S(2)}) collective-permute-start(f32[3,8,128]{2,1,0:T(8,128)S(1)} %get-tuple-element.23), channel_id=1, source_target_pairs={{0,16},{32,48},{64,80},{96,112},{128,144},{160,176},{192,208},{224... | collective-permute-start | bytes 36872 | tf_op jit(solution)/shard_map/ppermute | solution.py:407
  6.3 0.0 collective-permute-start.3
  6.3 3.2 %collective-permute-start = (f32[5,8,128]{2,1,0:T(8,128)S(1)}, f32[5,8,128]{2,1,0:T(8,128)S(1)}, u32[]{:S(2)}, u32[]{:S(2)}) collective-permute-start(f32[5,8,128]{2,1,0:T(8,128)S(1)} %get-tuple-element.22), channel_id=1, source_target_pairs={{0,1},{2,3},{4,5},{6,7},{8,9},{10,11},{12,13},{14,15},{1,0},{3,2},... | collective-permute-start | bytes 61448 | tf_op jit(solution)/shard_map/ppermute | solution.py:407
  9.5 1.2 %shard_map.79 = (f32[8,128]{1,0:T(8,128)S(1)}, s32[80,8,128]{2,1,0:T(8,128)S(1)}, f32[8,128]{1,0:T(8,128)S(1)}) custom-call(f32[5,80,8,128]{3,2,1,0:T(8,128)S(1)} %bitcast.41, f32[80,8,128]{2,1,0:T(8,128)S(1)} %bitcast.46, f32[80,8,128]{2,1,0:T(8,128)S(1)} %bitcast.51, s32[80,8,128]{2,1,0:T(8,128)S(1)} %bitcast.56, s32[8,128]{1,0:T(8,128)S(1)} %bitcast.63, ...), custom_call_target="tpu_custom_call" | custom-call | flops 300000000 | bytes 100000 | tf_op jit(solution)/shard_map/pallas_call | solution.py:451
  10.7 0.0 collective-permute-done.2.from_a_ref
  10.7 0.0 collective-permute-done.3.from_b_ref
  10.7 0.0 collective-permute-done.1.dec_b_ref
  10.7 0.3 collective-permute-done.dec_a_ref
  11.0 1.4 %shard_map.80 = (f32[256,128]{1,0:T(8,128)}, f32[8,128]{1,0:T(8,128)S(1)}) custom-call(f32[5,80,8,128]{3,2,1,0:T(8,128)S(1)} %bitcast.42, f32[80,8,128]{2,1,0:T(8,128)S(1)} %bitcast.47, f32[80,8,128]{2,1,0:T(8,128)S(1)} %bitcast.52, s32[80,8,128]{2,1,0:T(8,128)S(1)} %get-tuple-element.19.code_ref, f32[8,128]{1,0:T(8,128)S(1)} %get-tuple-element.20.chi_ref, ...), custom_call_target="tpu_custom_call" | custom-call | flops 5000000 | bytes 100000 | tf_op jit(solution)/shard_map/pallas_call | solution.py:457
  12.4 16.2 %all-to-all-start = ((f32[256,1,128]{2,1,0:T(1,128)}), f32[256,1,128]{2,1,0:T(1,128)S(1)}, u32[]{:S(2)}, u32[]{:S(2)}) async-start(f32[256,1,128]{2,1,0:T(1,128)} %bitcast.31), calls=%async_computation | async-start | bytes 262144 | tf_op jit(solution)/shard_map/all_to_all | solution.py:460
  28.6 3.9 %shard_map.81 = (f32[5,8,128]{2,1,0:T(8,128)S(1)}, f32[5,8,128]{2,1,0:T(8,128)S(1)}, f32[6,20,8,128]{3,2,1,0:T(8,128)S(1)}) custom-call(f32[5,80,8,128]{3,2,1,0:T(8,128)S(1)} %bitcast.43, f32[80,8,128]{2,1,0:T(8,128)S(1)} %bitcast.48, f32[80,8,128]{2,1,0:T(8,128)S(1)} %bitcast.53, s32[80,8,128]{2,1,0:T(8,128)S(1)} %get-tuple-element.19.code_ref, ...), custom_call_target="tpu_custom_call" | custom-call | flops 1000000000 | bytes 100000 | tf_op jit(solution)/shard_map/pallas_call | solution.py:462
  32.5 2.2 %collective-permute-start.4 = (f32[5,8,128]{2,1,0:T(8,128)S(1)}, f32[5,8,128]{2,1,0:T(8,128)S(1)}, u32[]{:S(2)}, u32[]{:S(2)}) collective-permute-start(f32[5,8,128]{2,1,0:T(8,128)S(1)} %get-tuple-element.27), channel_id=1, source_target_pairs={{0,16},{32,48},{64,80},{96,112},{128,144},{160,176},{192,208},{224... | collective-permute-start | bytes 61448 | tf_op jit(solution)/shard_map/ppermute | solution.py:407
  34.7 0.0 collective-permute-start.5
  34.7 2.1 %shard_map.82.total_ref = f32[20,8,128]{2,1,0:T(8,128)S(1)} custom-call(f32[5,80,8,128]{3,2,1,0:T(8,128)S(1)} %bitcast.44, f32[80,8,128]{2,1,0:T(8,128)S(1)} %bitcast.49, f32[80,8,128]{2,1,0:T(8,128)S(1)} %bitcast.54, s32[80,8,128]{2,1,0:T(8,128)S(1)} %get-tuple-element.19.code_ref, f32[6,20,8,128]{3,2,1,0:T(8,128)S(1)} %get-tuple-element.26.cross_ref), custom_call_target="tpu_custom_call" | custom-call | flops 1000000000 | bytes 100000 | tf_op jit(solution)/shard_map/pallas_call | solution.py:467
  36.8 0.0 collective-permute-done.4.from_a_ref
  36.8 1.5 %collective-permute-done.5.from_b_ref = f32[5,8,128]{2,1,0:T(8,128)S(1)} collective-permute-done((f32[5,8,128]{2,1,0:T(8,128)S(1)}, f32[5,8,128]{2,1,0:T(8,128)S(1)}, u32[]{:S(2)}, u32[]{:S(2)}) %collective-permute-start.5) | collective-permute-done | bytes 20512 | tf_op jit(solution)/shard_map/ppermute | solution.py:407
  38.3 3.2 %all-to-all-done = f32[256,1,128]{2,1,0:T(1,128)S(1)} async-done(((f32[256,1,128]{2,1,0:T(1,128)}), f32[256,1,128]{2,1,0:T(1,128)S(1)}, u32[]{:S(2)}, u32[]{:S(2)}) %all-to-all-start) | async-done | bytes 131104 | tf_op jit(solution)/shard_map/all_to_all | solution.py:460
  41.5 0.9 %shard_map.83 = (f32[5,8,128]{2,1,0:T(8,128)}, f32[1,1]{1,0:T(1,128)}) custom-call(f32[5,8,128]{2,1,0:T(8,128)S(1)} %bitcast.61, f32[20,8,128]{2,1,0:T(8,128)S(1)} %shard_map.82.total_ref, f32[5,8,128]{2,1,0:T(8,128)S(1)} %collective-permute-done.4.from_a_ref, f32[5,8,128]{2,1,0:T(8,128)S(1)} %collective-permute-done.5.from_b_ref, f32[256,128]{1,0:T(8,128)S(1)} %bitcast.57), custom_call_target="tpu_custom_call" | custom-call | flops 100000 | bytes 100000 | tf_op jit(solution)/shard_map/pallas_call | solution.py:470
  (1 shorter events, 0.0 us)
Async XLA Ops:
  0.6 1.4 %copy-start = (f32[5,80,4,256]{3,2,1,0:T(4,128)S(1)}, f32[5,80,4,256]{3,2,1,0:T(4,128)}, u32[]{:S(2)}) copy-start(f32[5,80,4,256]{3,2,1,0:T(4,128)} %param.6) | copy-start | bytes 4915204
  0.6 1.5 %copy-start.1 = (f32[80,4,256]{2,1,0:T(4,128)S(1)}, f32[80,4,256]{2,1,0:T(4,128)}, u32[]{:S(2)}) copy-start(f32[80,4,256]{2,1,0:T(4,128)} %param.7) | copy-start | bytes 983044
  0.7 1.5 %copy-start.2 = (f32[80,4,256]{2,1,0:T(4,128)S(1)}, f32[80,4,256]{2,1,0:T(4,128)}, u32[]{:S(2)}) copy-start(f32[80,4,256]{2,1,0:T(4,128)} %param.8) | copy-start | bytes 983044
  0.7 1.6 %copy-start.3 = (s32[80,4,256]{2,1,0:T(4,128)S(1)}, s32[80,4,256]{2,1,0:T(4,128)}, u32[]{:S(2)}) copy-start(s32[80,4,256]{2,1,0:T(4,128)} %param.10) | copy-start | bytes 983044
  0.7 1.6 %copy-start.4 = (f32[5,4,256]{2,1,0:T(4,128)S(1)}, f32[5,4,256]{2,1,0:T(4,128)}, u32[]{:S(2)}) copy-start(f32[5,4,256]{2,1,0:T(4,128)} %param.9) | copy-start | bytes 61444
  0.7 1.6 %copy-start.5 = (s32[4,256]{1,0:T(4,128)S(1)}, s32[4,256]{1,0:T(4,128)}, u32[]{:S(2)}) copy-start(s32[4,256]{1,0:T(4,128)} %param.11) | copy-start | bytes 12292
  0.7 10.0 %collective-permute-start.1 = (f32[5,8,128]{2,1,0:T(8,128)}, f32[5,8,128]{2,1,0:T(8,128)S(1)}, u32[]{:S(2)}, u32[]{:S(2)}) collective-permute-start(f32[5,8,128]{2,1,0:T(8,128)} %bitcast.58), channel_id=1, source_target_pairs={{1,2},{3,4},{5,6},{7,8},{9,10},{11,12},{13,14},{2,1},{4,3},{6,5},{... | collective-permute-start | bytes 61448 | tf_op jit(solution)/shard_map/ppermute | solution.py:407
  3.1 7.7 %collective-permute-start.2 = (f32[3,8,128]{2,1,0:T(8,128)S(1)}, f32[3,8,128]{2,1,0:T(8,128)S(1)}, u32[]{:S(2)}, u32[]{:S(2)}) collective-permute-start(f32[3,8,128]{2,1,0:T(8,128)S(1)} %get-tuple-element.23), channel_id=1, source_target_pairs={{0,16},{32,48},{64,80},{96,112},{128,144},{160,176},{192,208},{224... | collective-permute-start | bytes 36872 | tf_op jit(solution)/shard_map/ppermute | solution.py:407
  6.3 4.4 %collective-permute-start.3 = (f32[3,8,128]{2,1,0:T(8,128)S(1)}, f32[3,8,128]{2,1,0:T(8,128)S(1)}, u32[]{:S(2)}, u32[]{:S(2)}) collective-permute-start(f32[3,8,128]{2,1,0:T(8,128)S(1)} %get-tuple-element.24), channel_id=1, source_target_pairs={{16,32},{48,64},{80,96},{112,128},{144,160},{176,192},{208,224},{2... | collective-permute-start | bytes 36872 | tf_op jit(solution)/shard_map/ppermute | solution.py:407
  6.3 4.6 %collective-permute-start = (f32[5,8,128]{2,1,0:T(8,128)S(1)}, f32[5,8,128]{2,1,0:T(8,128)S(1)}, u32[]{:S(2)}, u32[]{:S(2)}) collective-permute-start(f32[5,8,128]{2,1,0:T(8,128)S(1)} %get-tuple-element.22), channel_id=1, source_target_pairs={{0,1},{2,3},{4,5},{6,7},{8,9},{10,11},{12,13},{14,15},{1,0},{3,2},... | collective-permute-start | bytes 61448 | tf_op jit(solution)/shard_map/ppermute | solution.py:407
  12.4 29.1 %all-to-all-start = ((f32[256,1,128]{2,1,0:T(1,128)}), f32[256,1,128]{2,1,0:T(1,128)S(1)}, u32[]{:S(2)}, u32[]{:S(2)}) async-start(f32[256,1,128]{2,1,0:T(1,128)} %bitcast.31), calls=%async_computation | async-start | bytes 262144 | tf_op jit(solution)/shard_map/all_to_all | solution.py:460
  32.5 4.3 %collective-permute-start.4 = (f32[5,8,128]{2,1,0:T(8,128)S(1)}, f32[5,8,128]{2,1,0:T(8,128)S(1)}, u32[]{:S(2)}, u32[]{:S(2)}) collective-permute-start(f32[5,8,128]{2,1,0:T(8,128)S(1)} %get-tuple-element.27), channel_id=1, source_target_pairs={{0,16},{32,48},{64,80},{96,112},{128,144},{160,176},{192,208},{224... | collective-permute-start | bytes 61448 | tf_op jit(solution)/shard_map/ppermute | solution.py:407
  34.7 3.5 %collective-permute-start.5 = (f32[5,8,128]{2,1,0:T(8,128)S(1)}, f32[5,8,128]{2,1,0:T(8,128)S(1)}, u32[]{:S(2)}, u32[]{:S(2)}) collective-permute-start(f32[5,8,128]{2,1,0:T(8,128)S(1)} %get-tuple-element.28), channel_id=1, source_target_pairs={{16,32},{48,64},{80,96},{112,128},{144,160},{176,192},{208,224},{2... | collective-permute-start | bytes 61448 | tf_op jit(solution)/shard_map/ppermute | solution.py:407
